TPU v7x, 16 devices: a whole 2x2x2 slice. The times are simulated.
16 devices in a mesh: dp: 4 (over z, y), tp: 4 (over x, core).
Axes of the slice: x: 2, y: 2, z: 2, core: 2. Of those that a mesh axis runs over, the one named last changes fastest.
Arguments:
- tokens: int32 [4, 128], P('dp'), parts along dimension 0
- positions: int32 [4, 128], P('dp'), parts along dimension 0
- embedding: bfloat16 [8192, 2048], P('tp')
- gain_attn: float32 [2048], replicated
- gain_mlp: float32 [2048], replicated
- w_query: bfloat16 [2048, 32, 64], P(None, 'tp')
- w_key: bfloat16 [2048, 8, 64], P(None, 'tp')
- w_value: bfloat16 [2048, 8, 64], P(None, 'tp')
- w_out: bfloat16 [32, 64, 2048], P('tp')
- w_gate: bfloat16 [2048, 8192], P(None, 'tp')
- w_up: bfloat16 [2048, 8192], P(None, 'tp')
- w_down: bfloat16 [8192, 2048], P('tp')
- grad_hidden: bfloat16 [4, 128, 2048], P('dp', 'tp'), parts along dimension 0
Outputs:
- output 1: bfloat16 [4, 128, 2048], P('dp', 'tp'), parts along dimension 0
- output 2: float32 [32768, 2048], P(('dp', 'tp')), parts along dimension 0
- output 3: float32 [8192, 32, 64], P('dp', 'tp'), parts along dimension 0
- output 4: float32 [8192, 8, 64], P('dp', 'tp'), parts along dimension 0
- output 5: float32 [8192, 8, 64], P('dp', 'tp'), parts along dimension 0
- output 6: float32 [128, 64, 2048], P(('dp', 'tp')), parts along dimension 0
- output 7: float32 [8192, 8192], P('dp', 'tp'), parts along dimension 0
- output 8: float32 [8192, 8192], P('dp', 'tp'), parts along dimension 0
- output 9: float32 [32768, 2048], P(('dp', 'tp')), parts along dimension 0
- output 10: float32 [8192], P('dp'), parts along dimension 0
- output 11: float32 [8192], P('dp'), parts along dimension 0
There are 4 independent parts. A program takes and returns all parts, laid end to end along the dimension named above; an argument that names none is the same for every part.
All inputs are finite; a program needn't handle non-finite values.
Results may differ from a plain program's by a relative error of at most 0.0182023.
Values are sent between devices in bfloat16 or wider.
A program may use at most 1 GiB of HBM per device.

v0:
```python
import jax
import jax.numpy as jnp
from jax import lax
from jax.sharding import PartitionSpec as P

ROPE_THETA = 1000000.0
RMS_EPS = 1e-5


def rope_tables(positions, head_dim):
    half_dim = head_dim // 2
    inv_freq = ROPE_THETA ** (-jnp.arange(half_dim, dtype=jnp.float32) * (2.0 / head_dim))
    angles = positions.astype(jnp.float32)[:, :, None] * inv_freq
    return jnp.cos(angles)[:, :, None, :], jnp.sin(angles)[:, :, None, :]


def rotate(values, cos_tab, sin_tab):
    half_dim = values.shape[-1] // 2
    first_half = values[..., :half_dim]
    second_half = values[..., half_dim:]
    return jnp.concatenate([first_half * cos_tab - second_half * sin_tab, second_half * cos_tab + first_half * sin_tab], axis=-1)


def norm_fwd(hidden, gain_vec):
    hidden_f = hidden.astype(jnp.float32)
    inv_rms = lax.rsqrt(jnp.mean(hidden_f * hidden_f, axis=-1, keepdims=True) + RMS_EPS)
    normed = hidden_f * inv_rms
    return (normed * gain_vec).astype(jnp.bfloat16), normed, inv_rms


def norm_bwd(grad_normed, normed, inv_rms, gain_vec):
    grad_f = grad_normed.astype(jnp.float32)
    gain_part = jnp.sum(grad_f * normed, axis=(0, 1))
    scaled = grad_f * gain_vec
    grad_in = inv_rms * (scaled - normed * jnp.mean(scaled * normed, axis=-1, keepdims=True))
    return grad_in, gain_part


def layer_pass(first_x, positions, gain_attn, gain_mlp, w_query, w_key, w_value, w_out, w_gate, w_up, w_down, grad_hidden):
    batch_size, seq_len = positions.shape
    local_heads, head_dim = w_query.shape[1], w_query.shape[2]
    local_kv = w_key.shape[1]
    group_size = local_heads // local_kv
    score_scale = head_dim ** -0.5
    cos_tab, sin_tab = rope_tables(positions, head_dim)
    normed1_bf, normed1, inv_rms1 = norm_fwd(first_x, gain_attn)
    gathered1 = lax.all_gather(normed1_bf, 'tp', axis=1, tiled=True)
    queries = rotate(jnp.einsum('bsd,dhe->bshe', gathered1, w_query, preferred_element_type=jnp.float32), cos_tab, sin_tab).astype(jnp.bfloat16)
    keys_rot = rotate(jnp.einsum('bsd,dhe->bshe', gathered1, w_key, preferred_element_type=jnp.float32), cos_tab, sin_tab).astype(jnp.bfloat16)
    values = jnp.einsum('bsd,dhe->bshe', gathered1, w_value, preferred_element_type=jnp.float32).astype(jnp.bfloat16)
    queries5 = queries.reshape(batch_size, seq_len, local_kv, group_size, head_dim)
    causal = jnp.arange(seq_len)[:, None] >= jnp.arange(seq_len)[None, :]
    scores = jnp.einsum('bqkgd,bskd->bkgqs', queries5, keys_rot, preferred_element_type=jnp.float32) * score_scale
    probs_f = jax.nn.softmax(jnp.where(causal, scores, -1e30), axis=-1)
    probs_bf = probs_f.astype(jnp.bfloat16)
    attn_heads = jnp.einsum('bkgqs,bskd->bqkgd', probs_bf, values, preferred_element_type=jnp.float32)
    attn_heads = attn_heads.astype(jnp.bfloat16).reshape(batch_size, seq_len, local_heads, head_dim)
    attn_part = jnp.einsum('bshe,hed->bsd', attn_heads, w_out, preferred_element_type=jnp.float32).astype(jnp.bfloat16)
    attn_sum = lax.psum_scatter(attn_part, 'tp', scatter_dimension=1, tiled=True)
    hidden1 = (first_x.astype(jnp.float32) + attn_sum.astype(jnp.float32)).astype(jnp.bfloat16)
    normed2_bf, normed2, inv_rms2 = norm_fwd(hidden1, gain_mlp)
    gathered2 = lax.all_gather(normed2_bf, 'tp', axis=1, tiled=True)
    gate_pre = jnp.einsum('bsd,df->bsf', gathered2, w_gate, preferred_element_type=jnp.float32)
    up_pre = jnp.einsum('bsd,df->bsf', gathered2, w_up, preferred_element_type=jnp.float32)
    gate_sig = jax.nn.sigmoid(gate_pre)
    gate_act = gate_pre * gate_sig
    act_bf = (gate_act * up_pre).astype(jnp.bfloat16)
    mlp_part = jnp.einsum('bsf,fd->bsd', act_bf, w_down, preferred_element_type=jnp.float32).astype(jnp.bfloat16)
    mlp_sum = lax.psum_scatter(mlp_part, 'tp', scatter_dimension=1, tiled=True)
    hidden_out = (hidden1.astype(jnp.float32) + mlp_sum.astype(jnp.float32)).astype(jnp.bfloat16)

    grad_full = lax.all_gather(grad_hidden, 'tp', axis=1, tiled=True)
    grad_act = jnp.einsum('bsd,fd->bsf', grad_full, w_down, preferred_element_type=jnp.float32).astype(jnp.bfloat16).astype(jnp.float32)
    grad_up = (grad_act * gate_act).astype(jnp.bfloat16)
    grad_gate = (grad_act * up_pre * gate_sig * (1.0 + gate_pre * (1.0 - gate_sig))).astype(jnp.bfloat16)
    grad_w_down = jnp.einsum('bsf,bsd->fd', act_bf, grad_full, preferred_element_type=jnp.float32)
    grad_w_gate = jnp.einsum('bsd,bsf->df', gathered2, grad_gate, preferred_element_type=jnp.float32)
    grad_w_up = jnp.einsum('bsd,bsf->df', gathered2, grad_up, preferred_element_type=jnp.float32)
    grad_n2_part = (jnp.einsum('bsf,df->bsd', grad_gate, w_gate, preferred_element_type=jnp.float32) + jnp.einsum('bsf,df->bsd', grad_up, w_up, preferred_element_type=jnp.float32)).astype(jnp.bfloat16)
    grad_n2 = lax.psum_scatter(grad_n2_part, 'tp', scatter_dimension=1, tiled=True)
    grad_h1_norm, gain_mlp_part = norm_bwd(grad_n2, normed2, inv_rms2, gain_mlp)
    grad_h1 = (grad_hidden.astype(jnp.float32) + grad_h1_norm).astype(jnp.bfloat16)
    grad_h1_full = lax.all_gather(grad_h1, 'tp', axis=1, tiled=True)
    grad_heads = jnp.einsum('bsd,hed->bshe', grad_h1_full, w_out, preferred_element_type=jnp.float32).astype(jnp.bfloat16)
    grad_w_out = jnp.einsum('bshe,bsd->hed', attn_heads, grad_h1_full, preferred_element_type=jnp.float32)
    grad_heads5 = grad_heads.reshape(batch_size, seq_len, local_kv, group_size, head_dim)
    grad_probs = jnp.einsum('bqkgd,bskd->bkgqs', grad_heads5, values, preferred_element_type=jnp.float32).astype(jnp.bfloat16).astype(jnp.float32)
    grad_values = jnp.einsum('bkgqs,bqkgd->bskd', probs_bf, grad_heads5, preferred_element_type=jnp.float32).astype(jnp.bfloat16)
    grad_scores = (probs_f * (grad_probs - jnp.sum(grad_probs * probs_f, axis=-1, keepdims=True)) * score_scale).astype(jnp.bfloat16)
    grad_queries = jnp.einsum('bkgqs,bskd->bqkgd', grad_scores, keys_rot, preferred_element_type=jnp.float32).astype(jnp.bfloat16)
    grad_queries = grad_queries.reshape(batch_size, seq_len, local_heads, head_dim)
    grad_keys = jnp.einsum('bkgqs,bqkgd->bskd', grad_scores, queries5, preferred_element_type=jnp.float32).astype(jnp.bfloat16)
    grad_q_lin = rotate(grad_queries.astype(jnp.float32), cos_tab, -sin_tab).astype(jnp.bfloat16)
    grad_k_lin = rotate(grad_keys.astype(jnp.float32), cos_tab, -sin_tab).astype(jnp.bfloat16)
    grad_w_query = jnp.einsum('bsd,bshe->dhe', gathered1, grad_q_lin, preferred_element_type=jnp.float32)
    grad_w_key = jnp.einsum('bsd,bshe->dhe', gathered1, grad_k_lin, preferred_element_type=jnp.float32)
    grad_w_value = jnp.einsum('bsd,bshe->dhe', gathered1, grad_values, preferred_element_type=jnp.float32)
    grad_n1_part = (jnp.einsum('bshe,dhe->bsd', grad_q_lin, w_query, preferred_element_type=jnp.float32)
                    + jnp.einsum('bshe,dhe->bsd', grad_k_lin, w_key, preferred_element_type=jnp.float32)
                    + jnp.einsum('bshe,dhe->bsd', grad_values, w_value, preferred_element_type=jnp.float32)).astype(jnp.bfloat16)
    grad_n1 = lax.psum_scatter(grad_n1_part, 'tp', scatter_dimension=1, tiled=True)
    grad_x_norm, gain_attn_part = norm_bwd(grad_n1, normed1, inv_rms1, gain_attn)
    grad_first = (grad_h1.astype(jnp.float32) + grad_x_norm).astype(jnp.bfloat16)
    gain_grads = lax.psum(jnp.stack([gain_attn_part, gain_mlp_part]), 'tp')
    grad_weights = (grad_w_query, grad_w_key, grad_w_value, grad_w_out, grad_w_gate, grad_w_up, grad_w_down)
    return hidden_out, grad_first, grad_weights, gain_grads


def solution(mesh):
    in_specs = (P('dp', None), P('dp', None), P('tp', None), P(None), P(None),
                P(None, 'tp', None), P(None, 'tp', None), P(None, 'tp', None), P('tp', None, None),
                P(None, 'tp'), P(None, 'tp'), P('tp', None), P('dp', 'tp', None))
    out_specs = (P('dp', 'tp', None), P(('dp', 'tp'), None),
                 P('dp', 'tp', None), P('dp', 'tp', None), P('dp', 'tp', None), P(('dp', 'tp'), None, None),
                 P('dp', 'tp'), P('dp', 'tp'), P(('dp', 'tp'), None), P('dp'), P('dp'))

    def device_fn(tokens, positions, emb_shard, gain_attn, gain_mlp, w_query, w_key, w_value, w_out, w_gate, w_up, w_down, grad_hidden):
        rows_local = emb_shard.shape[0]
        local_ids = tokens - lax.axis_index('tp') * rows_local
        owned_row = (local_ids >= 0) & (local_ids < rows_local)
        looked_up = jnp.take(emb_shard, jnp.clip(local_ids, 0, rows_local - 1), axis=0)
        partial_emb = jnp.where(owned_row[:, :, None], looked_up, jnp.zeros((), jnp.bfloat16))
        first_x = lax.psum_scatter(partial_emb, 'tp', scatter_dimension=1, tiled=True)
        hidden_out, grad_first, grad_weights, gain_grads = layer_pass(
            first_x, positions, gain_attn, gain_mlp, w_query, w_key, w_value, w_out, w_gate, w_up, w_down, grad_hidden)
        grad_first_full = lax.all_gather(grad_first, 'tp', axis=1, tiled=True)
        seg_ids = jnp.where(owned_row, local_ids, rows_local).reshape(-1)
        grad_embedding = jax.ops.segment_sum(grad_first_full.reshape(-1, grad_first_full.shape[-1]).astype(jnp.float32), seg_ids, num_segments=rows_local)
        return (hidden_out, grad_embedding) + grad_weights + (gain_grads[0], gain_grads[1])

    return jax.shard_map(device_fn, mesh=mesh, in_specs=in_specs, out_specs=out_specs, check_vma=False)
```

profile of v0, /device:TPU:0, one launch (start us, length us, event | category | flops | bytes accessed | tf_op | source)
XLA Modules:
  0.0 218.0 jit_solution(18083461235995477214)
XLA Ops:
  8.7 5.9 %gather_fusion = bf16[128,2048]{1,0:T(8,128)(2,1)S(1)} fusion(bf16[2048,2048]{1,0:T(8,128)(2,1)} %param.15, s32[1024]{0:T(1024)S(1)} %pad_clamp_fusion), kind=kCustom, calls=%fused_computation | custom fusion | bytes 1049088 | tf_op jit(solution)/shard_map/jit(_take)/gather | solution.py:121
  17.7 18.7 %reduce-scatter.6.cloned.1.call-done = bf16[1,32,2048]{2,1,0:T(8,128)(2,1)} async-done(((bf16[1,128,2048]{2,1,0:T(8,128)(2,1)}), bf16[1,32,2048]{2,1,0:T(8,128)(2,1)}) %reduce-scatter.6.cloned.1.call-update) | async-done | bytes 131088 | tf_op jit(solution)/shard_map/reduce_scatter | solution.py:123
  38.6 6.5 %all_gather.15 = bf16[1,128,2048]{2,1,0:T(8,128)(2,1)S(1)} all-gather(bf16[1,32,2048]{2,1,0:T(8,128)(2,1)S(1)} %fusion.72), channel_id=1, replica_groups=mesh['dp'=4,'tp'=4] {'tp'}, dimensions={1}, use_global_device_ids=true | all-gather | bytes 655360 | tf_op jit(solution)/shard_map/all_gather | solution.py:47
  53.2 7.3 %all_gather.17 = bf16[1,128,2048]{2,1,0:T(8,128)(2,1)} all-gather(bf16[1,32,2048]{2,1,0:T(8,128)(2,1)S(1)} %copy-done.10), channel_id=1, replica_groups=mesh['dp'=4,'tp'=4] {'tp'}, dimensions={1}, use_global_device_ids=true | all-gather | bytes 655360 | tf_op jit(solution)/shard_map/all_gather | solution.py:72
  60.5 11.3 %reduce-scatter.8.cloned.1.call-done = bf16[1,32,2048]{2,1,0:T(8,128)(2,1)} async-done(((bf16[1,128,2048]{2,1,0:T(8,128)(2,1)}), bf16[1,32,2048]{2,1,0:T(8,128)(2,1)}) %reduce-scatter.8.cloned.1.call-update) | async-done | bytes 131088 | tf_op jit(solution)/shard_map/reduce_scatter | solution.py:59
  73.9 6.7 %all_gather.16 = bf16[1,128,2048]{2,1,0:T(8,128)(2,1)S(1)} all-gather(bf16[1,32,2048]{2,1,0:T(8,128)(2,1)S(1)} %fusion.77), channel_id=1, replica_groups=mesh['dp'=4,'tp'=4] {'tp'}, dimensions={1}, use_global_device_ids=true | all-gather | bytes 655360 | tf_op jit(solution)/shard_map/all_gather | solution.py:62
  80.6 4.8 %fusion.37 = f32[128,2048]{1,0:T(8,128)S(1)} fusion(bf16[2048,2048]{1,0:T(8,128)(2,1)} %param.23, bf16[1,128,2048]{2,1,0:T(8,128)(2,1)S(1)} %all_gather.16), kind=kOutput, calls=%fused_computation.57 | convolution fusion | flops 1073741824 | bytes 9961472 | tf_op jit(solution)/shard_map/bsd,df->bsf/dot_general | solution.py:64
  86.7 7.4 %multiply_convert_fusion = (bf16[128,2048]{1,0:T(8,128)(2,1)S(1)}, bf16[128,2048]{1,0:T(8,128)(2,1)S(1)}, bf16[128,2048]{1,0:T(8,128)(2,1)}) fusion(f32[128,2048]{1,0:T(8,128)S(1)} %fusion.39, f32[128,2048]{1,0:T(8,128)S(1)} %fusion.37, bf16[2048,2048]{1,0:T(8,128)(2,1)} %param.24, bf16[1,128,2048]{2,1,0:T(8,128)(2,1)S(1)} %copy-done.4), kind=kOutput, calls=%fused_computation.41 | convolution fusion | flops 1078198272 | bytes 12582912 | tf_op jit(solution)/shard_map/bsd,fd->bsf/dot_general | solution.py:73
  94.1 2.9 %fusion.109 = f32[128,2048]{1,0:T(8,128)S(1)} fusion(bf16[128,2048]{1,0:T(8,128)(2,1)S(1)} %get-tuple-element.20, bf16[2048,2048]{1,0:T(8,128)(2,1)S(1)} %bitcast.236), kind=kOutput, calls=%fused_computation.166 | convolution fusion | flops 1073741824 | bytes 9961472 | tf_op jit(solution)/shard_map/bsf,df->bsd/dot_general | solution.py:79
  97.0 3.7 %fusion.8 = bf16[1,128,2048]{2,1,0:T(8,128)(2,1)} fusion(f32[128,2048]{1,0:T(8,128)S(1)} %fusion.109, bf16[128,2048]{1,0:T(8,128)(2,1)S(1)} %get-tuple-element.19, bf16[2048,2048]{1,0:T(8,128)(2,1)S(1)} %bitcast.234), kind=kOutput, calls=%fused_computation.17 | convolution fusion | flops 1074266112 | bytes 10485760 | tf_op jit(solution)/shard_map/bsf,df->bsd/dot_general | solution.py:79
  101.0 5.6 %fusion.11 = bf16[1,128,2048]{2,1,0:T(8,128)(2,1)} fusion(bf16[128,2048]{1,0:T(8,128)(2,1)} %get-tuple-element.21, bf16[2048,2048]{1,0:T(8,128)(2,1)} %param.24), kind=kOutput, calls=%fused_computation.20 | convolution fusion | flops 1074003968 | bytes 9437184 | tf_op jit(solution)/shard_map/bsf,fd->bsd/dot_general | solution.py:68
  106.6 9.6 %fusion.33 = f32[2048,2048]{1,0:T(8,128)} fusion(bf16[128,2048]{1,0:T(8,128)(2,1)} %copy-done.7, bf16[1,128,2048]{2,1,0:T(8,128)(2,1)S(1)} %all_gather.16), kind=kOutput, calls=%fused_computation.53 | convolution fusion | flops 1073741824 | bytes 17825792 | tf_op jit(solution)/shard_map/bsd,bsf->df/dot_general | solution.py:78
  116.3 9.7 %fusion.35 = f32[2048,2048]{1,0:T(8,128)} fusion(bf16[128,2048]{1,0:T(8,128)(2,1)} %copy-done.6, bf16[1,128,2048]{2,1,0:T(8,128)(2,1)S(1)} %all_gather.16), kind=kOutput, calls=%fused_computation.55 | convolution fusion | flops 1073741824 | bytes 17825792 | tf_op jit(solution)/shard_map/bsd,bsf->df/dot_general | solution.py:77
  126.0 8.5 %fusion.30 = f32[2048,2048]{1,0:T(8,128)} fusion(bf16[128,2048]{1,0:T(8,128)(2,1)S(1)} %copy-done.2, bf16[1,128,2048]{2,1,0:T(8,128)(2,1)S(1)} %copy-done.5), kind=kOutput, calls=%fused_computation.50 | convolution fusion | flops 1073741824 | bytes 17825792 | tf_op jit(solution)/shard_map/bsf,bsd->fd/dot_general | solution.py:76
  136.2 3.9 %reduce-scatter.10.cloned.1.call-done = bf16[1,32,2048]{2,1,0:T(8,128)(2,1)} async-done(((bf16[1,128,2048]{2,1,0:T(8,128)(2,1)}), bf16[1,32,2048]{2,1,0:T(8,128)(2,1)}) %reduce-scatter.10.cloned.1.call-update) | async-done | bytes 131088 | tf_op jit(solution)/shard_map/reduce_scatter | solution.py:69
  141.7 6.8 %all_gather.18 = bf16[1,128,2048]{2,1,0:T(8,128)(2,1)S(1)} all-gather(bf16[1,32,2048]{2,1,0:T(8,128)(2,1)S(1)} %get-tuple-element.26), channel_id=1, replica_groups=mesh['dp'=4,'tp'=4] {'tp'}, dimensions={1}, use_global_device_ids=true | all-gather | bytes 655360 | tf_op jit(solution)/shard_map/all_gather | solution.py:83
  148.5 2.3 %convolution_convert_fusion.3 = bf16[128,8,64]{0,2,1:T(8,128)(2,1)S(1)} fusion(bf16[8,64,2048]{2,1,0:T(8,128)(2,1)} %param.21, bf16[1,128,2048]{2,1,0:T(8,128)(2,1)S(1)} %all_gather.18), kind=kOutput, calls=%fused_computation.28 | convolution fusion | flops 268500992 | bytes 2752512 | tf_op jit(solution)/shard_map/bsd,hed->bshe/dot_general | solution.py:84
  160.7 2.2 %fusion.10 = bf16[1,128,2048]{2,1,0:T(8,128)(2,1)} fusion(f32[128,2048]{1,0:T(8,128)S(1)} %convolution_bitcast_fusion, f32[128,2048]{1,0:T(8,128)S(1)} %convolution_bitcast_fusion.2, bf16[2048,2,64]{0,2,1:T(8,128)(2,1)} %param.19, bf16[128,2,32]{0,2,1:T(8,128)(2,1)S(1)} %get-tuple-element.29, bf16[128,2,32]{0,2,1:T(8,128)(2,1)S(1)} %get-tuple-element.28), kind=kOutput, calls=%fused_computation.19 | convolution fusion | flops 67960832 | bytes 3178496 | tf_op jit(solution)/shard_map/bshe,dhe->bsd/dot_general | solution.py:99
  166.9 3.6 %fusion.27 = f32[8,64,2048]{2,1,0:T(8,128)} fusion(bf16[128,8,64]{0,2,1:T(8,128)(2,1)} %bitcast.246, bf16[1,128,2048]{2,1,0:T(8,128)(2,1)S(1)} %all_gather.18), kind=kOutput, calls=%fused_computation.47 | convolution fusion | flops 268435456 | bytes 4849664 | tf_op jit(solution)/shard_map/bshe,bsd->hed/dot_general | solution.py:85
  170.5 2.7 %fusion.41 = f32[2048,512]{0,1} fusion(bf16[128,512]{0,1:T(8,128)(2,1)S(1)} %bitcast.244, bf16[1,128,2048]{2,1,0:T(8,128)(2,1)S(1)} %all_gather.15), kind=kOutput, calls=%fused_computation.61 | convolution fusion | flops 268435456 | bytes 4849664
  173.3 8.2 %reduce-scatter.14.cloned.1.call-done = bf16[1,32,2048]{2,1,0:T(8,128)(2,1)} async-done(((bf16[1,128,2048]{2,1,0:T(8,128)(2,1)}), bf16[1,32,2048]{2,1,0:T(8,128)(2,1)}) %reduce-scatter.14.cloned.1.call-update) | async-done | bytes 131088 | tf_op jit(solution)/shard_map/reduce_scatter | solution.py:101
  183.7 6.5 %all_gather.19 = bf16[1,128,2048]{2,1,0:T(8,128)(2,1)S(1)} all-gather(bf16[1,32,2048]{2,1,0:T(8,128)(2,1)S(1)} %fusion.68), channel_id=1, replica_groups=mesh['dp'=4,'tp'=4] {'tp'}, dimensions={1}, use_global_device_ids=true | all-gather | bytes 655360 | tf_op jit(solution)/shard_map/all_gather | solution.py:126
  190.2 11.1 %psum.7 = f32[2,2048]{1,0:T(2,128)S(1)} all-reduce(f32[2,2048]{1,0:T(2,128)S(1)} %pad_maximum_fusion.5), channel_id=1, replica_groups=mesh['dp'=4,'tp'=4] {'tp'}, use_global_device_ids=true, to_apply=%region_15.16 | all-reduce | flops 4096 | bytes 32768 | tf_op jit(solution)/shard_map/psum | solution.py:104
  202.0 9.5 %scatter_custom_fusion = f32[2048,2048]{1,0:T(8,128)} fusion(s32[128]{0:T(128)} %get-tuple-element.15, f32[]{:T(128)} %constant.21.clone.1, bf16[1,128,2048]{2,1,0:T(8,128)(2,1)S(1)} %all_gather.19), kind=kCustom, calls=%fused_computation.2 | custom fusion | flops 524288 | bytes 17302016 | tf_op jit(solution)/shard_map/scatter-add | solution.py:128
  (123 shorter events, 38.4 us)
Async XLA Ops:
  7.2 37.9 %copy-start = (bf16[2048,8,64]{0,2,1:T(8,128)(2,1)S(1)}, bf16[2048,8,64]{0,2,1:T(8,128)(2,1)}, u32[]{:S(2)}) copy-start(bf16[2048,8,64]{0,2,1:T(8,128)(2,1)} %param.18) | copy-start | bytes 6291460
  7.2 41.6 %copy-start.8 = (bf16[2048,2,64]{0,2,1:T(8,128)(2,1)S(1)}, bf16[2048,2,64]{0,2,1:T(8,128)(2,1)}, u32[]{:S(2)}) copy-start(bf16[2048,2,64]{0,2,1:T(8,128)(2,1)} %param.20) | copy-start | bytes 1572868
  7.2 29.2 %reduce-scatter.6.cloned.1.call-start = ((), (), s32[]{:S(2)}) async-start(), calls=%async_computation.5 | async-start | bytes 655360 | tf_op jit(solution)/shard_map/reduce_scatter | solution.py:123
  14.6 38.6 %copy-start.10 = (bf16[1,32,2048]{2,1,0:T(8,128)(2,1)S(1)}, bf16[1,32,2048]{2,1,0:T(8,128)(2,1)}, u32[]{:S(2)}) copy-start(bf16[1,32,2048]{2,1,0:T(8,128)(2,1)} %param.25) | copy-start | bytes 393220
  15.6 56.2 %reduce-scatter.8.cloned.1.call-start = ((), (), s32[]{:S(2)}) async-start(), calls=%async_computation.6 | async-start | bytes 655360 | tf_op jit(solution)/shard_map/reduce_scatter | solution.py:59
  36.4 15.5 %copy-start.1 = (bf16[8,64,2048]{2,1,0:T(8,128)(2,1)S(1)}, bf16[8,64,2048]{2,1,0:T(8,128)(2,1)}, u32[]{:S(2)}) copy-start(bf16[8,64,2048]{2,1,0:T(8,128)(2,1)} %param.21) | copy-start | bytes 6291460
  36.4 35.4 %copy-start.3 = (bf16[1,32,2048]{2,1,0:T(8,128)(2,1)S(1)}, bf16[1,32,2048]{2,1,0:T(8,128)(2,1)}, u32[]{:S(2)}) copy-start(bf16[1,32,2048]{2,1,0:T(8,128)(2,1)} %reduce-scatter.6.cloned.1.call-done) | copy-start | bytes 393220
  37.6 8.2 %copy-start.26 = (f32[32]{0:T(128)}, f32[32]{0:T(128)S(1)}, u32[]{:S(2)}) copy-start(f32[32]{0:T(128)S(1)} %add_rsqrt_fusion.1) | copy-start | bytes 388
  47.9 37.4 %copy-start.13 = (bf16[1,128,8,32]{1,3,2,0:T(8,128)(2,1)}, bf16[1,128,8,32]{1,3,2,0:T(8,128)(2,1)S(1)}, u32[]{:S(2)}) copy-start(bf16[1,128,8,32]{1,3,2,0:T(8,128)(2,1)S(1)} %get-tuple-element.24) | copy-start | bytes 196612
  49.1 36.3 %copy-start.18 = (f32[128,128]{0,1}, f32[128,128]{0,1:S(1)}, u32[]{:S(2)}) copy-start(f32[128,128]{0,1:S(1)} %fusion.51) | copy-start | bytes 196612
  53.1 81.4 %reduce-scatter.12.cloned.1.call-start = ((), (), s32[]{:S(2)}) async-start(), calls=%async_computation.8 | async-start | bytes 655360 | tf_op jit(solution)/shard_map/reduce_scatter | solution.py:80
  71.7 13.7 %slice-start.2 = ((s8[8388608]{0:T(1024)(128)(4,1)}), s8[4194304]{0:T(1024)(128)(4,1)S(1)}, s32[]{:S(2)}) async-start(s8[8388608]{0:T(1024)(128)(4,1)} %bitcast.235), calls=%async_computation.12 | async-start | bytes 8388608
  85.4 11.6 %slice-start = ((s8[8388608]{0:T(1024)(128)(4,1)}), s8[4194304]{0:T(1024)(128)(4,1)S(1)}, s32[]{:S(2)}) async-start(s8[8388608]{0:T(1024)(128)(4,1)} %bitcast.233), calls=%async_computation.10 | async-start | bytes 8388608
  86.7 10.3 %slice-start.1 = ((s8[8388608]{0:T(1024)(128)(4,1)}), s8[4194304]{0:T(1024)(128)(4,1)S(1)}, s32[]{:S(2)}) async-start(s8[8388608]{0:T(1024)(128)(4,1)} %bitcast.233), calls=%async_computation.11 | async-start | bytes 8388608
  100.7 39.3 %reduce-scatter.10.cloned.1.call-start = ((), (), s32[]{:S(2)}) async-start(), calls=%async_computation.7 | async-start | bytes 655360 | tf_op jit(solution)/shard_map/reduce_scatter | solution.py:69
  116.2 65.2 %reduce-scatter.14.cloned.1.call-start = ((), (), s32[]{:S(2)}) async-start(), calls=%async_computation.9 | async-start | bytes 655360 | tf_op jit(solution)/shard_map/reduce_scatter | solution.py:101
  116.3 9.7 %copy-start.2 = (bf16[128,2048]{1,0:T(8,128)(2,1)S(1)}, bf16[128,2048]{1,0:T(8,128)(2,1)}, u32[]{:S(2)}) copy-start(bf16[128,2048]{1,0:T(8,128)(2,1)} %get-tuple-element.21) | copy-start | bytes 1572868
  116.3 9.7 %copy-start.5 = (bf16[1,128,2048]{2,1,0:T(8,128)(2,1)S(1)}, bf16[1,128,2048]{2,1,0:T(8,128)(2,1)}, u32[]{:S(2)}) copy-start(bf16[1,128,2048]{2,1,0:T(8,128)(2,1)} %all_gather.17) | copy-start | bytes 1572868
  126.0 8.6 %copy-start.16 = (f32[2048]{0:T(1024)S(1)}, f32[2048]{0:T(1024)}, u32[]{:S(2)}) copy-start(f32[2048]{0:T(1024)} %param.17) | copy-start | bytes 24580
  126.0 8.6 %copy-start.25 = (f32[32]{0:T(128)S(1)}, f32[32]{0:T(128)}, u32[]{:S(2)}) copy-start(f32[32]{0:T(128)} %copy-done.24) | copy-start | bytes 388
  126.0 14.1 %copy-start.11 = (bf16[1,32,2048]{2,1,0:T(8,128)(2,1)S(1)}, bf16[1,32,2048]{2,1,0:T(8,128)(2,1)}, u32[]{:S(2)}) copy-start(bf16[1,32,2048]{2,1,0:T(8,128)(2,1)} %param.25) | copy-start | bytes 393220
  160.7 20.8 %copy-start.17 = (f32[2048]{0:T(1024)S(1)}, f32[2048]{0:T(1024)}, u32[]{:S(2)}) copy-start(f32[2048]{0:T(1024)} %param.16) | copy-start | bytes 24580
  160.7 29.5 %copy-start.21 = (f32[2048]{0:T(1024)S(1)}, f32[2048]{0:T(1024)}, u32[]{:S(2)}) copy-start(f32[2048]{0:T(1024)} %get-tuple-element.13) | copy-start | bytes 24580
  164.9 16.6 %copy-start.27 = (f32[32]{0:T(128)S(1)}, f32[32]{0:T(128)}, u32[]{:S(2)}) copy-start(f32[32]{0:T(128)} %copy-done.26) | copy-start | bytes 388
  (13 other events, 27.2 us)
Sparse Core Ops, SparseCore 0:
  15.7 20.6 reduce-scatter.5
  53.2 18.4 reduce-scatter.7
  100.9 18.4 reduce-scatter.11
  122.2 17.7 reduce-scatter.9
  163.0 18.4 reduce-scatter.13
where the time goes:
time: 219 us; the launch traced here: 218 us
  matrix products  79.5 us (36%)
  blocking collectives  44.9 us (21%)
  waiting for transfers between devices  42.1 us (19%)
  other arithmetic  28.7 us (13%)
  between operations  14.3 us (7%)
  local copies, waits for them, and re-layouts  7.97 us (4%)
    reduce_scatter x1, waiting for transfers between devices, device_fn(): lax.psum_scatter(partial_emb, 'tp', scatter_dimension=1, tiled=True)  18.7 us
    reduce_scatter x1, waiting for transfers between devices, layer_pass(): lax.psum_scatter(attn_part, 'tp', scatter_dimension=1, tiled=True)  11.3 us
    psum x1, blocking collectives, layer_pass(): gain_grads = lax.psum(jnp.stack([gain_attn_part, gain_mlp_part]), 'tp')  11.1 us
    dot_general x1, matrix products, layer_pass(): jnp.einsum('bsd,bsf->df', gathered2, grad_gate, preferred_element_type=jn...  9.66 us
    dot_general x1, matrix products, layer_pass(): jnp.einsum('bsd,bsf->df', gathered2, grad_up, preferred_element_type=jnp....  9.57 us
    scatter-add x1, other arithmetic, device_fn(): jax.ops.segment_sum(grad_first_full.reshape(-1, grad_first_full.shape[-1]...  9.52 us
    unnamed x6, matrix products  9.08 us
    dot_general x1, matrix products, layer_pass(): jnp.einsum('bsf,bsd->fd', act_bf, grad_full, preferred_element_type=jnp.f...  8.53 us
  transfers between devices with their start and end apart: 5, of which 4 were waited for; matrix products, arithmetic and copies ran while one was open for 22% of the time, Pallas kernels for 0%

commit v1 on v0

v1 whole, which is shorter than its diff:
```python
import functools

import jax
import jax.numpy as jnp
import numpy as np
from jax import lax
from jax.experimental import pallas as pl
from jax.experimental.pallas import tpu as pltpu
from jax.sharding import PartitionSpec as P

ROPE_THETA = 1000000.0
RMS_EPS = 1e-5
MESH = pl.DeviceIdType.MESH
BF = jnp.bfloat16
F32 = jnp.float32

SEQ = 128
DIM = 2048
VLOC = 2048
FLOC = 2048
HLOC = 8
KVLOC = 2
HD = 64
QC = HLOC * HD
KC = KVLOC * HD
QKV = QC + 2 * KC
GROUP = HLOC // KVLOC
SCALE = HD ** -0.5
NC = 4
W = DIM // NC
VMEM = pltpu.VMEM
HBM = pltpu.HBM


def nn(a, b):
    return lax.dot_general(a, b, (((1,), (0,)), ((), ())), preferred_element_type=F32)


def nt(a, b):
    return lax.dot_general(a, b, (((1,), (1,)), ((), ())), preferred_element_type=F32)


def tn(a, b):
    return lax.dot_general(a, b, (((0,), (0,)), ((), ())), preferred_element_type=F32)


def place():
    tp = lax.axis_index("tp")
    x = tp // 2
    c = tp - 2 * x
    return x, c, 2 * x + (1 - c), 2 * (1 - x) + c


def greet(*peers):
    sem = pltpu.get_barrier_semaphore()
    for peer in peers:
        pl.semaphore_signal(sem, inc=1, device_id={"tp": peer}, device_id_type=MESH)
    pl.semaphore_wait(sem, len(peers))


def remote(src, dst, send, recv, peer):
    return pltpu.make_async_remote_copy(
        src_ref=src, dst_ref=dst, send_sem=send, recv_sem=recv, device_id={"tp": peer}, device_id_type=MESH)


def cols(j):
    return pl.ds(pl.multiple_of(j * W, W), W)


class PairSum:
    def __init__(self, part, got, own, sems, c, partner):
        self.part, self.got, self.own, self.c, self.partner = part, got, own, c, partner
        self.send, self.recv = sems

    def copy(self, j):
        return remote(self.part.at[:, 1 - self.c, :, cols(j)], self.got.at[:, :, cols(j)],
                      self.send.at[j], self.recv.at[j], self.partner)

    def put(self, j, value):
        self.part[:, :, :, cols(j)] = value.astype(BF).reshape(2, 2, 32, W)
        self.copy(j).start()

    def take(self, j):
        self.copy(j).wait_recv()
        total = self.part[:, self.c, :, cols(j)].astype(F32) + self.got[:, :, cols(j)].astype(F32)
        self.own[:, :, cols(j)] = total.astype(BF)

    def run(self, chunk, then=lambda j: None):
        def body(j, carry):
            self.put(j, chunk(j))

            @pl.when(j > 0)
            def _():
                self.take(j - 1)
                then(j - 1)
            return carry
        lax.fori_loop(0, NC, body, 0)
        self.take(NC - 1)
        then(NC - 1)

    def drain(self):
        for j in range(NC):
            self.copy(j).wait_send()


def rows16(fn):
    for b in range(2):
        for r in range(0, 32, 16):
            fn(b, slice(r, r + 16))


def norm_rows(x, gain):
    inv = lax.rsqrt(jnp.mean(x * x, axis=-1, keepdims=True) + RMS_EPS)
    return (x * inv * gain).astype(BF)


def norm_back(grad, x, gain):
    inv = lax.rsqrt(jnp.mean(x * x, axis=-1, keepdims=True) + RMS_EPS)
    normed = x * inv
    scaled = grad * gain
    back = inv * (scaled - normed * jnp.mean(scaled * normed, axis=-1, keepdims=True))
    return back, jnp.sum(grad * normed, axis=0, keepdims=True)


def spread(row):
    return jnp.transpose(jnp.broadcast_to(row, (SEQ, SEQ)))


def rope_pair(values, cos_tab, sin_tab):
    lane = lax.broadcasted_iota(jnp.int32, (SEQ, 128), 1)
    low = (lane % HD) < HD // 2
    other = jnp.where(low, pltpu.roll(values, 128 - HD // 2, 1), pltpu.roll(values, HD // 2, 1))
    return values * cos_tab + other * jnp.where(low, -sin_tab, sin_tab)


def probs_of(q, k):
    scores = nt(q, k) * SCALE
    causal = (lax.broadcasted_iota(jnp.int32, (SEQ, SEQ), 0) >= lax.broadcasted_iota(jnp.int32, (SEQ, SEQ), 1))
    scores = jnp.where(causal, scores, -1e30)
    e = jnp.exp(scores - jnp.max(scores, axis=-1, keepdims=True))
    return e / jnp.sum(e, axis=-1, keepdims=True)


def front_kernel(tok, pos, freq, gain_a, gain_m, gh, emb, wq, wk, wv, wo, wd, wg, wu,
                 n1_o, x0_o, qkv_o, cs_o, heads_o, h1_o, n2_o, act_o, ggate_o, gup_o, gfull_o, gn2_o, mlp_o,
                 emb_v, wqkv_v, wo_v, wd_v, wg_v, wu_v, hot_v, gact_v,
                 p0, g0, s0, r0, p1, g1, s1, r1, p2, g2, p3, g3,
                 emb_sem, w_sem, ps, pr, xs, xr, hs, hr, qs, qr):
    x, c, partner, cross = place()
    tp = 2 * x + c

    def fetch_emb(j):
        return pltpu.make_async_copy(emb.at[:, cols(j)], emb_v.at[:, cols(j)], emb_sem.at[j])

    fetches = (
        pltpu.make_async_copy(wq, wqkv_v.at[pl.ds(0, QC)], w_sem.at[0]),
        pltpu.make_async_copy(wk, wqkv_v.at[pl.ds(QC, KC)], w_sem.at[1]),
        pltpu.make_async_copy(wv, wqkv_v.at[pl.ds(QC + KC, KC)], w_sem.at[2]),
        pltpu.make_async_copy(wo, wo_v, w_sem.at[3]),
        pltpu.make_async_copy(wd, wd_v, w_sem.at[4]),
        pltpu.make_async_copy(wg, wg_v, w_sem.at[5]),
        pltpu.make_async_copy(wu, wu_v, w_sem.at[6]),
    )
    for j in range(NC):
        fetch_emb(j).start()
    greet(partner, cross)

    ids = spread(tok[...].astype(F32))
    base = (tp * VLOC).astype(F32)
    lane = lax.broadcasted_iota(jnp.int32, (SEQ, 128), 1).astype(F32)
    for v in range(VLOC // 128):
        hot_v[:, v * 128:(v + 1) * 128] = jnp.where(ids == lane + (base + float(v * 128)), 1.0, 0.0).astype(BF)

    def cross_copy(k, src, dst, j):
        return remote(src.at[:, :, cols(j)], dst.at[:, :, cols(j)], xs.at[k, j], xr.at[k, j], cross)

    sum0 = PairSum(p0, g0, s0, (ps.at[0], pr.at[0]), c, partner)

    def lookup(j):
        fetch_emb(j).wait()
        return nn(hot_v[...], emb_v[:, cols(j)])

    sum0.run(lookup, lambda j: cross_copy(0, s0, r0, j).start())
    for f in fetches:
        f.start()
    gfull_o[x, c] = gh[...]
    to_cross = remote(gh, gfull_o.at[x, c], hs.at[0], hr.at[0], cross)
    to_partner = remote(gh, gfull_o.at[x, c], hs.at[1], hr.at[1], partner)
    to_cross.start()
    to_partner.start()
    angle = spread(pos[...].astype(F32)) * freq[...]
    cs_o[0] = jnp.cos(angle)
    cs_o[1] = jnp.sin(angle)

    for j in range(NC):
        cross_copy(0, s0, r0, j).wait_recv()

    def first(b, r):
        xv = s0[b, r].astype(F32) + r0[b, r].astype(F32)
        x0_o[b, r] = xv.astype(BF)
        n1_o[b, c, r] = norm_rows(xv, gain_a[...])
    rows16(first)
    share1 = remote(n1_o.at[:, c], n1_o.at[:, c], hs.at[2], hr.at[2], partner)
    share1.start()
    for f in fetches[:3]:
        f.wait()
    share1.wait_recv()

    n1 = n1_o[...].reshape(SEQ, DIM)
    cos_tab, sin_tab = cs_o[0], cs_o[1]

    for v in range(QKV // 256):
        lin = nt(n1, wqkv_v[v * 256:(v + 1) * 256, :])
        for h in range(2):
            lo = v * 256 + h * 128
            piece = lin[:, h * 128:(h + 1) * 128]
            if lo < QC + KC:
                piece = rope_pair(piece, cos_tab, sin_tab)
            qkv_o[:, lo:lo + 128] = piece.astype(BF)
    for pair in range(HLOC // 2):
        outs = []
        for h in (2 * pair, 2 * pair + 1):
            g = h // GROUP
            k = qkv_o[:, QC + g * HD:QC + (g + 1) * HD]
            v = qkv_o[:, QC + KC + g * HD:QC + KC + (g + 1) * HD]
            probs = probs_of(qkv_o[:, h * HD:(h + 1) * HD], k).astype(BF)
            outs.append(nn(probs, v).astype(BF))
        heads_o[:, pair * 128:(pair + 1) * 128] = jnp.concatenate(outs, axis=1)
    to_cross.wait_recv()
    onward = remote(gfull_o.at[1 - x, c], gfull_o.at[1 - x, c], hs.at[3], hr.at[3], partner)
    onward.start()
    fetches[3].wait()

    sum1 = PairSum(p1, g1, s1, (ps.at[1], pr.at[1]), c, partner)
    sum1.run(lambda j: nn(heads_o[...], wo_v[:, cols(j)]), lambda j: cross_copy(1, s1, r1, j).start())

    to_partner.wait_recv()
    onward.wait_recv()
    fetches[4].wait()
    gfull = gfull_o[...].reshape(SEQ, DIM)

    def grad_act(j, carry):
        gact_v[:, cols(j)] = nt(gfull, wd_v[pl.ds(pl.multiple_of(j * W, W), W), :]).astype(BF)
        return carry
    lax.fori_loop(0, FLOC // W, grad_act, 0)

    for j in range(NC):
        cross_copy(1, s1, r1, j).wait_recv()

    def second(b, r):
        total = s1[b, r].astype(F32) + r1[b, r].astype(F32)
        h1 = (x0_o[b, r].astype(F32) + total).astype(BF)
        h1_o[b, r] = h1
        n2_o[b, c, r] = norm_rows(h1.astype(F32), gain_m[...])
    rows16(second)
    share2 = remote(n2_o.at[:, c], n2_o.at[:, c], hs.at[4], hr.at[4], partner)
    share2.start()
    fetches[5].wait()
    fetches[6].wait()
    share2.wait_recv()
    n2 = n2_o[...].reshape(SEQ, DIM)

    def mlp(j, carry):
        cj = pl.ds(pl.multiple_of(j * 256, 256), 256)
        gate = nn(n2, wg_v[:, cj])
        up = nn(n2, wu_v[:, cj])
        sig = jax.nn.sigmoid(gate)
        gate_act = gate * sig
        act_o[:, cj] = (gate_act * up).astype(BF)
        grad = gact_v[:, cj].astype(F32)
        gup_o[:, cj] = (grad * gate_act).astype(BF)
        ggate_o[:, cj] = (grad * up * sig * (1.0 + gate * (1.0 - sig))).astype(BF)
        return carry
    lax.fori_loop(0, FLOC // 256, mlp, 0)

    sum2 = PairSum(p2, g2, gn2_o, (ps.at[2], pr.at[2]), c, partner)

    def back_n2(j):
        rj = pl.ds(pl.multiple_of(j * W, W), W)
        return nt(ggate_o[...], wg_v[rj, :]) + nt(gup_o[...], wu_v[rj, :])
    sum2.run(back_n2)
    sum3 = PairSum(p3, g3, mlp_o, (ps.at[3], pr.at[3]), c, partner)
    sum3.run(lambda j: nn(act_o[...], wd_v[:, cols(j)]))

    for s in (sum0, sum1, sum2, sum3):
        s.drain()
    for j in range(NC):
        cross_copy(0, s0, r0, j).wait_send()
        cross_copy(1, s1, r1, j).wait_send()
    for copy in (to_cross, to_partner, share1, onward, share2):
        copy.wait_send()


def middle_kernel(gn2_own, gn2_got, mlp, h1, gfull, gain_m, qkv, cs, wq, wk, wv, wo,
                  gh1_o, gqkv_o, gn1_o, hid_o, gain_o,
                  wqkv_v, wo_v, gheads_v, mlp_got, p0, g0,
                  w_sem, ps, pr, hs, hr):
    x, c, partner, cross = place()
    fetches = (
        pltpu.make_async_copy(wo, wo_v, w_sem.at[3]),
        pltpu.make_async_copy(wq, wqkv_v.at[pl.ds(0, QC)], w_sem.at[0]),
        pltpu.make_async_copy(wk, wqkv_v.at[pl.ds(QC, KC)], w_sem.at[1]),
        pltpu.make_async_copy(wv, wqkv_v.at[pl.ds(QC + KC, KC)], w_sem.at[2]),
    )
    for f in fetches:
        f.start()
    greet(partner, cross)
    out_send = remote(mlp.at[1 - x], mlp_got, hs.at[0], hr.at[0], cross)
    out_send.start()

    gains = []

    def first(b, r):
        grad = (gn2_own[b, r].astype(F32) + gn2_got[b, r].astype(F32)).astype(BF).astype(F32)
        back, part = norm_back(grad, h1[b, r].astype(F32), gain_m[...])
        gh1_o[b, c, r] = (gfull[b, c, r].astype(F32) + back).astype(BF)
        gains.append(part)
    rows16(first)
    share = remote(gh1_o.at[:, c], gh1_o.at[:, c], hs.at[1], hr.at[1], partner)
    share.start()
    gain_o[...] = gains[0] + gains[1] + gains[2] + gains[3]
    fetches[0].wait()
    share.wait_recv()

    gh1 = gh1_o[...].reshape(SEQ, DIM)
    for v in range(QC // 256):
        gheads_v[:, v * 256:(v + 1) * 256] = nt(gh1, wo_v[v * 256:(v + 1) * 256, :]).astype(BF)

    cos_tab, sin_tab = cs[0], -cs[1]
    gks, gvs = [], []
    for g in range(KVLOC):
        k = qkv[:, QC + g * HD:QC + (g + 1) * HD]
        v = qkv[:, QC + KC + g * HD:QC + KC + (g + 1) * HD]
        gk = gv = None
        for pair in range(GROUP // 2):
            outs = []
            for h in (g * GROUP + 2 * pair, g * GROUP + 2 * pair + 1):
                q = qkv[:, h * HD:(h + 1) * HD]
                probs = probs_of(q, k)
                gh = gheads_v[:, h * HD:(h + 1) * HD]
                gp = nt(gh, v).astype(BF).astype(F32)
                gvh = tn(probs.astype(BF), gh)
                gs = (probs * (gp - jnp.sum(gp * probs, axis=-1, keepdims=True)) * SCALE).astype(BF)
                outs.append(nn(gs, k).astype(BF).astype(F32))
                gkh = tn(gs, q)
                gk = gkh if gk is None else gk + gkh
                gv = gvh if gv is None else gv + gvh
            lo = (g * GROUP + 2 * pair) * HD
            gqkv_o[:, lo:lo + 128] = rope_pair(jnp.concatenate(outs, axis=1), cos_tab, sin_tab).astype(BF)
        gks.append(gk.astype(BF).astype(F32))
        gvs.append(gv.astype(BF))
    gqkv_o[:, QC:QC + KC] = rope_pair(jnp.concatenate(gks, axis=1), cos_tab, sin_tab).astype(BF)
    gqkv_o[:, QC + KC:] = jnp.concatenate(gvs, axis=1)

    for f in fetches[1:]:
        f.wait()
    sum0 = PairSum(p0, g0, gn1_o, (ps, pr), c, partner)
    sum0.run(lambda j: nn(gqkv_o[...], wqkv_v[:, cols(j)]))
    out_send.wait_recv()
    hid_o[...] = (h1[x].astype(F32) + (mlp[x].astype(F32) + mlp_got[...].astype(F32))).astype(BF)
    sum0.drain()
    out_send.wait_send()
    share.wait_send()


def back_kernel(gn1_own, gn1_got, x0, gh1, gain_a, gain_mp, gx_o, gain_o, gbuf, hs, hr):
    x, c, partner, cross = place()
    greet(partner)
    gains = []

    def first(b, r):
        grad = (gn1_own[b, r].astype(F32) + gn1_got[b, r].astype(F32)).astype(BF).astype(F32)
        back, part = norm_back(grad, x0[b, r].astype(F32), gain_a[...])
        gx_o[b, c, r] = (gh1[b, c, r].astype(F32) + back).astype(BF)
        gains.append(part)
    rows16(first)
    gbuf[c, 0:1] = gains[0] + gains[1] + gains[2] + gains[3]
    gbuf[c, 1:2] = gain_mp[...]
    share = remote(gx_o.at[:, c], gx_o.at[:, c], hs.at[0], hr.at[0], partner)
    share.start()
    share_gain = remote(gbuf.at[c], gbuf.at[c], hs.at[1], hr.at[1], partner)
    share_gain.start()
    share_gain.wait_recv()
    gain_o[...] = gbuf[0, 0:2] + gbuf[1, 0:2]
    share.wait_recv()
    share.wait_send()
    share_gain.wait_send()


NB = 4
BM = 256


def outer_kernel(spec, *refs):
    n_in = 1 + max(max(l, r) for l, r, _ in spec)
    ins, outs = refs[:n_in], refs[n_in:n_in + len(spec)]
    buf, sem = refs[n_in + len(spec):]

    done = 0
    copies = []
    for (l, r, off), out in zip(spec, outs):
        lhs, rhs = ins[l], ins[r]
        steps = out.shape[0] // BM if lhs is not None else 0
        bm = min(BM, out.shape[0])
        steps = out.shape[0] // bm
        if bm == BM:
            def copy(i, out=out, done=done):
                slot = lax.rem(i + done, NB)
                return pltpu.make_async_copy(buf.at[slot], out.at[pl.ds(pl.multiple_of(i * BM, BM), BM)], sem.at[slot])

            def step(i, carry, copy=copy, lhs=lhs, rhs=rhs, off=off, done=done):
                slot = lax.rem(i + done, NB)

                @pl.when(i + done >= NB)
                def _():
                    copy(i).wait()
                a = lhs[:, pl.ds(pl.multiple_of(off + i * BM, 128), BM)]
                buf[slot] = tn(a, rhs[...])
                copy(i).start()
                return carry
            lax.fori_loop(0, steps, step, 0)
            done += steps
        else:
            slot = done % NB
            if done >= NB:
                pltpu.make_async_copy(buf.at[slot], outs[0].at[pl.ds(0, BM)], sem.at[slot]).wait()
            buf[slot, 0:bm] = tn(lhs[:, off:off + bm], rhs[...])
            copies.append(pltpu.make_async_copy(buf.at[slot, pl.ds(0, bm)], out, sem.at[slot]))
            copies[-1].start()
            done += 1
    small = len(copies)
    for k in range(max(0, done - NB), done - small):
        slot = k % NB
        pltpu.make_async_copy(buf.at[slot], outs[0].at[pl.ds(0, BM)], sem.at[slot]).wait()
    for copy in copies:
        copy.wait()


def outer(ins, spec, rows):
    total = sum(rows)
    return pl.pallas_call(
        functools.partial(outer_kernel, spec),
        out_shape=tuple(jax.ShapeDtypeStruct((m, DIM), F32) for m in rows),
        in_specs=[pl.BlockSpec(memory_space=VMEM)] * len(ins),
        out_specs=tuple(pl.BlockSpec(memory_space=HBM) for _ in rows),
        scratch_shapes=[pltpu.VMEM((NB, BM, DIM), F32), pltpu.SemaphoreType.DMA((NB,))],
        cost_estimate=pl.CostEstimate(flops=2 * total * DIM * SEQ, bytes_accessed=4 * total * DIM, transcendentals=0),
        compiler_params=pltpu.CompilerParams(vmem_limit_bytes=24 * 2 ** 20),
    )(*ins)


def emb_kernel(tok, gx, out, buf, sem):
    base = lax.axis_index("tp") * VLOC
    ids = jnp.broadcast_to(tok[...], (BM, SEQ)) - base
    row = lax.broadcasted_iota(jnp.int32, (BM, SEQ), 0)
    grad = gx[...].reshape(SEQ, DIM)

    def copy(i):
        slot = lax.rem(i, NB)
        return pltpu.make_async_copy(buf.at[slot], out.at[pl.ds(pl.multiple_of(i * BM, BM), BM)], sem.at[slot])

    def step(i, carry):
        @pl.when(i >= NB)
        def _():
            copy(i).wait()
        hot = jnp.where(ids == row + i * BM, 1.0, 0.0).astype(BF)
        buf[lax.rem(i, NB)] = nn(hot, grad)
        copy(i).start()
        return carry
    steps = VLOC // BM
    lax.fori_loop(0, steps, step, 0)
    for k in range(steps - NB, steps):
        copy(k).wait()


def vm(n):
    return [pl.BlockSpec(memory_space=VMEM)] * n


def hb(n):
    return [pl.BlockSpec(memory_space=HBM)] * n


def sds(shape, dtype=BF):
    return jax.ShapeDtypeStruct(shape, dtype)


FULL = (2, 2, 32, DIM)
MINE = (2, 32, DIM)


def dma(*shape):
    return pltpu.SemaphoreType.DMA(shape)


def device_fn(tokens, positions, emb, gain_a, gain_m, wq, wk, wv, wo, wg, wu, wd, gh):
    inv_freq = (ROPE_THETA ** (-np.arange(HD // 2, dtype=np.float32) * np.float32(2.0 / HD))).astype(np.float32)
    freq = jnp.asarray(np.tile(inv_freq, 4)[None, :])
    ga, gm = gain_a.reshape(1, DIM), gain_m.reshape(1, DIM)
    flat = lambda w: jnp.transpose(w, (1, 2, 0)).reshape(-1, DIM)
    wqt, wkt, wvt = flat(wq), flat(wk), flat(wv)
    wo2 = wo.reshape(QC, DIM)
    gh2 = gh.reshape(32, DIM)

    n1, x0, qkv, cs, heads, h1, n2, act, ggate, gup, gfull, gn2, mlp = pl.pallas_call(
        front_kernel,
        out_shape=(sds(FULL), sds(MINE), sds((SEQ, QKV)), sds((2, SEQ, 128), F32), sds((SEQ, QC)), sds(MINE),
                   sds(FULL), sds((SEQ, FLOC)), sds((SEQ, FLOC)), sds((SEQ, FLOC)), sds(FULL), sds(MINE), sds(MINE)),
        in_specs=vm(6) + hb(8),
        out_specs=tuple(vm(13)),
        scratch_shapes=[
            pltpu.VMEM((VLOC, DIM), BF), pltpu.VMEM((QKV, DIM), BF), pltpu.VMEM((QC, DIM), BF),
            pltpu.VMEM((FLOC, DIM), BF), pltpu.VMEM((DIM, FLOC), BF), pltpu.VMEM((DIM, FLOC), BF),
            pltpu.VMEM((SEQ, VLOC), BF), pltpu.VMEM((SEQ, FLOC), BF),
            pltpu.VMEM(FULL, BF), pltpu.VMEM(MINE, BF), pltpu.VMEM(MINE, BF), pltpu.VMEM(MINE, BF),
            pltpu.VMEM(FULL, BF), pltpu.VMEM(MINE, BF), pltpu.VMEM(MINE, BF), pltpu.VMEM(MINE, BF),
            pltpu.VMEM(FULL, BF), pltpu.VMEM(MINE, BF), pltpu.VMEM(FULL, BF), pltpu.VMEM(MINE, BF),
            dma(NC), dma(7), dma(4, NC), dma(4, NC), dma(2, NC), dma(2, NC), dma(5), dma(5), dma(1), dma(1)],
        compiler_params=pltpu.CompilerParams(collective_id=0, has_side_effects=True, vmem_limit_bytes=52 * 2 ** 20),
    )(tokens, positions, freq, ga, gm, gh2, emb, wqt, wkt, wvt, wo2, wd, wg, wu)

    swap = [(i, i ^ 2) for i in range(4)]
    gn2_got = lax.ppermute(gn2, 'tp', swap)
    gfull2 = gfull.reshape(SEQ, DIM)
    n2f = n2.reshape(SEQ, DIM)
    g_gate, = outer((n2f, ggate), ((0, 1, 0),), (DIM,))

    gh1, gqkv, gn1, hidden, gain_mp = pl.pallas_call(
        middle_kernel,
        out_shape=(sds(FULL), sds((SEQ, QKV)), sds(MINE), sds((32, DIM)), sds((1, DIM), F32)),
        in_specs=vm(8) + hb(4),
        out_specs=tuple(vm(5)),
        scratch_shapes=[
            pltpu.VMEM((QKV, DIM), BF), pltpu.VMEM((QC, DIM), BF), pltpu.VMEM((SEQ, QC), BF), pltpu.VMEM((32, DIM), BF),
            pltpu.VMEM(FULL, BF), pltpu.VMEM(MINE, BF), dma(4), dma(NC), dma(NC), dma(2), dma(2)],
        compiler_params=pltpu.CompilerParams(collective_id=1, has_side_effects=True, vmem_limit_bytes=24 * 2 ** 20),
    )(gn2, gn2_got, mlp, h1, gfull, gm, qkv, cs, wqt, wkt, wvt, wo2)

    gn1_got = lax.ppermute(gn1, 'tp', swap)
    g_up, g_down, g_out, g_q, g_k, g_v = outer(
        (n2f, gup, act, gfull2, heads, gh1.reshape(SEQ, DIM), gqkv, n1.reshape(SEQ, DIM)),
        ((0, 1, 0), (2, 3, 0), (4, 5, 0), (6, 7, 0), (6, 7, QC), (6, 7, QC + KC)),
        (DIM, FLOC, QC, QC, KC, KC))

    gx, gains = pl.pallas_call(
        back_kernel,
        out_shape=(sds(FULL), sds((2, DIM), F32)),
        in_specs=vm(6),
        out_specs=tuple(vm(2)),
        scratch_shapes=[pltpu.VMEM((2, 8, DIM), F32), dma(2), dma(2)],
        compiler_params=pltpu.CompilerParams(collective_id=2, has_side_effects=True, vmem_limit_bytes=16 * 2 ** 20),
    )(gn1, gn1_got, x0, gh1, ga, gain_mp)

    g_emb = pl.pallas_call(
        emb_kernel,
        out_shape=sds((VLOC, DIM), F32),
        in_specs=vm(2),
        out_specs=hb(1)[0],
        scratch_shapes=[pltpu.VMEM((NB, BM, DIM), F32), dma(NB)],
        compiler_params=pltpu.CompilerParams(vmem_limit_bytes=24 * 2 ** 20),
    )(tokens, gx)

    back3 = lambda g: jnp.transpose(g.reshape(-1, HD, DIM), (2, 0, 1))
    return (hidden.reshape(1, 32, DIM), g_emb, back3(g_q), back3(g_k), back3(g_v), g_out.reshape(HLOC, HD, DIM),
            g_gate, g_up, g_down, gains[0], gains[1])


def solution(mesh):
    in_specs = (P('dp', None), P('dp', None), P('tp', None), P(None), P(None),
                P(None, 'tp', None), P(None, 'tp', None), P(None, 'tp', None), P('tp', None, None),
                P(None, 'tp'), P(None, 'tp'), P('tp', None), P('dp', 'tp', None))
    out_specs = (P('dp', 'tp', None), P(('dp', 'tp'), None),
                 P('dp', 'tp', None), P('dp', 'tp', None), P('dp', 'tp', None), P(('dp', 'tp'), None, None),
                 P('dp', 'tp'), P('dp', 'tp'), P(('dp', 'tp'), None), P('dp'), P('dp'))
    return jax.shard_map(device_fn, mesh=mesh, in_specs=in_specs, out_specs=out_specs, check_vma=False)
```

time: 219 us -> 98.1 us (0.45)
  Pallas kernels: 0 us -> 86.6 us
  matrix products: 79.5 us -> 0 us
  blocking collectives: 44.9 us -> 0 us
  waiting for transfers between devices: 42.1 us -> 0.01 us
  other arithmetic: 28.7 us -> 0 us
  between operations: 14.3 us -> 0.82 us
  starting transfers between devices: 0.43 us -> 2.72 us
    pallas_call x0 -> x6, Pallas kernels: none -> 86.6 us  [the longest x1 45.7 us: device_fn(): pl.pallas_call(front_kernel, out_shape=(sds(FULL), sds(MINE), sds((SEQ, Q...]
    dot_general x21 -> x0, matrix products: 70.5 us -> none  [the longest x1 9.66 us: layer_pass(): jnp.einsum('bsd,bsf->df', gathered2, grad_gate, preferred_element_type=jn...]
    reduce_scatter x5 -> x0, waiting for transfers between devices: 42 us -> none  [the longest x1 18.7 us: device_fn(): lax.psum_scatter(partial_emb, 'tp', scatter_dimension=1, tiled=True)]
    all_gather x5 -> x0, blocking collectives: 33.8 us -> none  [the longest x1 7.28 us: layer_pass(): grad_full = lax.all_gather(grad_hidden, 'tp', axis=1, tiled=True)]
    psum x1 -> x0, blocking collectives: 11.1 us -> none  [layer_pass(): gain_grads = lax.psum(jnp.stack([gain_attn_part, gain_mlp_part]), 'tp')]
    scatter-add x1 -> x0, other arithmetic: 9.52 us -> none  [device_fn(): jax.ops.segment_sum(grad_first_full.reshape(-1, grad_first_full.shape[-1]...]
    unnamed x6 -> x0, matrix products: 9.08 us -> none
    gather x1 -> x0, local copies, waits for them, and re-layouts: 5.9 us -> none  [device_fn(): jnp.take(emb_shard, jnp.clip(local_ids, 0, rows_local - 1), axis=0)]
  transfers between devices with their start and end apart: 5 -> 2, of which waited for: 4 -> 0; matrix products, arithmetic and copies ran while one was open for 22% -> 0% of each run, Pallas kernels for 0% -> 23%
where the time goes in v1:
time: 98.1 us; the launch traced here: 97.8 us
  Pallas kernels  86.6 us (88%)
  local copies, waits for them, and re-layouts  7.64 us (8%)
  starting transfers between devices  2.72 us (3%)
    pallas_call x1, Pallas kernels, device_fn(): pl.pallas_call(front_kernel, out_shape=(sds(FULL), sds(MINE), sds((SEQ, Q...  45.7 us
    pallas_call x2, Pallas kernels, outer(): pl.pallas_call(functools.partial(outer_kernel, spec), out_shape=tuple((ja...  22.4 us
    pallas_call x1, Pallas kernels, device_fn(): pl.pallas_call(middle_kernel, out_shape=(sds(FULL), sds((SEQ, QKV)), sds(...  9.97 us
    unnamed x35, local copies, waits for them, and re-layouts  7.03 us
    pallas_call x1, Pallas kernels, device_fn(): pl.pallas_call(emb_kernel, out_shape=sds((VLOC, DIM), F32), in_specs=vm(2...  6.34 us
    pallas_call x1, Pallas kernels, device_fn(): pl.pallas_call(back_kernel, out_shape=(sds(FULL), sds((2, DIM), F32)), in...  2.14 us
  transfers between devices with their start and end apart: 2, of which 0 were waited for; matrix products, arithmetic and copies ran while one was open for 0% of the time, Pallas kernels for 23%

profile of v1, /device:TPU:0, one launch (start us, length us, event | category | flops | bytes accessed | tf_op | source)
XLA Modules:
  0.0 97.8 jit_solution(5387599173296868549)
XLA Ops:
  0.7 0.9 copy-done.8
  1.6 0.7 copy-done.9
  2.3 0.7 copy-done.10
  2.9 0.7 copy-done.11
  3.6 0.7 copy-done.12
  4.3 0.7 copy-done.13
  4.9 45.7 %shard_map.221 = (bf16[2,2,32,2048]{3,2,1,0:T(8,128)(2,1)}, bf16[2,32,2048]{2,1,0:T(8,128)(2,1)S(1)}, bf16[128,768]{1,0:T(8,128)(2,1)S(1)}, f32[2,128,128]{2,1,0...) custom-call(s32[1,128]{1,0:T(1,128)S(1)} %copy-done.11, ...), custom_call_target="tpu_custom_call" | custom-call | tf_op jit(solution)/shard_map/pallas_call | solution.py:505
  50.7 1.4 %collective-permute-start = (bf16[2,32,2048]{2,1,0:T(8,128)(2,1)S(1)}, bf16[2,32,2048]{2,1,0:T(8,128)(2,1)S(1)}, u32[]{:S(2)}, u32[]{:S(2)}) collective-permute-start(bf16[2,32,2048]{2,1,0:T(8,128)(2,1)S(1)} %get-tuple-element.37.gn2_own), channel_id=1, source_target_pairs={{0,2},{1,3},{2,0},{3,1},{4,6},{5,7},{6,4},{7,5},{8,10},{9,11},{10,... | collective-permute-start | bytes 786440 | tf_op jit(solution)/shard_map/ppermute | solution.py:523
  52.0 1.0 %copy-done.4 = bf16[2,2,32,2048]{3,2,1,0:T(8,128)(2,1)S(1)} copy-done((bf16[2,2,32,2048]{3,2,1,0:T(8,128)(2,1)S(1)}, bf16[2,2,32,2048]{3,2,1,0:T(8,128)(2,1)}, u32[]{:S(2)}) %copy-start.4) | copy-done | bytes 524312
  53.1 1.0 %copy-done.6 = bf16[128,2048]{1,0:T(8,128)(2,1)S(1)} copy-done((bf16[128,2048]{1,0:T(8,128)(2,1)S(1)}, bf16[128,2048]{1,0:T(8,128)(2,1)}, u32[]{:S(2)}) %copy-start.6) | copy-done | bytes 524312
  54.1 0.0 copy-start.7
  54.1 0.0 copy-start.5
  54.1 0.0 copy-start.14
  54.2 0.0 copy-start.15
  54.2 7.9 %shard_map.226 = f32[2048,2048]{1,0:T(8,128)} custom-call(bf16[128,2048]{1,0:T(8,128)(2,1)S(1)} %bitcast.38, bf16[128,2048]{1,0:T(8,128)(2,1)S(1)} %copy-done.6), custom_call_target="tpu_custom_call" | custom-call | flops 1073741824 | bytes 16777216 | tf_op jit(solution)/shard_map/pallas_call | solution.py:441
  62.0 0.0 collective-permute-done.gn2_got
  62.1 10.0 %shard_map.222 = (bf16[2,2,32,2048]{3,2,1,0:T(8,128)(2,1)S(1)}, bf16[128,768]{1,0:T(8,128)(2,1)S(1)}, bf16[2,32,2048]{2,1,0:T(8,128)(2,1)S(1)}, bf16[32,2048]{1,0:T(8,128)(2,1)S(1)}, f32[1,2048]{1,0:T(1,128)S(1)}) custom-call(bf16[2,32,2048]{2,1,0:T(8,128)(2,1)S(1)} %get-tuple-element.37.gn2_own, bf16[2,32,2048]{2,1,0:T(8,128)(2,1)S(1)} %collective-permute-done.gn2_got, ...), custom_call_target="tpu_custom_call" | custom-call | tf_op jit(solution)/shard_map/pallas_call | solution.py:528
  72.1 1.4 %collective-permute-start.1 = (bf16[2,32,2048]{2,1,0:T(8,128)(2,1)S(1)}, bf16[2,32,2048]{2,1,0:T(8,128)(2,1)S(1)}, u32[]{:S(2)}, u32[]{:S(2)}) collective-permute-start(bf16[2,32,2048]{2,1,0:T(8,128)(2,1)S(1)} %get-tuple-element.44.gn1_own), channel_id=1, source_target_pairs={{0,2},{1,3},{2,0},{3,1},{4,6},{5,7},{6,4},{7,5},{8,10},{9,11},{10,... | collective-permute-start | bytes 786440 | tf_op jit(solution)/shard_map/ppermute | solution.py:539
  73.5 14.5 %shard_map.225 = (f32[2048,2048]{1,0:T(8,128)}, f32[2048,2048]{1,0:T(8,128)}, f32[512,2048]{1,0:T(8,128)}, f32[512,2048]{1,0:T(8,128)}, f32[128,2048]{1,0:T(8,128)}, /*index=5*/f32[128,2048]{1,0:T(8,128)}) custom-call(bf16[128,2048]{1,0:T(8,128)(2,1)S(1)} %bitcast.39, bf16[128,2048]{1,0:T(8,128)(2,1)S(1)} %copy-done.16, bf16[128,2048]{1,0:T(8,128)(2,1)S(1)} %copy-done.15, ...), custom_call_target="tpu_custom_call" | custom-call | flops 2818572288 | bytes 44040192 | tf_op jit(solution)/shard_map/pallas_call | solution.py:441
  88.0 0.0 collective-permute-done.1.gn1_got
  88.0 2.1 %shard_map.223 = (bf16[2,2,32,2048]{3,2,1,0:T(8,128)(2,1)S(1)}, f32[2,2048]{1,0:T(2,128)S(1)}) custom-call(bf16[2,32,2048]{2,1,0:T(8,128)(2,1)S(1)} %get-tuple-element.44.gn1_own, bf16[2,32,2048]{2,1,0:T(8,128)(2,1)S(1)} %collective-permute-done.1.gn1_got, bf16[2,32,2048]{2,1,0:T(8,128)(2,1)S(1)} %get-tuple-element.45.x0, ...), custom_call_target="tpu_custom_call" | custom-call | tf_op jit(solution)/shard_map/pallas_call | solution.py:545
  90.1 6.3 %shard_map.224 = f32[2048,2048]{1,0:T(8,128)} custom-call(s32[1,128]{1,0:T(1,128)S(1)} %copy-done.11, bf16[2,2,32,2048]{3,2,1,0:T(8,128)(2,1)S(1)} %get-tuple-element.48.gx), custom_call_target="tpu_custom_call" | custom-call | tf_op jit(solution)/shard_map/pallas_call | solution.py:554
  96.5 0.6 fusion
  97.1 0.7 copy.26
  (22 shorter events, 0.0 us)
Async XLA Ops:
  0.6 0.9 copy-start.8
  1.6 0.7 copy-start.9
  2.2 0.7 copy-start.10
  2.9 0.7 copy-start.11
  3.6 0.7 copy-start.12
  4.3 0.7 copy-start.13
  50.7 11.4 %collective-permute-start = (bf16[2,32,2048]{2,1,0:T(8,128)(2,1)S(1)}, bf16[2,32,2048]{2,1,0:T(8,128)(2,1)S(1)}, u32[]{:S(2)}, u32[]{:S(2)}) collective-permute-start(bf16[2,32,2048]{2,1,0:T(8,128)(2,1)S(1)} %get-tuple-element.37.gn2_own), channel_id=1, source_target_pairs={{0,2},{1,3},{2,0},{3,1},{4,6},{5,7},{6,4},{7,5},{8,10},{9,11},{10,... | collective-permute-start | bytes 786440 | tf_op jit(solution)/shard_map/ppermute | solution.py:523
  52.0 1.0 %copy-start.4 = (bf16[2,2,32,2048]{3,2,1,0:T(8,128)(2,1)S(1)}, bf16[2,2,32,2048]{3,2,1,0:T(8,128)(2,1)}, u32[]{:S(2)}) copy-start(bf16[2,2,32,2048]{3,2,1,0:T(8,128)(2,1)} %get-tuple-element.49) | copy-start | bytes 1572868
  53.1 1.0 %copy-start.6 = (bf16[128,2048]{1,0:T(8,128)(2,1)S(1)}, bf16[128,2048]{1,0:T(8,128)(2,1)}, u32[]{:S(2)}) copy-start(bf16[128,2048]{1,0:T(8,128)(2,1)} %get-tuple-element.59.refs_1_) | copy-start | bytes 1572868
  54.1 7.9 %copy-start = (bf16[2048,8,64]{0,2,1:T(8,128)(2,1)S(1)}, bf16[2048,8,64]{0,2,1:T(8,128)(2,1)}, u32[]{:S(2)}) copy-start(bf16[2048,8,64]{0,2,1:T(8,128)(2,1)} %param.19) | copy-start | bytes 6291460
  54.1 7.9 %copy-start.1 = (bf16[8,64,2048]{2,1,0:T(8,128)(2,1)S(1)}, bf16[8,64,2048]{2,1,0:T(8,128)(2,1)}, u32[]{:S(2)}) copy-start(bf16[8,64,2048]{2,1,0:T(8,128)(2,1)} %param.22) | copy-start | bytes 6291460
  54.1 8.0 %copy-start.2 = (bf16[2048,2,64]{0,2,1:T(8,128)(2,1)S(1)}, bf16[2048,2,64]{0,2,1:T(8,128)(2,1)}, u32[]{:S(2)}) copy-start(bf16[2048,2,64]{0,2,1:T(8,128)(2,1)} %param.20) | copy-start | bytes 1572868
  54.1 8.0 %copy-start.3 = (bf16[2048,2,64]{0,2,1:T(8,128)(2,1)S(1)}, bf16[2048,2,64]{0,2,1:T(8,128)(2,1)}, u32[]{:S(2)}) copy-start(bf16[2048,2,64]{0,2,1:T(8,128)(2,1)} %param.21) | copy-start | bytes 1572868
  54.1 8.0 %copy-start.7 = (bf16[2,2,32,2048]{3,2,1,0:T(8,128)(2,1)S(1)}, bf16[2,2,32,2048]{3,2,1,0:T(8,128)(2,1)}, u32[]{:S(2)}) copy-start(bf16[2,2,32,2048]{3,2,1,0:T(8,128)(2,1)} %get-tuple-element.40.gfull) | copy-start | bytes 1572868
  54.1 19.3 %copy-start.5 = (bf16[2,2,32,2048]{3,2,1,0:T(8,128)(2,1)S(1)}, bf16[2,2,32,2048]{3,2,1,0:T(8,128)(2,1)}, u32[]{:S(2)}) copy-start(bf16[2,2,32,2048]{3,2,1,0:T(8,128)(2,1)} %get-tuple-element.49) | copy-start | bytes 1572868
  54.1 19.3 %copy-start.14 = (bf16[2,2,32,2048]{3,2,1,0:T(8,128)(2,1)S(1)}, bf16[2,2,32,2048]{3,2,1,0:T(8,128)(2,1)}, u32[]{:S(2)}) copy-start(bf16[2,2,32,2048]{3,2,1,0:T(8,128)(2,1)} %get-tuple-element.54) | copy-start | bytes 1572868
  54.2 19.3 %copy-start.15 = (bf16[128,2048]{1,0:T(8,128)(2,1)S(1)}, bf16[128,2048]{1,0:T(8,128)(2,1)}, u32[]{:S(2)}) copy-start(bf16[128,2048]{1,0:T(8,128)(2,1)} %get-tuple-element.51.refs_2_) | copy-start | bytes 1572868
  54.2 19.3 %copy-start.16 = (bf16[128,2048]{1,0:T(8,128)(2,1)S(1)}, bf16[128,2048]{1,0:T(8,128)(2,1)}, u32[]{:S(2)}) copy-start(bf16[128,2048]{1,0:T(8,128)(2,1)} %get-tuple-element.50.refs_1_) | copy-start | bytes 1572868
  72.1 15.9 %collective-permute-start.1 = (bf16[2,32,2048]{2,1,0:T(8,128)(2,1)S(1)}, bf16[2,32,2048]{2,1,0:T(8,128)(2,1)S(1)}, u32[]{:S(2)}, u32[]{:S(2)}) collective-permute-start(bf16[2,32,2048]{2,1,0:T(8,128)(2,1)S(1)} %get-tuple-element.44.gn1_own), channel_id=1, source_target_pairs={{0,2},{1,3},{2,0},{3,1},{4,6},{5,7},{6,4},{7,5},{8,10},{9,11},{10,... | collective-permute-start | bytes 786440 | tf_op jit(solution)/shard_map/ppermute | solution.py:539

commit v2 on v1

--- a/solution.py
+++ b/solution.py
@@ -83,7 +83,7 @@
     def take(self, j):
         self.copy(j).wait_recv()
         total = self.part[:, self.c, :, cols(j)].astype(F32) + self.got[:, :, cols(j)].astype(F32)
-        self.own[:, :, cols(j)] = total.astype(BF)
+        self.own[0:2, :, cols(j)] = total.astype(BF)
 
     def run(self, chunk, then=lambda j: None):
         def body(j, carry):
@@ -142,30 +142,35 @@
 
 
 def front_kernel(tok, pos, freq, gain_a, gain_m, gh, emb, wq, wk, wv, wo, wd, wg, wu,
-                 n1_o, x0_o, qkv_o, cs_o, heads_o, h1_o, n2_o, act_o, ggate_o, gup_o, gfull_o, gn2_o, mlp_o,
-                 emb_v, wqkv_v, wo_v, wd_v, wg_v, wu_v, hot_v, gact_v,
-                 p0, g0, s0, r0, p1, g1, s1, r1, p2, g2, p3, g3,
-                 emb_sem, w_sem, ps, pr, xs, xr, hs, hr, qs, qr):
+                 n1_o, x0_o, qkv_o, cs_o, heads_o, h1_o, n2_o, act_o, ggate_o, gup_o, gfull_o, gn2_o,
+                 wqkv_v, wo_v, wd_v,
+                 tok_v, pos_v, freq_v, ga_v, gm_v, emb_v, wg_v, wu_v, wut_v, wqkvt_v, hot_v, gact_v,
+                 p0, g0, s0, r0, p1, g1, s1, r1, p2, g2,
+                 in_sem, emb_sem, w_sem, ps, pr, xs, xr, hs, hr):
     x, c, partner, cross = place()
     tp = 2 * x + c
 
     def fetch_emb(j):
         return pltpu.make_async_copy(emb.at[:, cols(j)], emb_v.at[:, cols(j)], emb_sem.at[j])
 
-    fetches = (
-        pltpu.make_async_copy(wq, wqkv_v.at[pl.ds(0, QC)], w_sem.at[0]),
-        pltpu.make_async_copy(wk, wqkv_v.at[pl.ds(QC, KC)], w_sem.at[1]),
-        pltpu.make_async_copy(wv, wqkv_v.at[pl.ds(QC + KC, KC)], w_sem.at[2]),
-        pltpu.make_async_copy(wo, wo_v, w_sem.at[3]),
-        pltpu.make_async_copy(wd, wd_v, w_sem.at[4]),
-        pltpu.make_async_copy(wg, wg_v, w_sem.at[5]),
-        pltpu.make_async_copy(wu, wu_v, w_sem.at[6]),
-    )
-    for j in range(NC):
-        fetch_emb(j).start()
+    get_q = pltpu.make_async_copy(wq, wqkv_v.at[pl.ds(0, QC)], w_sem.at[0])
+    get_k = pltpu.make_async_copy(wk, wqkv_v.at[pl.ds(QC, KC)], w_sem.at[1])
+    get_v = pltpu.make_async_copy(wv, wqkv_v.at[pl.ds(QC + KC, KC)], w_sem.at[2])
+    get_out = pltpu.make_async_copy(wo, wo_v, w_sem.at[3])
+    get_down = pltpu.make_async_copy(wd, wd_v, w_sem.at[4])
+    get_gate = pltpu.make_async_copy(wg, wg_v, w_sem.at[5])
+    get_up = pltpu.make_async_copy(wu, wu_v, w_sem.at[6])
+    get_small = [pltpu.make_async_copy(src, dst, in_sem.at[i]) for i, (src, dst) in enumerate(
+        ((tok, tok_v), (pos, pos_v), (freq, freq_v), (gain_a, ga_v), (gain_m, gm_v), (gh, gfull_o.at[x, c])))]
+    get_small[0].start()
+    fetch_emb(0).start()
+    fetch_emb(1).start()
+    for g in get_small[1:]:
+        g.start()
     greet(partner, cross)
 
-    ids = spread(tok[...].astype(F32))
+    get_small[0].wait()
+    ids = spread(tok_v[...].astype(F32))
     base = (tp * VLOC).astype(F32)
     lane = lax.broadcasted_iota(jnp.int32, (SEQ, 128), 1).astype(F32)
     for v in range(VLOC // 128):
@@ -178,19 +183,45 @@
 
     def lookup(j):
         fetch_emb(j).wait()
+
+        @pl.when(j + 2 < NC)
+        def _():
+            fetch_emb(j + 2).start()
+
+        @pl.when(j == 2)
+        def _():
+            for g in (get_q, get_k, get_v):
+                g.start()
         return nn(hot_v[...], emb_v[:, cols(j)])
 
     sum0.run(lookup, lambda j: cross_copy(0, s0, r0, j).start())
-    for f in fetches:
-        f.start()
-    gfull_o[x, c] = gh[...]
-    to_cross = remote(gh, gfull_o.at[x, c], hs.at[0], hr.at[0], cross)
-    to_partner = remote(gh, gfull_o.at[x, c], hs.at[1], hr.at[1], partner)
+    for g in (get_up, get_out, get_down, get_gate):
+        g.start()
+    for g in get_small[1:]:
+        g.wait()
+    mine = gfull_o.at[x, c]
+    to_cross = remote(mine, mine, hs.at[0], hr.at[0], cross)
+    to_partner = remote(mine, mine, hs.at[1], hr.at[1], partner)
     to_cross.start()
     to_partner.start()
-    angle = spread(pos[...].astype(F32)) * freq[...]
+    angle = spread(pos_v[...].astype(F32)) * freq_v[...]
     cs_o[0] = jnp.cos(angle)
     cs_o[1] = jnp.sin(angle)
+
+    for g in (get_q, get_k, get_v):
+        g.wait()
+
+    def turn_qkv(j, carry):
+        rj = pl.ds(pl.multiple_of(j * 256, 256), 256)
+        wqkvt_v[:, rj] = jnp.transpose(wqkv_v[rj, :])
+        return carry
+    lax.fori_loop(0, QKV // 256, turn_qkv, 0)
+    get_up.wait()
+
+    def turn_up(j, carry):
+        wut_v[:, cols(j)] = jnp.transpose(wu_v[cols(j), :])
+        return carry
+    lax.fori_loop(0, NC, turn_up, 0)
 
     for j in range(NC):
         cross_copy(0, s0, r0, j).wait_recv()
@@ -198,19 +229,17 @@
     def first(b, r):
         xv = s0[b, r].astype(F32) + r0[b, r].astype(F32)
         x0_o[b, r] = xv.astype(BF)
-        n1_o[b, c, r] = norm_rows(xv, gain_a[...])
+        n1_o[b, c, r] = norm_rows(xv, ga_v[...])
     rows16(first)
     share1 = remote(n1_o.at[:, c], n1_o.at[:, c], hs.at[2], hr.at[2], partner)
     share1.start()
-    for f in fetches[:3]:
-        f.wait()
     share1.wait_recv()
 
     n1 = n1_o[...].reshape(SEQ, DIM)
     cos_tab, sin_tab = cs_o[0], cs_o[1]
 
     for v in range(QKV // 256):
-        lin = nt(n1, wqkv_v[v * 256:(v + 1) * 256, :])
+        lin = nn(n1, wqkvt_v[:, v * 256:(v + 1) * 256])
         for h in range(2):
             lo = v * 256 + h * 128
             piece = lin[:, h * 128:(h + 1) * 128]
@@ -229,20 +258,23 @@
     to_cross.wait_recv()
     onward = remote(gfull_o.at[1 - x, c], gfull_o.at[1 - x, c], hs.at[3], hr.at[3], partner)
     onward.start()
-    fetches[3].wait()
+    get_out.wait()
 
     sum1 = PairSum(p1, g1, s1, (ps.at[1], pr.at[1]), c, partner)
     sum1.run(lambda j: nn(heads_o[...], wo_v[:, cols(j)]), lambda j: cross_copy(1, s1, r1, j).start())
 
     to_partner.wait_recv()
     onward.wait_recv()
-    fetches[4].wait()
+    get_down.wait()
+    get_gate.wait()
     gfull = gfull_o[...].reshape(SEQ, DIM)
+    wgt_v = emb_v
 
     def grad_act(j, carry):
-        gact_v[:, cols(j)] = nt(gfull, wd_v[pl.ds(pl.multiple_of(j * W, W), W), :]).astype(BF)
+        gact_v[:, cols(j)] = nt(gfull, wd_v[cols(j), :]).astype(BF)
+        wgt_v[:, cols(j)] = jnp.transpose(wg_v[cols(j), :])
         return carry
-    lax.fori_loop(0, FLOC // W, grad_act, 0)
+    lax.fori_loop(0, NC, grad_act, 0)
 
     for j in range(NC):
         cross_copy(1, s1, r1, j).wait_recv()
@@ -251,12 +283,10 @@
         total = s1[b, r].astype(F32) + r1[b, r].astype(F32)
         h1 = (x0_o[b, r].astype(F32) + total).astype(BF)
         h1_o[b, r] = h1
-        n2_o[b, c, r] = norm_rows(h1.astype(F32), gain_m[...])
+        n2_o[b, c, r] = norm_rows(h1.astype(F32), gm_v[...])
     rows16(second)
     share2 = remote(n2_o.at[:, c], n2_o.at[:, c], hs.at[4], hr.at[4], partner)
     share2.start()
-    fetches[5].wait()
-    fetches[6].wait()
     share2.wait_recv()
     n2 = n2_o[...].reshape(SEQ, DIM)
 
@@ -274,15 +304,9 @@
     lax.fori_loop(0, FLOC // 256, mlp, 0)
 
     sum2 = PairSum(p2, g2, gn2_o, (ps.at[2], pr.at[2]), c, partner)
-
-    def back_n2(j):
-        rj = pl.ds(pl.multiple_of(j * W, W), W)
-        return nt(ggate_o[...], wg_v[rj, :]) + nt(gup_o[...], wu_v[rj, :])
-    sum2.run(back_n2)
-    sum3 = PairSum(p3, g3, mlp_o, (ps.at[3], pr.at[3]), c, partner)
-    sum3.run(lambda j: nn(act_o[...], wd_v[:, cols(j)]))
-
-    for s in (sum0, sum1, sum2, sum3):
+    sum2.run(lambda j: nn(ggate_o[...], wgt_v[:, cols(j)]) + nn(gup_o[...], wut_v[:, cols(j)]))
+
+    for s in (sum0, sum1, sum2):
         s.drain()
     for j in range(NC):
         cross_copy(0, s0, r0, j).wait_send()
@@ -291,23 +315,11 @@
         copy.wait_send()
 
 
-def middle_kernel(gn2_own, gn2_got, mlp, h1, gfull, gain_m, qkv, cs, wq, wk, wv, wo,
-                  gh1_o, gqkv_o, gn1_o, hid_o, gain_o,
-                  wqkv_v, wo_v, gheads_v, mlp_got, p0, g0,
-                  w_sem, ps, pr, hs, hr):
+def middle_kernel(gn2_own, gn2_got, act, h1, gfull, gain_m, qkv, cs, wqkv, wo, wd,
+                  gh1_o, gqkv_o, give_o, keep_o, gain_o,
+                  gheads_v, p0, g0, s0, p1, g1, ps, pr, hs, hr):
     x, c, partner, cross = place()
-    fetches = (
-        pltpu.make_async_copy(wo, wo_v, w_sem.at[3]),
-        pltpu.make_async_copy(wq, wqkv_v.at[pl.ds(0, QC)], w_sem.at[0]),
-        pltpu.make_async_copy(wk, wqkv_v.at[pl.ds(QC, KC)], w_sem.at[1]),
-        pltpu.make_async_copy(wv, wqkv_v.at[pl.ds(QC + KC, KC)], w_sem.at[2]),
-    )
-    for f in fetches:
-        f.start()
-    greet(partner, cross)
-    out_send = remote(mlp.at[1 - x], mlp_got, hs.at[0], hr.at[0], cross)
-    out_send.start()
-
+    greet(partner)
     gains = []
 
     def first(b, r):
@@ -316,15 +328,18 @@
         gh1_o[b, c, r] = (gfull[b, c, r].astype(F32) + back).astype(BF)
         gains.append(part)
     rows16(first)
-    share = remote(gh1_o.at[:, c], gh1_o.at[:, c], hs.at[1], hr.at[1], partner)
+    share = remote(gh1_o.at[:, c], gh1_o.at[:, c], hs.at[0], hr.at[0], partner)
     share.start()
     gain_o[...] = gains[0] + gains[1] + gains[2] + gains[3]
-    fetches[0].wait()
+    sum0 = PairSum(p0, g0, s0, (ps.at[0], pr.at[0]), c, partner)
+    sum0.run(lambda j: nn(act[...], wd[:, cols(j)]))
+    give_o[2] = s0[1 - x]
+    keep_o[...] = s0[x]
     share.wait_recv()
 
     gh1 = gh1_o[...].reshape(SEQ, DIM)
     for v in range(QC // 256):
-        gheads_v[:, v * 256:(v + 1) * 256] = nt(gh1, wo_v[v * 256:(v + 1) * 256, :]).astype(BF)
+        gheads_v[:, v * 256:(v + 1) * 256] = nt(gh1, wo[v * 256:(v + 1) * 256, :]).astype(BF)
 
     cos_tab, sin_tab = cs[0], -cs[1]
     gks, gvs = [], []
@@ -352,34 +367,31 @@
     gqkv_o[:, QC:QC + KC] = rope_pair(jnp.concatenate(gks, axis=1), cos_tab, sin_tab).astype(BF)
     gqkv_o[:, QC + KC:] = jnp.concatenate(gvs, axis=1)
 
-    for f in fetches[1:]:
-        f.wait()
-    sum0 = PairSum(p0, g0, gn1_o, (ps, pr), c, partner)
-    sum0.run(lambda j: nn(gqkv_o[...], wqkv_v[:, cols(j)]))
-    out_send.wait_recv()
-    hid_o[...] = (h1[x].astype(F32) + (mlp[x].astype(F32) + mlp_got[...].astype(F32))).astype(BF)
+    sum1 = PairSum(p1, g1, give_o, (ps.at[1], pr.at[1]), c, partner)
+    sum1.run(lambda j: nn(gqkv_o[...], wqkv[:, cols(j)]))
     sum0.drain()
-    out_send.wait_send()
+    sum1.drain()
     share.wait_send()
 
 
-def back_kernel(gn1_own, gn1_got, x0, gh1, gain_a, gain_mp, gx_o, gain_o, gbuf, hs, hr):
+def back_kernel(give, got, keep, h1, x0, gh1, gain_a, gain_mp, gx_o, gain_o, hid_o, gbuf, hs, hr):
     x, c, partner, cross = place()
     greet(partner)
     gains = []
 
     def first(b, r):
-        grad = (gn1_own[b, r].astype(F32) + gn1_got[b, r].astype(F32)).astype(BF).astype(F32)
+        grad = (give[b, r].astype(F32) + got[b, r].astype(F32)).astype(BF).astype(F32)
         back, part = norm_back(grad, x0[b, r].astype(F32), gain_a[...])
         gx_o[b, c, r] = (gh1[b, c, r].astype(F32) + back).astype(BF)
         gains.append(part)
     rows16(first)
+    share = remote(gx_o.at[:, c], gx_o.at[:, c], hs.at[0], hr.at[0], partner)
+    share.start()
     gbuf[c, 0:1] = gains[0] + gains[1] + gains[2] + gains[3]
     gbuf[c, 1:2] = gain_mp[...]
-    share = remote(gx_o.at[:, c], gx_o.at[:, c], hs.at[0], hr.at[0], partner)
-    share.start()
     share_gain = remote(gbuf.at[c], gbuf.at[c], hs.at[1], hr.at[1], partner)
     share_gain.start()
+    hid_o[...] = (h1[x].astype(F32) + (keep[...].astype(F32) + got[2].astype(F32))).astype(BF)
     share_gain.wait_recv()
     gain_o[...] = gbuf[0, 0:2] + gbuf[1, 0:2]
     share.wait_recv()
@@ -449,7 +461,14 @@
     )(*ins)
 
 
-def emb_kernel(tok, gx, out, buf, sem):
+def emb_kernel(tok, gx, gains, hid, out, ga_o, gm_o, hid_o, buf, sem, out_sem):
+    extra = (
+        pltpu.make_async_copy(gains.at[pl.ds(0, 1)], ga_o, out_sem.at[0]),
+        pltpu.make_async_copy(gains.at[pl.ds(1, 1)], gm_o, out_sem.at[1]),
+        pltpu.make_async_copy(hid, hid_o, out_sem.at[2]),
+    )
+    for e in extra:
+        e.start()
     base = lax.axis_index("tp") * VLOC
     ids = jnp.broadcast_to(tok[...], (BM, SEQ)) - base
     row = lax.broadcasted_iota(jnp.int32, (BM, SEQ), 0)
@@ -471,6 +490,8 @@
     lax.fori_loop(0, steps, step, 0)
     for k in range(steps - NB, steps):
         copy(k).wait()
+    for e in extra:
+        e.wait()
 
 
 def vm(n):
@@ -483,6 +504,10 @@
 
 def sds(shape, dtype=BF):
     return jax.ShapeDtypeStruct(shape, dtype)
+
+
+def on(shape, dtype=BF):
+    return pltpu.VMEM(shape, dtype)
 
 
 FULL = (2, 2, 32, DIM)
@@ -502,21 +527,24 @@
     wo2 = wo.reshape(QC, DIM)
     gh2 = gh.reshape(32, DIM)
 
-    n1, x0, qkv, cs, heads, h1, n2, act, ggate, gup, gfull, gn2, mlp = pl.pallas_call(
+    n1, x0, qkv, cs, heads, h1, n2, act, ggate, gup, gfull, gn2, wqkv_v, wo_v, wd_v = pl.pallas_call(
         front_kernel,
-        out_shape=(sds(FULL), sds(MINE), sds((SEQ, QKV)), sds((2, SEQ, 128), F32), sds((SEQ, QC)), sds(MINE),
-                   sds(FULL), sds((SEQ, FLOC)), sds((SEQ, FLOC)), sds((SEQ, FLOC)), sds(FULL), sds(MINE), sds(MINE)),
-        in_specs=vm(6) + hb(8),
-        out_specs=tuple(vm(13)),
+        out_shape=(on(FULL), on(MINE), on((SEQ, QKV)), on((2, SEQ, 128), F32), on((SEQ, QC)), on(MINE),
+                   on(FULL), on((SEQ, FLOC)), on((SEQ, FLOC)), on((SEQ, FLOC)), on(FULL), on(MINE),
+                   on((QKV, DIM)), on((QC, DIM)), on((FLOC, DIM))),
+        in_specs=hb(14),
+        out_specs=tuple(vm(15)),
         scratch_shapes=[
-            pltpu.VMEM((VLOC, DIM), BF), pltpu.VMEM((QKV, DIM), BF), pltpu.VMEM((QC, DIM), BF),
-            pltpu.VMEM((FLOC, DIM), BF), pltpu.VMEM((DIM, FLOC), BF), pltpu.VMEM((DIM, FLOC), BF),
+            pltpu.VMEM((1, SEQ), jnp.int32), pltpu.VMEM((1, SEQ), jnp.int32), pltpu.VMEM((1, SEQ), F32),
+            pltpu.VMEM((1, DIM), F32), pltpu.VMEM((1, DIM), F32),
+            pltpu.VMEM((VLOC, DIM), BF), pltpu.VMEM((DIM, FLOC), BF), pltpu.VMEM((DIM, FLOC), BF),
+            pltpu.VMEM((FLOC, DIM), BF), pltpu.VMEM((DIM, QKV), BF),
             pltpu.VMEM((SEQ, VLOC), BF), pltpu.VMEM((SEQ, FLOC), BF),
             pltpu.VMEM(FULL, BF), pltpu.VMEM(MINE, BF), pltpu.VMEM(MINE, BF), pltpu.VMEM(MINE, BF),
             pltpu.VMEM(FULL, BF), pltpu.VMEM(MINE, BF), pltpu.VMEM(MINE, BF), pltpu.VMEM(MINE, BF),
-            pltpu.VMEM(FULL, BF), pltpu.VMEM(MINE, BF), pltpu.VMEM(FULL, BF), pltpu.VMEM(MINE, BF),
-            dma(NC), dma(7), dma(4, NC), dma(4, NC), dma(2, NC), dma(2, NC), dma(5), dma(5), dma(1), dma(1)],
-        compiler_params=pltpu.CompilerParams(collective_id=0, has_side_effects=True, vmem_limit_bytes=52 * 2 ** 20),
+            pltpu.VMEM(FULL, BF), pltpu.VMEM(MINE, BF),
+            dma(6), dma(NC), dma(7), dma(3, NC), dma(3, NC), dma(2, NC), dma(2, NC), dma(5), dma(5)],
+        compiler_params=pltpu.CompilerParams(collective_id=0, has_side_effects=True, vmem_limit_bytes=42 * 2 ** 20),
     )(tokens, positions, freq, ga, gm, gh2, emb, wqt, wkt, wvt, wo2, wd, wg, wu)
 
     swap = [(i, i ^ 2) for i in range(4)]
@@ -525,44 +553,45 @@
     n2f = n2.reshape(SEQ, DIM)
     g_gate, = outer((n2f, ggate), ((0, 1, 0),), (DIM,))
 
-    gh1, gqkv, gn1, hidden, gain_mp = pl.pallas_call(
+    gh1, gqkv, give, keep, gain_mp = pl.pallas_call(
         middle_kernel,
-        out_shape=(sds(FULL), sds((SEQ, QKV)), sds(MINE), sds((32, DIM)), sds((1, DIM), F32)),
-        in_specs=vm(8) + hb(4),
+        out_shape=(on(FULL), on((SEQ, QKV)), on((3, 32, DIM)), on((32, DIM)), on((1, DIM), F32)),
+        in_specs=vm(11),
         out_specs=tuple(vm(5)),
         scratch_shapes=[
-            pltpu.VMEM((QKV, DIM), BF), pltpu.VMEM((QC, DIM), BF), pltpu.VMEM((SEQ, QC), BF), pltpu.VMEM((32, DIM), BF),
-            pltpu.VMEM(FULL, BF), pltpu.VMEM(MINE, BF), dma(4), dma(NC), dma(NC), dma(2), dma(2)],
-        compiler_params=pltpu.CompilerParams(collective_id=1, has_side_effects=True, vmem_limit_bytes=24 * 2 ** 20),
-    )(gn2, gn2_got, mlp, h1, gfull, gm, qkv, cs, wqt, wkt, wvt, wo2)
-
-    gn1_got = lax.ppermute(gn1, 'tp', swap)
+            pltpu.VMEM((SEQ, QC), BF),
+            pltpu.VMEM(FULL, BF), pltpu.VMEM(MINE, BF), pltpu.VMEM(MINE, BF), pltpu.VMEM(FULL, BF), pltpu.VMEM(MINE, BF),
+            dma(2, NC), dma(2, NC), dma(1), dma(1)],
+        compiler_params=pltpu.CompilerParams(collective_id=1, has_side_effects=True, vmem_limit_bytes=8 * 2 ** 20),
+    )(gn2, gn2_got, act, h1, gfull, gm, qkv, cs, wqkv_v, wo_v, wd_v)
+
+    got = lax.ppermute(give, 'tp', swap)
     g_up, g_down, g_out, g_q, g_k, g_v = outer(
         (n2f, gup, act, gfull2, heads, gh1.reshape(SEQ, DIM), gqkv, n1.reshape(SEQ, DIM)),
         ((0, 1, 0), (2, 3, 0), (4, 5, 0), (6, 7, 0), (6, 7, QC), (6, 7, QC + KC)),
         (DIM, FLOC, QC, QC, KC, KC))
 
-    gx, gains = pl.pallas_call(
+    gx, gains, hid = pl.pallas_call(
         back_kernel,
-        out_shape=(sds(FULL), sds((2, DIM), F32)),
-        in_specs=vm(6),
-        out_specs=tuple(vm(2)),
+        out_shape=(on(FULL), on((2, DIM), F32), on((32, DIM))),
+        in_specs=vm(8),
+        out_specs=tuple(vm(3)),
         scratch_shapes=[pltpu.VMEM((2, 8, DIM), F32), dma(2), dma(2)],
-        compiler_params=pltpu.CompilerParams(collective_id=2, has_side_effects=True, vmem_limit_bytes=16 * 2 ** 20),
-    )(gn1, gn1_got, x0, gh1, ga, gain_mp)
-
-    g_emb = pl.pallas_call(
+        compiler_params=pltpu.CompilerParams(collective_id=2, has_side_effects=True, vmem_limit_bytes=8 * 2 ** 20),
+    )(give, got, keep, h1, x0, gh1, ga, gain_mp)
+
+    g_emb, gain_1, gain_2, hidden = pl.pallas_call(
         emb_kernel,
-        out_shape=sds((VLOC, DIM), F32),
-        in_specs=vm(2),
-        out_specs=hb(1)[0],
-        scratch_shapes=[pltpu.VMEM((NB, BM, DIM), F32), dma(NB)],
+        out_shape=(sds((VLOC, DIM), F32), sds((1, DIM), F32), sds((1, DIM), F32), sds((32, DIM))),
+        in_specs=vm(4),
+        out_specs=tuple(hb(4)),
+        scratch_shapes=[pltpu.VMEM((NB, BM, DIM), F32), dma(NB), dma(3)],
         compiler_params=pltpu.CompilerParams(vmem_limit_bytes=24 * 2 ** 20),
-    )(tokens, gx)
+    )(tokens, gx, gains, hid)
 
     back3 = lambda g: jnp.transpose(g.reshape(-1, HD, DIM), (2, 0, 1))
     return (hidden.reshape(1, 32, DIM), g_emb, back3(g_q), back3(g_k), back3(g_v), g_out.reshape(HLOC, HD, DIM),
-            g_gate, g_up, g_down, gains[0], gains[1])
+            g_gate, g_up, g_down, gain_1.reshape(DIM), gain_2.reshape(DIM))
 
 
 def solution(mesh):

time: 98.1 us -> 88.8 us (0.905)
  waiting for transfers between devices: 0.01 us -> 8.02 us
  Pallas kernels: 86.6 us -> 78.6 us
  local copies, waits for them, and re-layouts: 7.64 us -> 0.02 us
  starting transfers between devices: 2.72 us -> 1.24 us
    ppermute x1, waiting for transfers between devices: 0.01 us -> 8.01 us  [device_fn(): gn2_got = lax.ppermute(gn2, 'tp', swap)]
    unnamed x35 -> x6, local copies, waits for them, and re-layouts: 7.03 us -> 0.02 us
    pallas_call x4, Pallas kernels: 64.2 us -> 57.8 us  [the longest x1 37.9 us: device_fn(): pl.pallas_call(front_kernel, out_shape=(on(FULL), on(MINE), on((SEQ, QKV)...]
    pallas_call x2, Pallas kernels: 22.4 us -> 20.9 us  [outer(): pl.pallas_call(functools.partial(outer_kernel, spec), out_shape=tuple((ja...]
  transfers between devices with their start and end apart: 2 -> 2, of which waited for: 0 -> 1; matrix products, arithmetic and copies ran while one was open for 0% -> 0% of each run, Pallas kernels for 23% -> 24%
where the time goes in v2:
time: 88.8 us; the launch traced here: 88.6 us
  Pallas kernels  78.6 us (89%)
  waiting for transfers between devices  8.02 us (9%)
  starting transfers between devices  1.24 us (1%)
    pallas_call x1, Pallas kernels, device_fn(): pl.pallas_call(front_kernel, out_shape=(on(FULL), on(MINE), on((SEQ, QKV)...  37.9 us
    pallas_call x2, Pallas kernels, outer(): pl.pallas_call(functools.partial(outer_kernel, spec), out_shape=tuple((ja...  20.9 us
    pallas_call x1, Pallas kernels, device_fn(): pl.pallas_call(middle_kernel, out_shape=(on(FULL), on((SEQ, QKV)), on((3,...  11.3 us
    ppermute x1, waiting for transfers between devices, device_fn(): gn2_got = lax.ppermute(gn2, 'tp', swap)  8.01 us
    pallas_call x1, Pallas kernels, device_fn(): pl.pallas_call(emb_kernel, out_shape=(sds((VLOC, DIM), F32), sds((1, DIM)...  6.38 us
    pallas_call x1, Pallas kernels, device_fn(): pl.pallas_call(back_kernel, out_shape=(on(FULL), on((2, DIM), F32), on((3...  2.13 us
  transfers between devices with their start and end apart: 2, of which 1 were waited for; matrix products, arithmetic and copies ran while one was open for 0% of the time, Pallas kernels for 24%

profile of v2, /device:TPU:0, one launch (start us, length us, event | category | flops | bytes accessed | tf_op | source)
XLA Modules:
  0.0 88.6 jit_solution(1127772643974080853)
XLA Ops:
  0.6 0.0 copy-start
  0.7 37.9 %shard_map.221 = (bf16[2,2,32,2048]{3,2,1,0:T(8,128)(2,1)S(1)}, bf16[2,32,2048]{2,1,0:T(8,128)(2,1)S(1)}, bf16[128,768]{1,0:T(8,128)(2,1)S(1)}, f32[2,128,128]{2...) custom-call(s32[1,128]{1,0:T(1,128)} %tok.3, ...), custom_call_target="tpu_custom_call" | custom-call | tf_op jit(solution)/shard_map/pallas_call | solution.py:530
  38.6 0.6 collective-permute-start
  39.2 8.0 %collective-permute-done.gn2_got = bf16[2,32,2048]{2,1,0:T(8,128)(2,1)S(1)} collective-permute-done((bf16[2,32,2048]{2,1,0:T(8,128)(2,1)S(1)}, bf16[2,32,2048]{2,1,0:T(8,128)(2,1)S(1)}, u32[]{:S(2)}, u32[]{:S(2)}) %collective-permute-start) | collective-permute-done | bytes 262176 | tf_op jit(solution)/shard_map/ppermute | solution.py:551
  47.2 0.0 copy-done
  47.2 11.3 %shard_map.222 = (bf16[2,2,32,2048]{3,2,1,0:T(8,128)(2,1)S(1)}, bf16[128,768]{1,0:T(8,128)(2,1)S(1)}, bf16[3,32,2048]{2,1,0:T(8,128)(2,1)S(1)}, bf16[32,2048]{1,0:T(8,128)(2,1)S(1)}, f32[1,2048]{1,0:T(1,128)S(1)}) custom-call(bf16[2,32,2048]{2,1,0:T(8,128)(2,1)S(1)} %get-tuple-element.44.gn2_own, bf16[2,32,2048]{2,1,0:T(8,128)(2,1)S(1)} %collective-permute-done.gn2_got, ...), custom_call_target="tpu_custom_call" | custom-call | tf_op jit(solution)/shard_map/pallas_call | solution.py:556
  58.6 0.6 collective-permute-start.1
  59.2 6.3 %shard_map.226 = f32[2048,2048]{1,0:T(8,128)} custom-call(bf16[128,2048]{1,0:T(8,128)(2,1)S(1)} %bitcast.30, bf16[128,2048]{1,0:T(8,128)(2,1)S(1)} %get-tuple-element.72.refs_1_), custom_call_target="tpu_custom_call" | custom-call | flops 1073741824 | bytes 16777216 | tf_op jit(solution)/shard_map/pallas_call | solution.py:453
  65.5 0.0 copy-start.1
  65.6 0.0 copy-start.2
  65.6 14.5 %shard_map.225 = (f32[2048,2048]{1,0:T(8,128)}, f32[2048,2048]{1,0:T(8,128)}, f32[512,2048]{1,0:T(8,128)}, f32[512,2048]{1,0:T(8,128)}, f32[128,2048]{1,0:T(8,128)}, /*index=5*/f32[128,2048]{1,0:T(8,128)}) custom-call(bf16[128,2048]{1,0:T(8,128)(2,1)S(1)} %bitcast.31, bf16[128,2048]{1,0:T(8,128)(2,1)S(1)} %get-tuple-element.64.refs_1_, ...), custom_call_target="tpu_custom_call" | custom-call | flops 2818572288 | bytes 44040192 | tf_op jit(solution)/shard_map/pallas_call | solution.py:453
  80.1 0.0 collective-permute-done.1.got
  80.1 0.0 copy-done.1
  80.1 2.1 %shard_map.223 = (bf16[2,2,32,2048]{3,2,1,0:T(8,128)(2,1)S(1)}, f32[2,2048]{1,0:T(2,128)S(1)}, bf16[32,2048]{1,0:T(8,128)(2,1)S(1)}) custom-call(bf16[3,32,2048]{2,1,0:T(8,128)(2,1)S(1)} %get-tuple-element.53.give, bf16[3,32,2048]{2,1,0:T(8,128)(2,1)S(1)} %collective-permute-done.1.got, bf16[32,2048]{1,0:T(8,128)(2,1)S(1)} %get-tuple-element.54.keep, ...), custom_call_target="tpu_custom_call" | custom-call | tf_op jit(solution)/shard_map/pallas_call | solution.py:574
  82.2 0.0 copy-done.2
  82.3 6.4 %shard_map.224 = (f32[2048,2048]{1,0:T(8,128)}, f32[1,2048]{1,0:T(1,128)}, f32[1,2048]{1,0:T(1,128)}, bf16[32,2048]{1,0:T(8,128)(2,1)}) custom-call(s32[1,128]{1,0:T(1,128)S(1)} %copy-done.2, bf16[2,2,32,2048]{3,2,1,0:T(8,128)(2,1)S(1)} %get-tuple-element.58.gx, f32[2,2048]{1,0:T(2,128)S(1)} %get-tuple-element.59.gains, ...), custom_call_target="tpu_custom_call" | custom-call | tf_op jit(solution)/shard_map/pallas_call | solution.py:583
Async XLA Ops:
  0.6 46.6 %copy-start = (f32[2048]{0:T(1024)S(1)}, f32[2048]{0:T(1024)}, u32[]{:S(2)}) copy-start(f32[2048]{0:T(1024)} %param.18) | copy-start | bytes 24580
  38.6 8.6 %collective-permute-start = (bf16[2,32,2048]{2,1,0:T(8,128)(2,1)S(1)}, bf16[2,32,2048]{2,1,0:T(8,128)(2,1)S(1)}, u32[]{:S(2)}, u32[]{:S(2)}) collective-permute-start(bf16[2,32,2048]{2,1,0:T(8,128)(2,1)S(1)} %get-tuple-element.44.gn2_own), channel_id=1, source_target_pairs={{0,2},{1,3},{2,0},{3,1},{4,6},{5,7},{6,4},{7,5},{8,10},{9,11},{10,... | collective-permute-start | bytes 786440 | tf_op jit(solution)/shard_map/ppermute | solution.py:551
  58.6 21.5 %collective-permute-start.1 = (bf16[3,32,2048]{2,1,0:T(8,128)(2,1)S(1)}, bf16[3,32,2048]{2,1,0:T(8,128)(2,1)S(1)}, u32[]{:S(2)}, u32[]{:S(2)}) collective-permute-start(bf16[3,32,2048]{2,1,0:T(8,128)(2,1)S(1)} %get-tuple-element.53.give), channel_id=1, source_target_pairs={{0,2},{1,3},{2,0},{3,1},{4,6},{5,7},{6,4},{7,5},{8,10},{9,11},{10,... | collective-permute-start | bytes 1179656 | tf_op jit(solution)/shard_map/ppermute | solution.py:568
  65.5 14.6 %copy-start.1 = (f32[2048]{0:T(1024)S(1)}, f32[2048]{0:T(1024)}, u32[]{:S(2)}) copy-start(f32[2048]{0:T(1024)} %param.17) | copy-start | bytes 24580
  65.6 16.7 %copy-start.2 = (s32[1,128]{1,0:T(1,128)S(1)}, s32[1,128]{1,0:T(1,128)}, u32[]{:S(2)}) copy-start(s32[1,128]{1,0:T(1,128)} %tok.3) | copy-start | bytes 1540

commit v3 on v2

--- a/solution.py
+++ b/solution.py
@@ -85,18 +85,27 @@
         total = self.part[:, self.c, :, cols(j)].astype(F32) + self.got[:, :, cols(j)].astype(F32)
         self.own[0:2, :, cols(j)] = total.astype(BF)
 
-    def run(self, chunk, then=lambda j: None):
+    def send_all(self, chunk):
         def body(j, carry):
             self.put(j, chunk(j))
-
-            @pl.when(j > 0)
-            def _():
-                self.take(j - 1)
-                then(j - 1)
             return carry
         lax.fori_loop(0, NC, body, 0)
-        self.take(NC - 1)
-        then(NC - 1)
+
+    def run(self, chunk, then=lambda j: None, lag=NC):
+        def finish(j):
+            self.take(j)
+            then(j)
+
+        def body(j, carry):
+            self.put(j, chunk(j))
+            if lag < NC:
+                @pl.when(j >= lag)
+                def _():
+                    finish(j - lag)
+            return carry
+        lax.fori_loop(0, NC, body, 0)
+        for j in range(NC - lag, NC):
+            finish(j)
 
     def drain(self):
         for j in range(NC):
@@ -194,8 +203,8 @@
                 g.start()
         return nn(hot_v[...], emb_v[:, cols(j)])
 
-    sum0.run(lookup, lambda j: cross_copy(0, s0, r0, j).start())
-    for g in (get_up, get_out, get_down, get_gate):
+    sum0.run(lookup, lambda j: cross_copy(0, s0, r0, j).start(), 1)
+    for g in (get_out, get_down, get_gate, get_up):
         g.start()
     for g in get_small[1:]:
         g.wait()
@@ -216,12 +225,6 @@
         wqkvt_v[:, rj] = jnp.transpose(wqkv_v[rj, :])
         return carry
     lax.fori_loop(0, QKV // 256, turn_qkv, 0)
-    get_up.wait()
-
-    def turn_up(j, carry):
-        wut_v[:, cols(j)] = jnp.transpose(wu_v[cols(j), :])
-        return carry
-    lax.fori_loop(0, NC, turn_up, 0)
 
     for j in range(NC):
         cross_copy(0, s0, r0, j).wait_recv()
@@ -275,6 +278,12 @@
         wgt_v[:, cols(j)] = jnp.transpose(wg_v[cols(j), :])
         return carry
     lax.fori_loop(0, NC, grad_act, 0)
+    get_up.wait()
+
+    def turn_up(j, carry):
+        wut_v[:, cols(j)] = jnp.transpose(wu_v[cols(j), :])
+        return carry
+    lax.fori_loop(0, NC, turn_up, 0)
 
     for j in range(NC):
         cross_copy(1, s1, r1, j).wait_recv()
@@ -315,7 +324,7 @@
         copy.wait_send()
 
 
-def middle_kernel(gn2_own, gn2_got, act, h1, gfull, gain_m, qkv, cs, wqkv, wo, wd,
+def middle_kernel(gn2_own, gn2_got, act, h1, gfull, gain_m, qkv, cs, wqkv, wo, wd, token,
                   gh1_o, gqkv_o, give_o, keep_o, gain_o,
                   gheads_v, p0, g0, s0, p1, g1, ps, pr, hs, hr):
     x, c, partner, cross = place()
@@ -332,9 +341,7 @@
     share.start()
     gain_o[...] = gains[0] + gains[1] + gains[2] + gains[3]
     sum0 = PairSum(p0, g0, s0, (ps.at[0], pr.at[0]), c, partner)
-    sum0.run(lambda j: nn(act[...], wd[:, cols(j)]))
-    give_o[2] = s0[1 - x]
-    keep_o[...] = s0[x]
+    sum0.send_all(lambda j: nn(act[...], wd[:, cols(j)]))
     share.wait_recv()
 
     gh1 = gh1_o[...].reshape(SEQ, DIM)
@@ -368,13 +375,19 @@
     gqkv_o[:, QC + KC:] = jnp.concatenate(gvs, axis=1)
 
     sum1 = PairSum(p1, g1, give_o, (ps.at[1], pr.at[1]), c, partner)
-    sum1.run(lambda j: nn(gqkv_o[...], wqkv[:, cols(j)]))
+    sum1.send_all(lambda j: nn(gqkv_o[...], wqkv[:, cols(j)]))
+    for j in range(NC):
+        sum0.take(j)
+    give_o[2] = s0[1 - x]
+    keep_o[...] = s0[x]
+    for j in range(NC):
+        sum1.take(j)
     sum0.drain()
     sum1.drain()
     share.wait_send()
 
 
-def back_kernel(give, got, keep, h1, x0, gh1, gain_a, gain_mp, gx_o, gain_o, hid_o, gbuf, hs, hr):
+def back_kernel(give, got, keep, h1, x0, gh1, gain_a, gain_mp, token, gx_o, gain_o, hid_o, gbuf, hs, hr):
     x, c, partner, cross = place()
     greet(partner)
     gains = []
@@ -399,66 +412,86 @@
     share_gain.wait_send()
 
 
+def vm(n):
+    return [pl.BlockSpec(memory_space=VMEM)] * n
+
+
+def hb(n):
+    return [pl.BlockSpec(memory_space=HBM)] * n
+
+
+def on(shape, dtype=BF):
+    return pltpu.VMEM(shape, dtype)
+
+
 NB = 4
+UP_FIRST = 768
 BM = 256
 
 
-def outer_kernel(spec, *refs):
-    n_in = 1 + max(max(l, r) for l, r, _ in spec)
-    ins, outs = refs[:n_in], refs[n_in:n_in + len(spec)]
-    buf, sem = refs[n_in + len(spec):]
-
+def outer_kernel(spec, n_in, n_held, *refs):
+    n_out = 1 + max(o for _, _, _, o, _, _ in spec)
+    ins, outs = refs[:n_in], refs[n_in + n_held:n_in + n_held + n_out]
+    token, buf, sem = refs[n_in + n_held + n_out:]
+    token[...] = jnp.zeros_like(token)
     done = 0
-    copies = []
-    for (l, r, off), out in zip(spec, outs):
-        lhs, rhs = ins[l], ins[r]
-        steps = out.shape[0] // BM if lhs is not None else 0
-        bm = min(BM, out.shape[0])
-        steps = out.shape[0] // bm
-        if bm == BM:
-            def copy(i, out=out, done=done):
-                slot = lax.rem(i + done, NB)
-                return pltpu.make_async_copy(buf.at[slot], out.at[pl.ds(pl.multiple_of(i * BM, BM), BM)], sem.at[slot])
-
-            def step(i, carry, copy=copy, lhs=lhs, rhs=rhs, off=off, done=done):
-                slot = lax.rem(i + done, NB)
-
-                @pl.when(i + done >= NB)
-                def _():
+    flying = {}
+    for l, r, off, o, row, rows in spec:
+        lhs, rhs, out = ins[l], ins[r], outs[o]
+        bm = min(BM, rows)
+        steps = rows // bm
+
+        def copy(i, out=out, done=done, bm=bm, row=row):
+            slot = lax.rem(i + done, NB)
+            where = pl.ds(pl.multiple_of(row + i * bm, bm), bm)
+            return pltpu.make_async_copy(buf.at[slot, pl.ds(0, bm)], out.at[where], sem.at[slot])
+
+        def compute(i, lhs=lhs, rhs=rhs, off=off, done=done, bm=bm):
+            a = lhs[:, pl.ds(pl.multiple_of(off + i * bm, 128), bm)]
+            buf[lax.rem(i + done, NB), 0:bm] = tn(a, rhs[...])
+
+        free = [(done + i) % NB for i in range(min(NB, steps))]
+        uniform = steps >= NB and all(flying.get(k, bm) == bm for k in range(NB)) and (not flying or len(flying) == NB)
+        if uniform:
+            def step(i, carry, copy=copy, compute=compute, waiting=bool(flying)):
+                if waiting:
                     copy(i).wait()
-                a = lhs[:, pl.ds(pl.multiple_of(off + i * BM, 128), BM)]
-                buf[slot] = tn(a, rhs[...])
+                else:
+                    @pl.when(i >= NB)
+                    def _():
+                        copy(i).wait()
+                compute(i)
                 copy(i).start()
                 return carry
             lax.fori_loop(0, steps, step, 0)
-            done += steps
+            flying = {k: bm for k in range(NB)}
         else:
-            slot = done % NB
-            if done >= NB:
-                pltpu.make_async_copy(buf.at[slot], outs[0].at[pl.ds(0, BM)], sem.at[slot]).wait()
-            buf[slot, 0:bm] = tn(lhs[:, off:off + bm], rhs[...])
-            copies.append(pltpu.make_async_copy(buf.at[slot, pl.ds(0, bm)], out, sem.at[slot]))
-            copies[-1].start()
-            done += 1
-    small = len(copies)
-    for k in range(max(0, done - NB), done - small):
-        slot = k % NB
-        pltpu.make_async_copy(buf.at[slot], outs[0].at[pl.ds(0, BM)], sem.at[slot]).wait()
-    for copy in copies:
-        copy.wait()
-
-
-def outer(ins, spec, rows):
-    total = sum(rows)
-    return pl.pallas_call(
-        functools.partial(outer_kernel, spec),
-        out_shape=tuple(jax.ShapeDtypeStruct((m, DIM), F32) for m in rows),
-        in_specs=[pl.BlockSpec(memory_space=VMEM)] * len(ins),
-        out_specs=tuple(pl.BlockSpec(memory_space=HBM) for _ in rows),
+            for i in range(steps):
+                slot = (done + i) % NB
+                if slot in flying:
+                    size = flying[slot]
+                    pltpu.make_async_copy(buf.at[slot, pl.ds(0, size)], outs[0].at[pl.ds(0, size)], sem.at[slot]).wait()
+                compute(i)
+                copy(i).start()
+                flying[slot] = bm
+        done += steps
+    for slot, size in flying.items():
+        pltpu.make_async_copy(buf.at[slot, pl.ds(0, size)], outs[0].at[pl.ds(0, size)], sem.at[slot]).wait()
+
+
+def outer(ins, spec, rows, held=()):
+    total = sum(n for *_, n in spec)
+    *outs, token = pl.pallas_call(
+        functools.partial(outer_kernel, spec, len(ins), len(held)),
+        out_shape=tuple(jax.ShapeDtypeStruct((m, DIM), F32) for m in rows) + (on((8, 128), F32),),
+        in_specs=vm(len(ins)) + hb(len(held)),
+        out_specs=tuple(hb(len(rows)) + vm(1)),
         scratch_shapes=[pltpu.VMEM((NB, BM, DIM), F32), pltpu.SemaphoreType.DMA((NB,))],
+        input_output_aliases={len(ins) + i: o for i, (_, o) in enumerate(held)},
         cost_estimate=pl.CostEstimate(flops=2 * total * DIM * SEQ, bytes_accessed=4 * total * DIM, transcendentals=0),
-        compiler_params=pltpu.CompilerParams(vmem_limit_bytes=24 * 2 ** 20),
-    )(*ins)
+        compiler_params=pltpu.CompilerParams(vmem_limit_bytes=16 * 2 ** 20),
+    )(*ins, *[h for h, _ in held])
+    return outs, token
 
 
 def emb_kernel(tok, gx, gains, hid, out, ga_o, gm_o, hid_o, buf, sem, out_sem):
@@ -494,20 +527,8 @@
         e.wait()
 
 
-def vm(n):
-    return [pl.BlockSpec(memory_space=VMEM)] * n
-
-
-def hb(n):
-    return [pl.BlockSpec(memory_space=HBM)] * n
-
-
 def sds(shape, dtype=BF):
     return jax.ShapeDtypeStruct(shape, dtype)
-
-
-def on(shape, dtype=BF):
-    return pltpu.VMEM(shape, dtype)
 
 
 FULL = (2, 2, 32, DIM)
@@ -551,34 +572,35 @@
     gn2_got = lax.ppermute(gn2, 'tp', swap)
     gfull2 = gfull.reshape(SEQ, DIM)
     n2f = n2.reshape(SEQ, DIM)
-    g_gate, = outer((n2f, ggate), ((0, 1, 0),), (DIM,))
+    (g_gate, g_up), token = outer((n2f, ggate, gup), ((0, 1, 0, 0, 0, DIM), (0, 2, 0, 1, 0, UP_FIRST)), (DIM, DIM))
 
     gh1, gqkv, give, keep, gain_mp = pl.pallas_call(
         middle_kernel,
         out_shape=(on(FULL), on((SEQ, QKV)), on((3, 32, DIM)), on((32, DIM)), on((1, DIM), F32)),
-        in_specs=vm(11),
+        in_specs=vm(12),
         out_specs=tuple(vm(5)),
         scratch_shapes=[
             pltpu.VMEM((SEQ, QC), BF),
             pltpu.VMEM(FULL, BF), pltpu.VMEM(MINE, BF), pltpu.VMEM(MINE, BF), pltpu.VMEM(FULL, BF), pltpu.VMEM(MINE, BF),
             dma(2, NC), dma(2, NC), dma(1), dma(1)],
         compiler_params=pltpu.CompilerParams(collective_id=1, has_side_effects=True, vmem_limit_bytes=8 * 2 ** 20),
-    )(gn2, gn2_got, act, h1, gfull, gm, qkv, cs, wqkv_v, wo_v, wd_v)
+    )(gn2, gn2_got, act, h1, gfull, gm, qkv, cs, wqkv_v, wo_v, wd_v, token)
 
     got = lax.ppermute(give, 'tp', swap)
-    g_up, g_down, g_out, g_q, g_k, g_v = outer(
+    (g_up, g_down, g_out, g_q, g_k, g_v), token2 = outer(
         (n2f, gup, act, gfull2, heads, gh1.reshape(SEQ, DIM), gqkv, n1.reshape(SEQ, DIM)),
-        ((0, 1, 0), (2, 3, 0), (4, 5, 0), (6, 7, 0), (6, 7, QC), (6, 7, QC + KC)),
-        (DIM, FLOC, QC, QC, KC, KC))
+        ((0, 1, UP_FIRST, 0, UP_FIRST, DIM - UP_FIRST), (2, 3, 0, 1, 0, FLOC), (4, 5, 0, 2, 0, QC),
+         (6, 7, 0, 3, 0, QC), (6, 7, QC, 4, 0, KC), (6, 7, QC + KC, 5, 0, KC)),
+        (DIM, FLOC, QC, QC, KC, KC), ((g_up, 0),))
 
     gx, gains, hid = pl.pallas_call(
         back_kernel,
         out_shape=(on(FULL), on((2, DIM), F32), on((32, DIM))),
-        in_specs=vm(8),
+        in_specs=vm(9),
         out_specs=tuple(vm(3)),
         scratch_shapes=[pltpu.VMEM((2, 8, DIM), F32), dma(2), dma(2)],
         compiler_params=pltpu.CompilerParams(collective_id=2, has_side_effects=True, vmem_limit_bytes=8 * 2 ** 20),
-    )(give, got, keep, h1, x0, gh1, ga, gain_mp)
+    )(give, got, keep, h1, x0, gh1, ga, gain_mp, token2)
 
     g_emb, gain_1, gain_2, hidden = pl.pallas_call(
         emb_kernel,

time: 88.8 us -> 78.2 us (0.88)
  waiting for transfers between devices: 8.02 us -> 0.01 us
  Pallas kernels: 78.6 us -> 75.1 us
    ppermute x1, waiting for transfers between devices: 8.01 us -> 0.01 us  [device_fn(): gn2_got = lax.ppermute(gn2, 'tp', swap)]
    pallas_call x1, Pallas kernels: 11.3 us -> 9.12 us  [device_fn(): pl.pallas_call(middle_kernel, out_shape=(on(FULL), on((SEQ, QKV)), on((3,...]
    pallas_call x1, Pallas kernels: 37.9 us -> 36.6 us  [device_fn(): pl.pallas_call(front_kernel, out_shape=(on(FULL), on(MINE), on((SEQ, QKV)...]
  transfers between devices with their start and end apart: 2 -> 2, of which waited for: 1 -> 0; matrix products, arithmetic and copies ran while one was open for 0% -> 0% of each run, Pallas kernels for 24% -> 27%
where the time goes in v3:
time: 78.2 us; the launch traced here: 78.1 us
  Pallas kernels  75.1 us (96%)
  starting transfers between devices  2.09 us (3%)
  between operations  0.9 us (1%)
    pallas_call x1, Pallas kernels, device_fn(): pl.pallas_call(front_kernel, out_shape=(on(FULL), on(MINE), on((SEQ, QKV)...  36.6 us
    pallas_call x2, Pallas kernels, outer(): pl.pallas_call(functools.partial(outer_kernel, spec, len(ins), len(held))...  20.9 us
    pallas_call x1, Pallas kernels, device_fn(): pl.pallas_call(middle_kernel, out_shape=(on(FULL), on((SEQ, QKV)), on((3,...  9.12 us
    pallas_call x1, Pallas kernels, device_fn(): pl.pallas_call(emb_kernel, out_shape=(sds((VLOC, DIM), F32), sds((1, DIM)...  6.38 us
    pallas_call x1, Pallas kernels, device_fn(): pl.pallas_call(back_kernel, out_shape=(on(FULL), on((2, DIM), F32), on((3...  2.13 us
  transfers between devices with their start and end apart: 2, of which 0 were waited for; matrix products, arithmetic and copies ran while one was open for 0% of the time, Pallas kernels for 27%

profile of v3, /device:TPU:0, one launch (start us, length us, event | category | flops | bytes accessed | tf_op | source)
XLA Modules:
  0.0 78.1 jit_solution(9257087911700050106)
XLA Ops:
  0.6 0.0 copy-start
  0.7 36.6 %shard_map.221 = (bf16[2,2,32,2048]{3,2,1,0:T(8,128)(2,1)S(1)}, bf16[2,32,2048]{2,1,0:T(8,128)(2,1)S(1)}, bf16[128,768]{1,0:T(8,128)(2,1)S(1)}, f32[2,128,128]{2...) custom-call(s32[1,128]{1,0:T(1,128)} %tok.3, ...), custom_call_target="tpu_custom_call" | custom-call | tf_op jit(solution)/shard_map/pallas_call | solution.py:551
  37.3 1.4 %collective-permute-start = (bf16[2,32,2048]{2,1,0:T(8,128)(2,1)S(1)}, bf16[2,32,2048]{2,1,0:T(8,128)(2,1)S(1)}, u32[]{:S(2)}, u32[]{:S(2)}) collective-permute-start(bf16[2,32,2048]{2,1,0:T(8,128)(2,1)S(1)} %get-tuple-element.48.gn2_own), channel_id=1, source_target_pairs={{0,2},{1,3},{2,0},{3,1},{4,6},{5,7},{6,4},{7,5},{8,10},{9,11},{10,... | collective-permute-start | bytes 786440 | tf_op jit(solution)/shard_map/ppermute | solution.py:572
  38.7 8.2 %shard_map.222 = (f32[2048,2048]{1,0:T(8,128)}, f32[2048,2048]{1,0:T(8,128)}, f32[8,128]{1,0:T(8,128)S(1)}) custom-call(bf16[128,2048]{1,0:T(8,128)(2,1)S(1)} %bitcast.33, bf16[128,2048]{1,0:T(8,128)(2,1)S(1)} %get-tuple-element.58.refs_1_, bf16[128,2048]{1,0:T(8,128)(2,1)S(1)} %get-tuple-element.59.refs_2_.refs_1_), custom_call_target="tpu_custom_call" | custom-call | flops 1476395008 | bytes 23068672 | tf_op jit(solution)/shard_map/pallas_call | solution.py:484
  46.9 0.0 collective-permute-done.gn2_got
  47.0 0.0 copy-done
  47.0 9.1 %shard_map.223 = (bf16[2,2,32,2048]{3,2,1,0:T(8,128)(2,1)S(1)}, bf16[128,768]{1,0:T(8,128)(2,1)S(1)}, bf16[3,32,2048]{2,1,0:T(8,128)(2,1)S(1)}, bf16[32,2048]{1,0:T(8,128)(2,1)S(1)}, f32[1,2048]{1,0:T(1,128)S(1)}) custom-call(bf16[2,32,2048]{2,1,0:T(8,128)(2,1)S(1)} %get-tuple-element.48.gn2_own, bf16[2,32,2048]{2,1,0:T(8,128)(2,1)S(1)} %collective-permute-done.gn2_got, ...), custom_call_target="tpu_custom_call" | custom-call | tf_op jit(solution)/shard_map/pallas_call | solution.py:577
  56.1 0.7 collective-permute-start.1
  56.8 0.0 copy-start.1
  56.8 0.0 copy-start.2
  56.8 12.6 %shard_map.224 = (f32[2048,2048]{1,0:T(8,128)}, f32[2048,2048]{1,0:T(8,128)}, f32[512,2048]{1,0:T(8,128)}, f32[512,2048]{1,0:T(8,128)}, f32[128,2048]{1,0:T(8,12...) custom-call(bf16[128,2048]{1,0:T(8,128)(2,1)S(1)} %bitcast.34, ...), custom_call_target="tpu_custom_call", output_to_operand_aliasing={{0}: (8, {})} | custom-call | flops 2415919104 | bytes 37748736 | tf_op jit(solution)/shard_map/pallas_call | solution.py:484
  69.4 0.0 collective-permute-done.1.got
  69.4 0.0 copy-done.1
  69.4 2.1 %shard_map.225 = (bf16[2,2,32,2048]{3,2,1,0:T(8,128)(2,1)S(1)}, f32[2,2048]{1,0:T(2,128)S(1)}, bf16[32,2048]{1,0:T(8,128)(2,1)S(1)}) custom-call(bf16[3,32,2048]{2,1,0:T(8,128)(2,1)S(1)} %get-tuple-element.61.give, bf16[3,32,2048]{2,1,0:T(8,128)(2,1)S(1)} %collective-permute-done.1.got, bf16[32,2048]{1,0:T(8,128)(2,1)S(1)} %get-tuple-element.62.keep, ...), custom_call_target="tpu_custom_call" | custom-call | tf_op jit(solution)/shard_map/pallas_call | solution.py:596
  71.5 0.0 copy-done.2
  71.5 6.4 %shard_map.226 = (f32[2048,2048]{1,0:T(8,128)}, f32[1,2048]{1,0:T(1,128)}, f32[1,2048]{1,0:T(1,128)}, bf16[32,2048]{1,0:T(8,128)(2,1)}) custom-call(s32[1,128]{1,0:T(1,128)S(1)} %copy-done.2, bf16[2,2,32,2048]{3,2,1,0:T(8,128)(2,1)S(1)} %get-tuple-element.71.gx, f32[2,2048]{1,0:T(2,128)S(1)} %get-tuple-element.72.gains, ...), custom_call_target="tpu_custom_call" | custom-call | tf_op jit(solution)/shard_map/pallas_call | solution.py:605
Async XLA Ops:
  0.6 46.3 %copy-start = (f32[2048]{0:T(1024)S(1)}, f32[2048]{0:T(1024)}, u32[]{:S(2)}) copy-start(f32[2048]{0:T(1024)} %param.18) | copy-start | bytes 24580
  37.3 9.7 %collective-permute-start = (bf16[2,32,2048]{2,1,0:T(8,128)(2,1)S(1)}, bf16[2,32,2048]{2,1,0:T(8,128)(2,1)S(1)}, u32[]{:S(2)}, u32[]{:S(2)}) collective-permute-start(bf16[2,32,2048]{2,1,0:T(8,128)(2,1)S(1)} %get-tuple-element.48.gn2_own), channel_id=1, source_target_pairs={{0,2},{1,3},{2,0},{3,1},{4,6},{5,7},{6,4},{7,5},{8,10},{9,11},{10,... | collective-permute-start | bytes 786440 | tf_op jit(solution)/shard_map/ppermute | solution.py:572
  56.1 13.3 %collective-permute-start.1 = (bf16[3,32,2048]{2,1,0:T(8,128)(2,1)S(1)}, bf16[3,32,2048]{2,1,0:T(8,128)(2,1)S(1)}, u32[]{:S(2)}, u32[]{:S(2)}) collective-permute-start(bf16[3,32,2048]{2,1,0:T(8,128)(2,1)S(1)} %get-tuple-element.61.give), channel_id=1, source_target_pairs={{0,2},{1,3},{2,0},{3,1},{4,6},{5,7},{6,4},{7,5},{8,10},{9,11},{10,... | collective-permute-start | bytes 1179656 | tf_op jit(solution)/shard_map/ppermute | solution.py:589
  56.8 12.6 %copy-start.1 = (f32[2048]{0:T(1024)S(1)}, f32[2048]{0:T(1024)}, u32[]{:S(2)}) copy-start(f32[2048]{0:T(1024)} %param.17) | copy-start | bytes 24580
  56.8 14.8 %copy-start.2 = (s32[1,128]{1,0:T(1,128)S(1)}, s32[1,128]{1,0:T(1,128)}, u32[]{:S(2)}) copy-start(s32[1,128]{1,0:T(1,128)} %tok.3) | copy-start | bytes 1540

commit v4 on v3

--- a/solution.py
+++ b/solution.py
@@ -28,6 +28,9 @@
 SCALE = HD ** -0.5
 NC = 4
 W = DIM // NC
+NE = 8
+WE = DIM // NE
+AHEAD = 3
 VMEM = pltpu.VMEM
 HBM = pltpu.HBM
 
@@ -63,52 +66,55 @@
         src_ref=src, dst_ref=dst, send_sem=send, recv_sem=recv, device_id={"tp": peer}, device_id_type=MESH)
 
 
-def cols(j):
-    return pl.ds(pl.multiple_of(j * W, W), W)
+def cols(j, width=W):
+    return pl.ds(pl.multiple_of(j * width, width), width)
 
 
 class PairSum:
-    def __init__(self, part, got, own, sems, c, partner):
+    def __init__(self, part, got, own, sems, c, partner, n=NC):
         self.part, self.got, self.own, self.c, self.partner = part, got, own, c, partner
         self.send, self.recv = sems
+        self.n, self.width = n, DIM // n
 
     def copy(self, j):
-        return remote(self.part.at[:, 1 - self.c, :, cols(j)], self.got.at[:, :, cols(j)],
+        return remote(self.part.at[:, 1 - self.c, :, cols(j, self.width)], self.got.at[:, :, cols(j, self.width)],
                       self.send.at[j], self.recv.at[j], self.partner)
 
     def put(self, j, value):
-        self.part[:, :, :, cols(j)] = value.astype(BF).reshape(2, 2, 32, W)
+        self.part[:, :, :, cols(j, self.width)] = value.astype(BF).reshape(2, 2, 32, self.width)
         self.copy(j).start()
 
     def take(self, j):
         self.copy(j).wait_recv()
-        total = self.part[:, self.c, :, cols(j)].astype(F32) + self.got[:, :, cols(j)].astype(F32)
-        self.own[0:2, :, cols(j)] = total.astype(BF)
+        total = self.part[:, self.c, :, cols(j, self.width)].astype(F32) + self.got[:, :, cols(j, self.width)].astype(F32)
+        self.own[0:2, :, cols(j, self.width)] = total.astype(BF)
 
     def send_all(self, chunk):
         def body(j, carry):
             self.put(j, chunk(j))
             return carry
-        lax.fori_loop(0, NC, body, 0)
-
-    def run(self, chunk, then=lambda j: None, lag=NC):
+        lax.fori_loop(0, self.n, body, 0)
+
+    def run(self, chunk, then=lambda j: None, lag=None):
+        lag = lag or self.n
+
         def finish(j):
             self.take(j)
             then(j)
 
         def body(j, carry):
             self.put(j, chunk(j))
-            if lag < NC:
+            if lag < self.n:
                 @pl.when(j >= lag)
                 def _():
                     finish(j - lag)
             return carry
-        lax.fori_loop(0, NC, body, 0)
-        for j in range(NC - lag, NC):
+        lax.fori_loop(0, self.n, body, 0)
+        for j in range(self.n - lag, self.n):
             finish(j)
 
     def drain(self):
-        for j in range(NC):
+        for j in range(self.n):
             self.copy(j).wait_send()
 
 
@@ -142,10 +148,22 @@
     return values * cos_tab + other * jnp.where(low, -sin_tab, sin_tab)
 
 
+def stack(ref, g):
+    return jnp.concatenate([ref[:, h * HD:(h + 1) * HD] for h in range(g * GROUP, (g + 1) * GROUP)], axis=0)
+
+
+def unstack(ref, g, value, fix=lambda pair: pair):
+    for i in range(0, GROUP, 2):
+        lo = (g * GROUP + i) * HD
+        pair = jnp.concatenate([value[i * SEQ:(i + 1) * SEQ], value[(i + 1) * SEQ:(i + 2) * SEQ]], axis=1)
+        ref[:, lo:lo + 128] = fix(pair).astype(BF)
+
+
 def probs_of(q, k):
     scores = nt(q, k) * SCALE
-    causal = (lax.broadcasted_iota(jnp.int32, (SEQ, SEQ), 0) >= lax.broadcasted_iota(jnp.int32, (SEQ, SEQ), 1))
-    scores = jnp.where(causal, scores, -1e30)
+    shape = (GROUP * SEQ, SEQ)
+    row = lax.broadcasted_iota(jnp.int32, shape, 0) % SEQ
+    scores = jnp.where(row >= lax.broadcasted_iota(jnp.int32, shape, 1), scores, -1e30)
     e = jnp.exp(scores - jnp.max(scores, axis=-1, keepdims=True))
     return e / jnp.sum(e, axis=-1, keepdims=True)
 
@@ -160,7 +178,7 @@
     tp = 2 * x + c
 
     def fetch_emb(j):
-        return pltpu.make_async_copy(emb.at[:, cols(j)], emb_v.at[:, cols(j)], emb_sem.at[j])
+        return pltpu.make_async_copy(emb.at[:, cols(j, WE)], emb_v.at[:, cols(j, WE)], emb_sem.at[j])
 
     get_q = pltpu.make_async_copy(wq, wqkv_v.at[pl.ds(0, QC)], w_sem.at[0])
     get_k = pltpu.make_async_copy(wk, wqkv_v.at[pl.ds(QC, KC)], w_sem.at[1])
@@ -172,12 +190,10 @@
     get_small = [pltpu.make_async_copy(src, dst, in_sem.at[i]) for i, (src, dst) in enumerate(
         ((tok, tok_v), (pos, pos_v), (freq, freq_v), (gain_a, ga_v), (gain_m, gm_v), (gh, gfull_o.at[x, c])))]
     get_small[0].start()
-    fetch_emb(0).start()
-    fetch_emb(1).start()
+    for j in range(AHEAD):
+        fetch_emb(j).start()
     for g in get_small[1:]:
         g.start()
-    greet(partner, cross)
-
     get_small[0].wait()
     ids = spread(tok_v[...].astype(F32))
     base = (tp * VLOC).astype(F32)
@@ -185,23 +201,26 @@
     for v in range(VLOC // 128):
         hot_v[:, v * 128:(v + 1) * 128] = jnp.where(ids == lane + (base + float(v * 128)), 1.0, 0.0).astype(BF)
 
+    greet(partner, cross)
+
     def cross_copy(k, src, dst, j):
-        return remote(src.at[:, :, cols(j)], dst.at[:, :, cols(j)], xs.at[k, j], xr.at[k, j], cross)
-
-    sum0 = PairSum(p0, g0, s0, (ps.at[0], pr.at[0]), c, partner)
+        cj = cols(j, WE if k == 0 else W)
+        return remote(src.at[:, :, cj], dst.at[:, :, cj], xs.at[k, j], xr.at[k, j], cross)
+
+    sum0 = PairSum(p0, g0, s0, (ps.at[0], pr.at[0]), c, partner, NE)
 
     def lookup(j):
         fetch_emb(j).wait()
 
-        @pl.when(j + 2 < NC)
+        @pl.when(j + AHEAD < NE)
         def _():
-            fetch_emb(j + 2).start()
-
-        @pl.when(j == 2)
+            fetch_emb(j + AHEAD).start()
+
+        @pl.when(j == NE - AHEAD)
         def _():
             for g in (get_q, get_k, get_v):
                 g.start()
-        return nn(hot_v[...], emb_v[:, cols(j)])
+        return nn(hot_v[...], emb_v[:, cols(j, WE)])
 
     sum0.run(lookup, lambda j: cross_copy(0, s0, r0, j).start(), 1)
     for g in (get_out, get_down, get_gate, get_up):
@@ -226,7 +245,7 @@
         return carry
     lax.fori_loop(0, QKV // 256, turn_qkv, 0)
 
-    for j in range(NC):
+    for j in range(NE):
         cross_copy(0, s0, r0, j).wait_recv()
 
     def first(b, r):
@@ -249,15 +268,10 @@
             if lo < QC + KC:
                 piece = rope_pair(piece, cos_tab, sin_tab)
             qkv_o[:, lo:lo + 128] = piece.astype(BF)
-    for pair in range(HLOC // 2):
-        outs = []
-        for h in (2 * pair, 2 * pair + 1):
-            g = h // GROUP
-            k = qkv_o[:, QC + g * HD:QC + (g + 1) * HD]
-            v = qkv_o[:, QC + KC + g * HD:QC + KC + (g + 1) * HD]
-            probs = probs_of(qkv_o[:, h * HD:(h + 1) * HD], k).astype(BF)
-            outs.append(nn(probs, v).astype(BF))
-        heads_o[:, pair * 128:(pair + 1) * 128] = jnp.concatenate(outs, axis=1)
+    for g in range(KVLOC):
+        k = qkv_o[:, QC + g * HD:QC + (g + 1) * HD]
+        v = qkv_o[:, QC + KC + g * HD:QC + KC + (g + 1) * HD]
+        unstack(heads_o, g, nn(probs_of(stack(qkv_o, g), k).astype(BF), v).astype(BF))
     to_cross.wait_recv()
     onward = remote(gfull_o.at[1 - x, c], gfull_o.at[1 - x, c], hs.at[3], hr.at[3], partner)
     onward.start()
@@ -317,8 +331,9 @@
 
     for s in (sum0, sum1, sum2):
         s.drain()
+    for j in range(NE):
+        cross_copy(0, s0, r0, j).wait_send()
     for j in range(NC):
-        cross_copy(0, s0, r0, j).wait_send()
         cross_copy(1, s1, r1, j).wait_send()
     for copy in (to_cross, to_partner, share1, onward, share2):
         copy.wait_send()
@@ -349,28 +364,18 @@
         gheads_v[:, v * 256:(v + 1) * 256] = nt(gh1, wo[v * 256:(v + 1) * 256, :]).astype(BF)
 
     cos_tab, sin_tab = cs[0], -cs[1]
+    turn_back = lambda pair: rope_pair(pair.astype(F32), cos_tab, sin_tab)
     gks, gvs = [], []
     for g in range(KVLOC):
         k = qkv[:, QC + g * HD:QC + (g + 1) * HD]
         v = qkv[:, QC + KC + g * HD:QC + KC + (g + 1) * HD]
-        gk = gv = None
-        for pair in range(GROUP // 2):
-            outs = []
-            for h in (g * GROUP + 2 * pair, g * GROUP + 2 * pair + 1):
-                q = qkv[:, h * HD:(h + 1) * HD]
-                probs = probs_of(q, k)
-                gh = gheads_v[:, h * HD:(h + 1) * HD]
-                gp = nt(gh, v).astype(BF).astype(F32)
-                gvh = tn(probs.astype(BF), gh)
-                gs = (probs * (gp - jnp.sum(gp * probs, axis=-1, keepdims=True)) * SCALE).astype(BF)
-                outs.append(nn(gs, k).astype(BF).astype(F32))
-                gkh = tn(gs, q)
-                gk = gkh if gk is None else gk + gkh
-                gv = gvh if gv is None else gv + gvh
-            lo = (g * GROUP + 2 * pair) * HD
-            gqkv_o[:, lo:lo + 128] = rope_pair(jnp.concatenate(outs, axis=1), cos_tab, sin_tab).astype(BF)
-        gks.append(gk.astype(BF).astype(F32))
-        gvs.append(gv.astype(BF))
+        q, gh = stack(qkv, g), stack(gheads_v, g)
+        probs = probs_of(q, k)
+        gp = nt(gh, v).astype(BF).astype(F32)
+        gvs.append(tn(probs.astype(BF), gh).astype(BF))
+        gs = (probs * (gp - jnp.sum(gp * probs, axis=-1, keepdims=True)) * SCALE).astype(BF)
+        gks.append(tn(gs, q).astype(BF).astype(F32))
+        unstack(gqkv_o, g, nn(gs, k).astype(BF), turn_back)
     gqkv_o[:, QC:QC + KC] = rope_pair(jnp.concatenate(gks, axis=1), cos_tab, sin_tab).astype(BF)
     gqkv_o[:, QC + KC:] = jnp.concatenate(gvs, axis=1)
 
@@ -564,7 +569,7 @@
             pltpu.VMEM(FULL, BF), pltpu.VMEM(MINE, BF), pltpu.VMEM(MINE, BF), pltpu.VMEM(MINE, BF),
             pltpu.VMEM(FULL, BF), pltpu.VMEM(MINE, BF), pltpu.VMEM(MINE, BF), pltpu.VMEM(MINE, BF),
             pltpu.VMEM(FULL, BF), pltpu.VMEM(MINE, BF),
-            dma(6), dma(NC), dma(7), dma(3, NC), dma(3, NC), dma(2, NC), dma(2, NC), dma(5), dma(5)],
+            dma(6), dma(NE), dma(7), dma(3, NE), dma(3, NE), dma(2, NE), dma(2, NE), dma(5), dma(5)],
         compiler_params=pltpu.CompilerParams(collective_id=0, has_side_effects=True, vmem_limit_bytes=42 * 2 ** 20),
     )(tokens, positions, freq, ga, gm, gh2, emb, wqt, wkt, wvt, wo2, wd, wg, wu)
 

time: 78.2 us -> 76 us (0.972)
  Pallas kernels: 75.1 us -> 72.8 us
    pallas_call x1, Pallas kernels: 9.12 us -> 7.49 us  [device_fn(): pl.pallas_call(middle_kernel, out_shape=(on(FULL), on((SEQ, QKV)), on((3,...]
    ppermute x1, starting transfers between devices: 0.66 us -> 1.5 us  [device_fn(): got = lax.ppermute(give, 'tp', swap)]
    ppermute x1, starting transfers between devices: 1.43 us -> 0.6 us  [device_fn(): gn2_got = lax.ppermute(gn2, 'tp', swap)]
  transfers between devices with their start and end apart: 2 -> 2, of which waited for: 0 -> 0; matrix products, arithmetic and copies ran while one was open for 0% -> 0% of each run, Pallas kernels for 27% -> 28%
where the time goes in v4:
time: 76 us; the launch traced here: 75.8 us
  Pallas kernels  72.8 us (96%)
  starting transfers between devices  2.1 us (3%)
  between operations  0.9 us (1%)
    pallas_call x1, Pallas kernels, device_fn(): pl.pallas_call(front_kernel, out_shape=(on(FULL), on(MINE), on((SEQ, QKV)...  36 us
    pallas_call x2, Pallas kernels, outer(): pl.pallas_call(functools.partial(outer_kernel, spec, len(ins), len(held))...  20.9 us
    pallas_call x1, Pallas kernels, device_fn(): pl.pallas_call(middle_kernel, out_shape=(on(FULL), on((SEQ, QKV)), on((3,...  7.49 us
    pallas_call x1, Pallas kernels, device_fn(): pl.pallas_call(emb_kernel, out_shape=(sds((VLOC, DIM), F32), sds((1, DIM)...  6.38 us
    pallas_call x1, Pallas kernels, device_fn(): pl.pallas_call(back_kernel, out_shape=(on(FULL), on((2, DIM), F32), on((3...  2.13 us
  transfers between devices with their start and end apart: 2, of which 0 were waited for; matrix products, arithmetic and copies ran while one was open for 0% of the time, Pallas kernels for 28%

profile of v4, /device:TPU:0, one launch (start us, length us, event | category | flops | bytes accessed | tf_op | source)
XLA Modules:
  0.0 75.8 jit_solution(17655562008661235614)
XLA Ops:
  0.6 0.0 copy-start
  0.7 36.0 %shard_map.221 = (bf16[2,2,32,2048]{3,2,1,0:T(8,128)(2,1)S(1)}, bf16[2,32,2048]{2,1,0:T(8,128)(2,1)S(1)}, bf16[128,768]{1,0:T(8,128)(2,1)S(1)}, f32[2,128,128]{2...) custom-call(s32[1,128]{1,0:T(1,128)} %tok.3, ...), custom_call_target="tpu_custom_call" | custom-call | tf_op jit(solution)/shard_map/pallas_call | solution.py:556
  36.6 0.6 collective-permute-start
  37.2 8.2 %shard_map.222 = (f32[2048,2048]{1,0:T(8,128)}, f32[2048,2048]{1,0:T(8,128)}, f32[8,128]{1,0:T(8,128)S(1)}) custom-call(bf16[128,2048]{1,0:T(8,128)(2,1)S(1)} %bitcast.33, bf16[128,2048]{1,0:T(8,128)(2,1)S(1)} %get-tuple-element.58.refs_1_, bf16[128,2048]{1,0:T(8,128)(2,1)S(1)} %get-tuple-element.59.refs_2_.refs_1_), custom_call_target="tpu_custom_call" | custom-call | flops 1476395008 | bytes 23068672 | tf_op jit(solution)/shard_map/pallas_call | solution.py:489
  45.5 0.0 collective-permute-done.gn2_got
  45.5 0.0 copy-done
  45.5 7.5 %shard_map.223 = (bf16[2,2,32,2048]{3,2,1,0:T(8,128)(2,1)S(1)}, bf16[128,768]{1,0:T(8,128)(2,1)S(1)}, bf16[3,32,2048]{2,1,0:T(8,128)(2,1)S(1)}, bf16[32,2048]{1,0:T(8,128)(2,1)S(1)}, f32[1,2048]{1,0:T(1,128)S(1)}) custom-call(bf16[2,32,2048]{2,1,0:T(8,128)(2,1)S(1)} %get-tuple-element.48.gn2_own, bf16[2,32,2048]{2,1,0:T(8,128)(2,1)S(1)} %collective-permute-done.gn2_got, ...), custom_call_target="tpu_custom_call" | custom-call | tf_op jit(solution)/shard_map/pallas_call | solution.py:582
  53.0 1.5 %collective-permute-start.1 = (bf16[3,32,2048]{2,1,0:T(8,128)(2,1)S(1)}, bf16[3,32,2048]{2,1,0:T(8,128)(2,1)S(1)}, u32[]{:S(2)}, u32[]{:S(2)}) collective-permute-start(bf16[3,32,2048]{2,1,0:T(8,128)(2,1)S(1)} %get-tuple-element.61.give), channel_id=1, source_target_pairs={{0,2},{1,3},{2,0},{3,1},{4,6},{5,7},{6,4},{7,5},{8,10},{9,11},{10,... | collective-permute-start | bytes 1179656 | tf_op jit(solution)/shard_map/ppermute | solution.py:594
  54.5 0.0 copy-start.1
  54.5 0.0 copy-start.2
  54.5 12.6 %shard_map.224 = (f32[2048,2048]{1,0:T(8,128)}, f32[2048,2048]{1,0:T(8,128)}, f32[512,2048]{1,0:T(8,128)}, f32[512,2048]{1,0:T(8,128)}, f32[128,2048]{1,0:T(8,12...) custom-call(bf16[128,2048]{1,0:T(8,128)(2,1)S(1)} %bitcast.34, ...), custom_call_target="tpu_custom_call", output_to_operand_aliasing={{0}: (8, {})} | custom-call | flops 2415919104 | bytes 37748736 | tf_op jit(solution)/shard_map/pallas_call | solution.py:489
  67.1 0.0 collective-permute-done.1.got
  67.1 0.0 copy-done.1
  67.1 2.1 %shard_map.225 = (bf16[2,2,32,2048]{3,2,1,0:T(8,128)(2,1)S(1)}, f32[2,2048]{1,0:T(2,128)S(1)}, bf16[32,2048]{1,0:T(8,128)(2,1)S(1)}) custom-call(bf16[3,32,2048]{2,1,0:T(8,128)(2,1)S(1)} %get-tuple-element.61.give, bf16[3,32,2048]{2,1,0:T(8,128)(2,1)S(1)} %collective-permute-done.1.got, bf16[32,2048]{1,0:T(8,128)(2,1)S(1)} %get-tuple-element.62.keep, ...), custom_call_target="tpu_custom_call" | custom-call | tf_op jit(solution)/shard_map/pallas_call | solution.py:601
  69.3 0.0 copy-done.2
  69.3 6.4 %shard_map.226 = (f32[2048,2048]{1,0:T(8,128)}, f32[1,2048]{1,0:T(1,128)}, f32[1,2048]{1,0:T(1,128)}, bf16[32,2048]{1,0:T(8,128)(2,1)}) custom-call(s32[1,128]{1,0:T(1,128)S(1)} %copy-done.2, bf16[2,2,32,2048]{3,2,1,0:T(8,128)(2,1)S(1)} %get-tuple-element.71.gx, f32[2,2048]{1,0:T(2,128)S(1)} %get-tuple-element.72.gains, ...), custom_call_target="tpu_custom_call" | custom-call | tf_op jit(solution)/shard_map/pallas_call | solution.py:610
Async XLA Ops:
  0.6 44.8 %copy-start = (f32[2048]{0:T(1024)S(1)}, f32[2048]{0:T(1024)}, u32[]{:S(2)}) copy-start(f32[2048]{0:T(1024)} %param.18) | copy-start | bytes 24580
  36.6 8.8 %collective-permute-start = (bf16[2,32,2048]{2,1,0:T(8,128)(2,1)S(1)}, bf16[2,32,2048]{2,1,0:T(8,128)(2,1)S(1)}, u32[]{:S(2)}, u32[]{:S(2)}) collective-permute-start(bf16[2,32,2048]{2,1,0:T(8,128)(2,1)S(1)} %get-tuple-element.48.gn2_own), channel_id=1, source_target_pairs={{0,2},{1,3},{2,0},{3,1},{4,6},{5,7},{6,4},{7,5},{8,10},{9,11},{10,... | collective-permute-start | bytes 786440 | tf_op jit(solution)/shard_map/ppermute | solution.py:577
  53.0 14.1 %collective-permute-start.1 = (bf16[3,32,2048]{2,1,0:T(8,128)(2,1)S(1)}, bf16[3,32,2048]{2,1,0:T(8,128)(2,1)S(1)}, u32[]{:S(2)}, u32[]{:S(2)}) collective-permute-start(bf16[3,32,2048]{2,1,0:T(8,128)(2,1)S(1)} %get-tuple-element.61.give), channel_id=1, source_target_pairs={{0,2},{1,3},{2,0},{3,1},{4,6},{5,7},{6,4},{7,5},{8,10},{9,11},{10,... | collective-permute-start | bytes 1179656 | tf_op jit(solution)/shard_map/ppermute | solution.py:594
  54.5 12.6 %copy-start.1 = (f32[2048]{0:T(1024)S(1)}, f32[2048]{0:T(1024)}, u32[]{:S(2)}) copy-start(f32[2048]{0:T(1024)} %param.17) | copy-start | bytes 24580
  54.5 14.8 %copy-start.2 = (s32[1,128]{1,0:T(1,128)S(1)}, s32[1,128]{1,0:T(1,128)}, u32[]{:S(2)}) copy-start(s32[1,128]{1,0:T(1,128)} %tok.3) | copy-start | bytes 1540

commit v5 on v4

--- a/solution.py
+++ b/solution.py
@@ -30,7 +30,10 @@
 W = DIM // NC
 NE = 8
 WE = DIM // NE
-AHEAD = 3
+AHEAD = 6
+NB2 = 2
+WB = DIM // NB2
+LAG = 2
 VMEM = pltpu.VMEM
 HBM = pltpu.HBM
 
@@ -58,7 +61,7 @@
     sem = pltpu.get_barrier_semaphore()
     for peer in peers:
         pl.semaphore_signal(sem, inc=1, device_id={"tp": peer}, device_id_type=MESH)
-    pl.semaphore_wait(sem, len(peers))
+    return lambda: pl.semaphore_wait(sem, len(peers))
 
 
 def remote(src, dst, send, recv, peer):
@@ -171,7 +174,7 @@
 def front_kernel(tok, pos, freq, gain_a, gain_m, gh, emb, wq, wk, wv, wo, wd, wg, wu,
                  n1_o, x0_o, qkv_o, cs_o, heads_o, h1_o, n2_o, act_o, ggate_o, gup_o, gfull_o, gn2_o,
                  wqkv_v, wo_v, wd_v,
-                 tok_v, pos_v, freq_v, ga_v, gm_v, emb_v, wg_v, wu_v, wut_v, wqkvt_v, hot_v, gact_v,
+                 tok_v, pos_v, freq_v, ga_v, gm_v, emb_v, wg_v, wu_v, wut_v, hot_v, gact_v,
                  p0, g0, s0, r0, p1, g1, s1, r1, p2, g2,
                  in_sem, emb_sem, w_sem, ps, pr, xs, xr, hs, hr):
     x, c, partner, cross = place()
@@ -194,6 +197,7 @@
         fetch_emb(j).start()
     for g in get_small[1:]:
         g.start()
+    met = greet(partner, cross)
     get_small[0].wait()
     ids = spread(tok_v[...].astype(F32))
     base = (tp * VLOC).astype(F32)
@@ -201,7 +205,7 @@
     for v in range(VLOC // 128):
         hot_v[:, v * 128:(v + 1) * 128] = jnp.where(ids == lane + (base + float(v * 128)), 1.0, 0.0).astype(BF)
 
-    greet(partner, cross)
+    met()
 
     def cross_copy(k, src, dst, j):
         cj = cols(j, WE if k == 0 else W)
@@ -222,20 +226,20 @@
                 g.start()
         return nn(hot_v[...], emb_v[:, cols(j, WE)])
 
-    sum0.run(lookup, lambda j: cross_copy(0, s0, r0, j).start(), 1)
-    for g in (get_out, get_down, get_gate, get_up):
+    sum0.run(lookup, lambda j: cross_copy(0, s0, r0, j).start(), LAG)
+    for g in (get_out, get_up, get_down, get_gate):
         g.start()
     for g in get_small[1:]:
         g.wait()
     mine = gfull_o.at[x, c]
     to_cross = remote(mine, mine, hs.at[0], hr.at[0], cross)
     to_partner = remote(mine, mine, hs.at[1], hr.at[1], partner)
-    to_cross.start()
     to_partner.start()
     angle = spread(pos_v[...].astype(F32)) * freq_v[...]
     cs_o[0] = jnp.cos(angle)
     cs_o[1] = jnp.sin(angle)
 
+    wqkvt_v = wut_v
     for g in (get_q, get_k, get_v):
         g.wait()
 
@@ -247,6 +251,8 @@
 
     for j in range(NE):
         cross_copy(0, s0, r0, j).wait_recv()
+
+    to_cross.start()
 
     def first(b, r):
         xv = s0[b, r].astype(F32) + r0[b, r].astype(F32)
@@ -272,13 +278,20 @@
         k = qkv_o[:, QC + g * HD:QC + (g + 1) * HD]
         v = qkv_o[:, QC + KC + g * HD:QC + KC + (g + 1) * HD]
         unstack(heads_o, g, nn(probs_of(stack(qkv_o, g), k).astype(BF), v).astype(BF))
+    get_out.wait()
+
+    sum1 = PairSum(p1, g1, s1, (ps.at[1], pr.at[1]), c, partner)
+    sum1.run(lambda j: nn(heads_o[...], wo_v[:, cols(j)]), lambda j: cross_copy(1, s1, r1, j).start())
+
     to_cross.wait_recv()
     onward = remote(gfull_o.at[1 - x, c], gfull_o.at[1 - x, c], hs.at[3], hr.at[3], partner)
     onward.start()
-    get_out.wait()
-
-    sum1 = PairSum(p1, g1, s1, (ps.at[1], pr.at[1]), c, partner)
-    sum1.run(lambda j: nn(heads_o[...], wo_v[:, cols(j)]), lambda j: cross_copy(1, s1, r1, j).start())
+    get_up.wait()
+
+    def turn_up(j, carry):
+        wut_v[:, cols(j)] = jnp.transpose(wu_v[cols(j), :])
+        return carry
+    lax.fori_loop(0, NC, turn_up, 0)
 
     to_partner.wait_recv()
     onward.wait_recv()
@@ -292,12 +305,6 @@
         wgt_v[:, cols(j)] = jnp.transpose(wg_v[cols(j), :])
         return carry
     lax.fori_loop(0, NC, grad_act, 0)
-    get_up.wait()
-
-    def turn_up(j, carry):
-        wut_v[:, cols(j)] = jnp.transpose(wu_v[cols(j), :])
-        return carry
-    lax.fori_loop(0, NC, turn_up, 0)
 
     for j in range(NC):
         cross_copy(1, s1, r1, j).wait_recv()
@@ -314,7 +321,7 @@
     n2 = n2_o[...].reshape(SEQ, DIM)
 
     def mlp(j, carry):
-        cj = pl.ds(pl.multiple_of(j * 256, 256), 256)
+        cj = cols(j, WB)
         gate = nn(n2, wg_v[:, cj])
         up = nn(n2, wu_v[:, cj])
         sig = jax.nn.sigmoid(gate)
@@ -324,10 +331,10 @@
         gup_o[:, cj] = (grad * gate_act).astype(BF)
         ggate_o[:, cj] = (grad * up * sig * (1.0 + gate * (1.0 - sig))).astype(BF)
         return carry
-    lax.fori_loop(0, FLOC // 256, mlp, 0)
-
-    sum2 = PairSum(p2, g2, gn2_o, (ps.at[2], pr.at[2]), c, partner)
-    sum2.run(lambda j: nn(ggate_o[...], wgt_v[:, cols(j)]) + nn(gup_o[...], wut_v[:, cols(j)]))
+    lax.fori_loop(0, FLOC // WB, mlp, 0)
+
+    sum2 = PairSum(p2, g2, gn2_o, (ps.at[2], pr.at[2]), c, partner, NB2)
+    sum2.run(lambda j: nn(ggate_o[...], wgt_v[:, cols(j, WB)]) + nn(gup_o[...], wut_v[:, cols(j, WB)]))
 
     for s in (sum0, sum1, sum2):
         s.drain()
@@ -343,7 +350,7 @@
                   gh1_o, gqkv_o, give_o, keep_o, gain_o,
                   gheads_v, p0, g0, s0, p1, g1, ps, pr, hs, hr):
     x, c, partner, cross = place()
-    greet(partner)
+    met = greet(partner)
     gains = []
 
     def first(b, r):
@@ -352,11 +359,12 @@
         gh1_o[b, c, r] = (gfull[b, c, r].astype(F32) + back).astype(BF)
         gains.append(part)
     rows16(first)
+    met()
     share = remote(gh1_o.at[:, c], gh1_o.at[:, c], hs.at[0], hr.at[0], partner)
     share.start()
     gain_o[...] = gains[0] + gains[1] + gains[2] + gains[3]
-    sum0 = PairSum(p0, g0, s0, (ps.at[0], pr.at[0]), c, partner)
-    sum0.send_all(lambda j: nn(act[...], wd[:, cols(j)]))
+    sum0 = PairSum(p0, g0, s0, (ps.at[0], pr.at[0]), c, partner, NB2)
+    sum0.send_all(lambda j: nn(act[...], wd[:, cols(j, WB)]))
     share.wait_recv()
 
     gh1 = gh1_o[...].reshape(SEQ, DIM)
@@ -379,13 +387,13 @@
     gqkv_o[:, QC:QC + KC] = rope_pair(jnp.concatenate(gks, axis=1), cos_tab, sin_tab).astype(BF)
     gqkv_o[:, QC + KC:] = jnp.concatenate(gvs, axis=1)
 
-    sum1 = PairSum(p1, g1, give_o, (ps.at[1], pr.at[1]), c, partner)
-    sum1.send_all(lambda j: nn(gqkv_o[...], wqkv[:, cols(j)]))
-    for j in range(NC):
+    sum1 = PairSum(p1, g1, give_o, (ps.at[1], pr.at[1]), c, partner, NB2)
+    sum1.send_all(lambda j: nn(gqkv_o[...], wqkv[:, cols(j, WB)]))
+    for j in range(NB2):
         sum0.take(j)
     give_o[2] = s0[1 - x]
     keep_o[...] = s0[x]
-    for j in range(NC):
+    for j in range(NB2):
         sum1.take(j)
     sum0.drain()
     sum1.drain()
@@ -394,7 +402,7 @@
 
 def back_kernel(give, got, keep, h1, x0, gh1, gain_a, gain_mp, token, gx_o, gain_o, hid_o, gbuf, hs, hr):
     x, c, partner, cross = place()
-    greet(partner)
+    met = greet(partner)
     gains = []
 
     def first(b, r):
@@ -403,6 +411,7 @@
         gx_o[b, c, r] = (gh1[b, c, r].astype(F32) + back).astype(BF)
         gains.append(part)
     rows16(first)
+    met()
     share = remote(gx_o.at[:, c], gx_o.at[:, c], hs.at[0], hr.at[0], partner)
     share.start()
     gbuf[c, 0:1] = gains[0] + gains[1] + gains[2] + gains[3]
@@ -564,13 +573,13 @@
             pltpu.VMEM((1, SEQ), jnp.int32), pltpu.VMEM((1, SEQ), jnp.int32), pltpu.VMEM((1, SEQ), F32),
             pltpu.VMEM((1, DIM), F32), pltpu.VMEM((1, DIM), F32),
             pltpu.VMEM((VLOC, DIM), BF), pltpu.VMEM((DIM, FLOC), BF), pltpu.VMEM((DIM, FLOC), BF),
-            pltpu.VMEM((FLOC, DIM), BF), pltpu.VMEM((DIM, QKV), BF),
+            pltpu.VMEM((FLOC, DIM), BF),
             pltpu.VMEM((SEQ, VLOC), BF), pltpu.VMEM((SEQ, FLOC), BF),
             pltpu.VMEM(FULL, BF), pltpu.VMEM(MINE, BF), pltpu.VMEM(MINE, BF), pltpu.VMEM(MINE, BF),
             pltpu.VMEM(FULL, BF), pltpu.VMEM(MINE, BF), pltpu.VMEM(MINE, BF), pltpu.VMEM(MINE, BF),
             pltpu.VMEM(FULL, BF), pltpu.VMEM(MINE, BF),
             dma(6), dma(NE), dma(7), dma(3, NE), dma(3, NE), dma(2, NE), dma(2, NE), dma(5), dma(5)],
-        compiler_params=pltpu.CompilerParams(collective_id=0, has_side_effects=True, vmem_limit_bytes=42 * 2 ** 20),
+        compiler_params=pltpu.CompilerParams(collective_id=0, has_side_effects=True, vmem_limit_bytes=44 * 2 ** 20),
     )(tokens, positions, freq, ga, gm, gh2, emb, wqt, wkt, wvt, wo2, wd, wg, wu)
 
     swap = [(i, i ^ 2) for i in range(4)]

time: 76 us -> 72 us (0.947)
  Pallas kernels: 72.8 us -> 68.8 us
    pallas_call x1, Pallas kernels: 36 us -> 33.4 us  [device_fn(): pl.pallas_call(front_kernel, out_shape=(on(FULL), on(MINE), on((SEQ, QKV)...]
    pallas_call x1, Pallas kernels: 7.49 us -> 6.46 us  [device_fn(): pl.pallas_call(middle_kernel, out_shape=(on(FULL), on((SEQ, QKV)), on((3,...]
  transfers between devices with their start and end apart: 2 -> 2, of which waited for: 0 -> 0; matrix products, arithmetic and copies ran while one was open for 0% -> 0% of each run, Pallas kernels for 28% -> 29%
where the time goes in v5:
time: 72 us; the launch traced here: 71.9 us
  Pallas kernels  68.8 us (96%)
  starting transfers between devices  2.1 us (3%)
  between operations  0.9 us (1%)
    pallas_call x1, Pallas kernels, device_fn(): pl.pallas_call(front_kernel, out_shape=(on(FULL), on(MINE), on((SEQ, QKV)...  33.4 us
    pallas_call x2, Pallas kernels, outer(): pl.pallas_call(functools.partial(outer_kernel, spec, len(ins), len(held))...  20.9 us
    pallas_call x1, Pallas kernels, device_fn(): pl.pallas_call(middle_kernel, out_shape=(on(FULL), on((SEQ, QKV)), on((3,...  6.46 us
    pallas_call x1, Pallas kernels, device_fn(): pl.pallas_call(emb_kernel, out_shape=(sds((VLOC, DIM), F32), sds((1, DIM)...  6.38 us
    pallas_call x1, Pallas kernels, device_fn(): pl.pallas_call(back_kernel, out_shape=(on(FULL), on((2, DIM), F32), on((3...  1.75 us
  transfers between devices with their start and end apart: 2, of which 0 were waited for; matrix products, arithmetic and copies ran while one was open for 0% of the time, Pallas kernels for 29%

profile of v5, /device:TPU:0, one launch (start us, length us, event | category | flops | bytes accessed | tf_op | source)
XLA Modules:
  0.0 71.9 jit_solution(776485575520579008)
XLA Ops:
  0.6 0.0 copy-start
  0.7 33.4 %shard_map.221 = (bf16[2,2,32,2048]{3,2,1,0:T(8,128)(2,1)S(1)}, bf16[2,32,2048]{2,1,0:T(8,128)(2,1)S(1)}, bf16[128,768]{1,0:T(8,128)(2,1)S(1)}, f32[2,128,128]{2...) custom-call(s32[1,128]{1,0:T(1,128)} %tok.3, ...), custom_call_target="tpu_custom_call" | custom-call | tf_op jit(solution)/shard_map/pallas_call | solution.py:565
  34.1 1.3 %collective-permute-start = (bf16[2,32,2048]{2,1,0:T(8,128)(2,1)S(1)}, bf16[2,32,2048]{2,1,0:T(8,128)(2,1)S(1)}, u32[]{:S(2)}, u32[]{:S(2)}) collective-permute-start(bf16[2,32,2048]{2,1,0:T(8,128)(2,1)S(1)} %get-tuple-element.48.gn2_own), channel_id=1, source_target_pairs={{0,2},{1,3},{2,0},{3,1},{4,6},{5,7},{6,4},{7,5},{8,10},{9,11},{10,... | collective-permute-start | bytes 786440 | tf_op jit(solution)/shard_map/ppermute | solution.py:586
  35.3 8.2 %shard_map.222 = (f32[2048,2048]{1,0:T(8,128)}, f32[2048,2048]{1,0:T(8,128)}, f32[8,128]{1,0:T(8,128)S(1)}) custom-call(bf16[128,2048]{1,0:T(8,128)(2,1)S(1)} %bitcast.33, bf16[128,2048]{1,0:T(8,128)(2,1)S(1)} %get-tuple-element.58.refs_1_, bf16[128,2048]{1,0:T(8,128)(2,1)S(1)} %get-tuple-element.59.refs_2_.refs_1_), custom_call_target="tpu_custom_call" | custom-call | flops 1476395008 | bytes 23068672 | tf_op jit(solution)/shard_map/pallas_call | solution.py:498
  43.6 0.0 collective-permute-done.gn2_got
  43.6 0.0 copy-done
  43.6 6.5 %shard_map.223 = (bf16[2,2,32,2048]{3,2,1,0:T(8,128)(2,1)S(1)}, bf16[128,768]{1,0:T(8,128)(2,1)S(1)}, bf16[3,32,2048]{2,1,0:T(8,128)(2,1)S(1)}, bf16[32,2048]{1,0:T(8,128)(2,1)S(1)}, f32[1,2048]{1,0:T(1,128)S(1)}) custom-call(bf16[2,32,2048]{2,1,0:T(8,128)(2,1)S(1)} %get-tuple-element.48.gn2_own, bf16[2,32,2048]{2,1,0:T(8,128)(2,1)S(1)} %collective-permute-done.gn2_got, ...), custom_call_target="tpu_custom_call" | custom-call | tf_op jit(solution)/shard_map/pallas_call | solution.py:591
  50.1 0.8 %collective-permute-start.1 = (bf16[3,32,2048]{2,1,0:T(8,128)(2,1)S(1)}, bf16[3,32,2048]{2,1,0:T(8,128)(2,1)S(1)}, u32[]{:S(2)}, u32[]{:S(2)}) collective-permute-start(bf16[3,32,2048]{2,1,0:T(8,128)(2,1)S(1)} %get-tuple-element.61.give), channel_id=1, source_target_pairs={{0,2},{1,3},{2,0},{3,1},{4,6},{5,7},{6,4},{7,5},{8,10},{9,11},{10,... | collective-permute-start | bytes 1179656 | tf_op jit(solution)/shard_map/ppermute | solution.py:603
  50.9 0.0 copy-start.1
  50.9 0.0 copy-start.2
  50.9 12.6 %shard_map.224 = (f32[2048,2048]{1,0:T(8,128)}, f32[2048,2048]{1,0:T(8,128)}, f32[512,2048]{1,0:T(8,128)}, f32[512,2048]{1,0:T(8,128)}, f32[128,2048]{1,0:T(8,12...) custom-call(bf16[128,2048]{1,0:T(8,128)(2,1)S(1)} %bitcast.34, ...), custom_call_target="tpu_custom_call", output_to_operand_aliasing={{0}: (8, {})} | custom-call | flops 2415919104 | bytes 37748736 | tf_op jit(solution)/shard_map/pallas_call | solution.py:498
  63.5 0.0 collective-permute-done.1.got
  63.5 0.0 copy-done.1
  63.6 1.7 %shard_map.225 = (bf16[2,2,32,2048]{3,2,1,0:T(8,128)(2,1)S(1)}, f32[2,2048]{1,0:T(2,128)S(1)}, bf16[32,2048]{1,0:T(8,128)(2,1)S(1)}) custom-call(bf16[3,32,2048]{2,1,0:T(8,128)(2,1)S(1)} %get-tuple-element.61.give, bf16[3,32,2048]{2,1,0:T(8,128)(2,1)S(1)} %collective-permute-done.1.got, bf16[32,2048]{1,0:T(8,128)(2,1)S(1)} %get-tuple-element.62.keep, ...), custom_call_target="tpu_custom_call" | custom-call | tf_op jit(solution)/shard_map/pallas_call | solution.py:610
  65.3 0.0 copy-done.2
  65.3 6.4 %shard_map.226 = (f32[2048,2048]{1,0:T(8,128)}, f32[1,2048]{1,0:T(1,128)}, f32[1,2048]{1,0:T(1,128)}, bf16[32,2048]{1,0:T(8,128)(2,1)}) custom-call(s32[1,128]{1,0:T(1,128)S(1)} %copy-done.2, bf16[2,2,32,2048]{3,2,1,0:T(8,128)(2,1)S(1)} %get-tuple-element.71.gx, f32[2,2048]{1,0:T(2,128)S(1)} %get-tuple-element.72.gains, ...), custom_call_target="tpu_custom_call" | custom-call | tf_op jit(solution)/shard_map/pallas_call | solution.py:619
Async XLA Ops:
  0.6 42.9 %copy-start = (f32[2048]{0:T(1024)S(1)}, f32[2048]{0:T(1024)}, u32[]{:S(2)}) copy-start(f32[2048]{0:T(1024)} %param.18) | copy-start | bytes 24580
  34.1 9.5 %collective-permute-start = (bf16[2,32,2048]{2,1,0:T(8,128)(2,1)S(1)}, bf16[2,32,2048]{2,1,0:T(8,128)(2,1)S(1)}, u32[]{:S(2)}, u32[]{:S(2)}) collective-permute-start(bf16[2,32,2048]{2,1,0:T(8,128)(2,1)S(1)} %get-tuple-element.48.gn2_own), channel_id=1, source_target_pairs={{0,2},{1,3},{2,0},{3,1},{4,6},{5,7},{6,4},{7,5},{8,10},{9,11},{10,... | collective-permute-start | bytes 786440 | tf_op jit(solution)/shard_map/ppermute | solution.py:586
  50.1 13.5 %collective-permute-start.1 = (bf16[3,32,2048]{2,1,0:T(8,128)(2,1)S(1)}, bf16[3,32,2048]{2,1,0:T(8,128)(2,1)S(1)}, u32[]{:S(2)}, u32[]{:S(2)}) collective-permute-start(bf16[3,32,2048]{2,1,0:T(8,128)(2,1)S(1)} %get-tuple-element.61.give), channel_id=1, source_target_pairs={{0,2},{1,3},{2,0},{3,1},{4,6},{5,7},{6,4},{7,5},{8,10},{9,11},{10,... | collective-permute-start | bytes 1179656 | tf_op jit(solution)/shard_map/ppermute | solution.py:603
  50.9 12.6 %copy-start.1 = (f32[2048]{0:T(1024)S(1)}, f32[2048]{0:T(1024)}, u32[]{:S(2)}) copy-start(f32[2048]{0:T(1024)} %param.17) | copy-start | bytes 24580
  50.9 14.4 %copy-start.2 = (s32[1,128]{1,0:T(1,128)S(1)}, s32[1,128]{1,0:T(1,128)}, u32[]{:S(2)}) copy-start(s32[1,128]{1,0:T(1,128)} %tok.3) | copy-start | bytes 1540

commit v6 on v5

--- a/solution.py
+++ b/solution.py
@@ -346,9 +346,9 @@
         copy.wait_send()
 
 
-def middle_kernel(gn2_own, gn2_got, act, h1, gfull, gain_m, qkv, cs, wqkv, wo, wd, token,
+def middle_kernel(gn2_own, gn2_got, part, h1, gfull, gain_m, qkv, cs, wqkv, wo, token,
                   gh1_o, gqkv_o, give_o, keep_o, gain_o,
-                  gheads_v, p0, g0, s0, p1, g1, ps, pr, hs, hr):
+                  gheads_v, probs_v, g0, s0, p1, g1, ps, pr, hs, hr):
     x, c, partner, cross = place()
     met = greet(partner)
     gains = []
@@ -363,8 +363,10 @@
     share = remote(gh1_o.at[:, c], gh1_o.at[:, c], hs.at[0], hr.at[0], partner)
     share.start()
     gain_o[...] = gains[0] + gains[1] + gains[2] + gains[3]
-    sum0 = PairSum(p0, g0, s0, (ps.at[0], pr.at[0]), c, partner, NB2)
-    sum0.send_all(lambda j: nn(act[...], wd[:, cols(j, WB)]))
+    sum0 = PairSum(part, g0, s0, (ps.at[0], pr.at[0]), c, partner, 1)
+    sum0.copy(0).start()
+    for g in range(KVLOC):
+        probs_v[g] = probs_of(stack(qkv, g), qkv[:, QC + g * HD:QC + (g + 1) * HD])
     share.wait_recv()
 
     gh1 = gh1_o[...].reshape(SEQ, DIM)
@@ -378,7 +380,7 @@
         k = qkv[:, QC + g * HD:QC + (g + 1) * HD]
         v = qkv[:, QC + KC + g * HD:QC + KC + (g + 1) * HD]
         q, gh = stack(qkv, g), stack(gheads_v, g)
-        probs = probs_of(q, k)
+        probs = probs_v[g]
         gp = nt(gh, v).astype(BF).astype(F32)
         gvs.append(tn(probs.astype(BF), gh).astype(BF))
         gs = (probs * (gp - jnp.sum(gp * probs, axis=-1, keepdims=True)) * SCALE).astype(BF)
@@ -389,8 +391,7 @@
 
     sum1 = PairSum(p1, g1, give_o, (ps.at[1], pr.at[1]), c, partner, NB2)
     sum1.send_all(lambda j: nn(gqkv_o[...], wqkv[:, cols(j, WB)]))
-    for j in range(NB2):
-        sum0.take(j)
+    sum0.take(0)
     give_o[2] = s0[1 - x]
     keep_o[...] = s0[x]
     for j in range(NB2):
@@ -438,15 +439,17 @@
     return pltpu.VMEM(shape, dtype)
 
 
-NB = 4
-UP_FIRST = 768
-BM = 256
-
-
-def outer_kernel(spec, n_in, n_held, *refs):
+NB = 3
+BM = 512
+UP_FIRST = 512
+EB = 256
+ENB = 4
+
+
+def outer_kernel(spec, n_in, n_held, side, *refs):
     n_out = 1 + max(o for _, _, _, o, _, _ in spec)
     ins, outs = refs[:n_in], refs[n_in + n_held:n_in + n_held + n_out]
-    token, buf, sem = refs[n_in + n_held + n_out:]
+    *part, token, buf, sem = refs[n_in + n_held + n_out:]
     token[...] = jnp.zeros_like(token)
     done = 0
     flying = {}
@@ -489,23 +492,28 @@
                 copy(i).start()
                 flying[slot] = bm
         done += steps
+        if side and done == steps:
+            for j in range(NB2):
+                lo, hi = j * WB, (j + 1) * WB
+                out = nn(ins[side[0]][...], ins[side[1]][:, lo:hi])
+                part[0][:, :, :, lo:hi] = out.astype(BF).reshape(2, 2, 32, WB)
     for slot, size in flying.items():
         pltpu.make_async_copy(buf.at[slot, pl.ds(0, size)], outs[0].at[pl.ds(0, size)], sem.at[slot]).wait()
 
 
-def outer(ins, spec, rows, held=()):
+def outer(ins, spec, rows, held=(), side=()):
     total = sum(n for *_, n in spec)
-    *outs, token = pl.pallas_call(
-        functools.partial(outer_kernel, spec, len(ins), len(held)),
-        out_shape=tuple(jax.ShapeDtypeStruct((m, DIM), F32) for m in rows) + (on((8, 128), F32),),
+    extra = (on(FULL),) if side else ()
+    return pl.pallas_call(
+        functools.partial(outer_kernel, spec, len(ins), len(held), side),
+        out_shape=tuple(jax.ShapeDtypeStruct((m, DIM), F32) for m in rows) + extra + (on((8, 128), F32),),
         in_specs=vm(len(ins)) + hb(len(held)),
-        out_specs=tuple(hb(len(rows)) + vm(1)),
+        out_specs=tuple(hb(len(rows)) + vm(1 + len(extra))),
         scratch_shapes=[pltpu.VMEM((NB, BM, DIM), F32), pltpu.SemaphoreType.DMA((NB,))],
         input_output_aliases={len(ins) + i: o for i, (_, o) in enumerate(held)},
         cost_estimate=pl.CostEstimate(flops=2 * total * DIM * SEQ, bytes_accessed=4 * total * DIM, transcendentals=0),
-        compiler_params=pltpu.CompilerParams(vmem_limit_bytes=16 * 2 ** 20),
+        compiler_params=pltpu.CompilerParams(vmem_limit_bytes=24 * 2 ** 20),
     )(*ins, *[h for h, _ in held])
-    return outs, token
 
 
 def emb_kernel(tok, gx, gains, hid, out, ga_o, gm_o, hid_o, buf, sem, out_sem):
@@ -517,25 +525,25 @@
     for e in extra:
         e.start()
     base = lax.axis_index("tp") * VLOC
-    ids = jnp.broadcast_to(tok[...], (BM, SEQ)) - base
-    row = lax.broadcasted_iota(jnp.int32, (BM, SEQ), 0)
+    ids = jnp.broadcast_to(tok[...], (EB, SEQ)) - base
+    row = lax.broadcasted_iota(jnp.int32, (EB, SEQ), 0)
     grad = gx[...].reshape(SEQ, DIM)
 
     def copy(i):
-        slot = lax.rem(i, NB)
-        return pltpu.make_async_copy(buf.at[slot], out.at[pl.ds(pl.multiple_of(i * BM, BM), BM)], sem.at[slot])
+        slot = lax.rem(i, ENB)
+        return pltpu.make_async_copy(buf.at[slot], out.at[pl.ds(pl.multiple_of(i * EB, EB), EB)], sem.at[slot])
 
     def step(i, carry):
-        @pl.when(i >= NB)
+        @pl.when(i >= ENB)
         def _():
             copy(i).wait()
-        hot = jnp.where(ids == row + i * BM, 1.0, 0.0).astype(BF)
-        buf[lax.rem(i, NB)] = nn(hot, grad)
+        hot = jnp.where(ids == row + i * EB, 1.0, 0.0).astype(BF)
+        buf[lax.rem(i, ENB)] = nn(hot, grad)
         copy(i).start()
         return carry
-    steps = VLOC // BM
+    steps = VLOC // EB
     lax.fori_loop(0, steps, step, 0)
-    for k in range(steps - NB, steps):
+    for k in range(steps - ENB, steps):
         copy(k).wait()
     for e in extra:
         e.wait()
@@ -586,22 +594,23 @@
     gn2_got = lax.ppermute(gn2, 'tp', swap)
     gfull2 = gfull.reshape(SEQ, DIM)
     n2f = n2.reshape(SEQ, DIM)
-    (g_gate, g_up), token = outer((n2f, ggate, gup), ((0, 1, 0, 0, 0, DIM), (0, 2, 0, 1, 0, UP_FIRST)), (DIM, DIM))
+    g_gate, g_up, part, token = outer(
+        (n2f, ggate, gup, act, wd_v), ((0, 1, 0, 0, 0, DIM), (0, 2, 0, 1, 0, UP_FIRST)), (DIM, DIM), side=(3, 4))
 
     gh1, gqkv, give, keep, gain_mp = pl.pallas_call(
         middle_kernel,
         out_shape=(on(FULL), on((SEQ, QKV)), on((3, 32, DIM)), on((32, DIM)), on((1, DIM), F32)),
-        in_specs=vm(12),
+        in_specs=vm(11),
         out_specs=tuple(vm(5)),
         scratch_shapes=[
-            pltpu.VMEM((SEQ, QC), BF),
-            pltpu.VMEM(FULL, BF), pltpu.VMEM(MINE, BF), pltpu.VMEM(MINE, BF), pltpu.VMEM(FULL, BF), pltpu.VMEM(MINE, BF),
+            pltpu.VMEM((SEQ, QC), BF), pltpu.VMEM((KVLOC, GROUP * SEQ, SEQ), F32),
+            pltpu.VMEM(MINE, BF), pltpu.VMEM(MINE, BF), pltpu.VMEM(FULL, BF), pltpu.VMEM(MINE, BF),
             dma(2, NC), dma(2, NC), dma(1), dma(1)],
         compiler_params=pltpu.CompilerParams(collective_id=1, has_side_effects=True, vmem_limit_bytes=8 * 2 ** 20),
-    )(gn2, gn2_got, act, h1, gfull, gm, qkv, cs, wqkv_v, wo_v, wd_v, token)
+    )(gn2, gn2_got, part, h1, gfull, gm, qkv, cs, wqkv_v, wo_v, token)
 
     got = lax.ppermute(give, 'tp', swap)
-    (g_up, g_down, g_out, g_q, g_k, g_v), token2 = outer(
+    g_up, g_down, g_out, g_q, g_k, g_v, token2 = outer(
         (n2f, gup, act, gfull2, heads, gh1.reshape(SEQ, DIM), gqkv, n1.reshape(SEQ, DIM)),
         ((0, 1, UP_FIRST, 0, UP_FIRST, DIM - UP_FIRST), (2, 3, 0, 1, 0, FLOC), (4, 5, 0, 2, 0, QC),
          (6, 7, 0, 3, 0, QC), (6, 7, QC, 4, 0, KC), (6, 7, QC + KC, 5, 0, KC)),
@@ -621,7 +630,7 @@
         out_shape=(sds((VLOC, DIM), F32), sds((1, DIM), F32), sds((1, DIM), F32), sds((32, DIM))),
         in_specs=vm(4),
         out_specs=tuple(hb(4)),
-        scratch_shapes=[pltpu.VMEM((NB, BM, DIM), F32), dma(NB), dma(3)],
+        scratch_shapes=[pltpu.VMEM((ENB, EB, DIM), F32), dma(ENB), dma(3)],
         compiler_params=pltpu.CompilerParams(vmem_limit_bytes=24 * 2 ** 20),
     )(tokens, gx, gains, hid)
 

time: 72 us -> 72 us (level)
  transfers between devices with their start and end apart: 2 -> 2, of which waited for: 0 -> 0; matrix products, arithmetic and copies ran while one was open for 0% -> 0% of each run, Pallas kernels for 29% -> 30%
where the time goes in v6:
time: 72 us; the launch traced here: 71.9 us
  Pallas kernels  68.9 us (96%)
  starting transfers between devices  2.1 us (3%)
  between operations  0.9 us (1%)
    pallas_call x1, Pallas kernels, device_fn(): pl.pallas_call(front_kernel, out_shape=(on(FULL), on(MINE), on((SEQ, QKV)...  33.4 us
    pallas_call x2, Pallas kernels, outer(): pl.pallas_call(functools.partial(outer_kernel, spec, len(ins), len(held),...  21.4 us
    pallas_call x1, Pallas kernels, device_fn(): pl.pallas_call(emb_kernel, out_shape=(sds((VLOC, DIM), F32), sds((1, DIM)...  6.38 us
    pallas_call x1, Pallas kernels, device_fn(): pl.pallas_call(middle_kernel, out_shape=(on(FULL), on((SEQ, QKV)), on((3,...  5.88 us
    pallas_call x1, Pallas kernels, device_fn(): pl.pallas_call(back_kernel, out_shape=(on(FULL), on((2, DIM), F32), on((3...  1.75 us
  transfers between devices with their start and end apart: 2, of which 0 were waited for; matrix products, arithmetic and copies ran while one was open for 0% of the time, Pallas kernels for 30%

profile of v6, /device:TPU:0, one launch (start us, length us, event | category | flops | bytes accessed | tf_op | source)
XLA Modules:
  0.0 71.9 jit_solution(1594682012987669423)
XLA Ops:
  0.6 33.4 %shard_map.221 = (bf16[2,2,32,2048]{3,2,1,0:T(8,128)(2,1)S(1)}, bf16[2,32,2048]{2,1,0:T(8,128)(2,1)S(1)}, bf16[128,768]{1,0:T(8,128)(2,1)S(1)}, f32[2,128,128]{2...) custom-call(s32[1,128]{1,0:T(1,128)} %tok.3, ...), custom_call_target="tpu_custom_call" | custom-call | tf_op jit(solution)/shard_map/pallas_call | solution.py:573
  34.1 0.0 copy-start.1
  34.1 1.2 %collective-permute-start = (bf16[2,32,2048]{2,1,0:T(8,128)(2,1)S(1)}, bf16[2,32,2048]{2,1,0:T(8,128)(2,1)S(1)}, u32[]{:S(2)}, u32[]{:S(2)}) collective-permute-start(bf16[2,32,2048]{2,1,0:T(8,128)(2,1)S(1)} %get-tuple-element.49.gn2_own), channel_id=1, source_target_pairs={{0,2},{1,3},{2,0},{3,1},{4,6},{5,7},{6,4},{7,5},{8,10},{9,11},{10,... | collective-permute-start | bytes 786440 | tf_op jit(solution)/shard_map/ppermute | solution.py:594
  35.3 7.9 %shard_map.222 = (f32[2048,2048]{1,0:T(8,128)}, f32[2048,2048]{1,0:T(8,128)}, bf16[2,2,32,2048]{3,2,1,0:T(8,128)(2,1)S(1)}, f32[8,128]{1,0:T(8,128)S(1)}) custom-call(bf16[128,2048]{1,0:T(8,128)(2,1)S(1)} %bitcast.30, bf16[128,2048]{1,0:T(8,128)(2,1)S(1)} %get-tuple-element.51.refs_1_, bf16[128,2048]{1,0:T(8,128)(2,1)S(1)} %get-tuple-element.52.refs_2_.refs_1_, ...), custom_call_target="tpu_custom_call" | custom-call | flops 1342177280 | bytes 20971520 | tf_op jit(solution)/shard_map/pallas_call | solution.py:507
  43.3 0.0 collective-permute-done.gn2_got
  43.3 0.0 copy-done.1
  43.3 5.9 %shard_map.223 = (bf16[2,2,32,2048]{3,2,1,0:T(8,128)(2,1)S(1)}, bf16[128,768]{1,0:T(8,128)(2,1)S(1)}, bf16[3,32,2048]{2,1,0:T(8,128)(2,1)S(1)}, bf16[32,2048]{1,0:T(8,128)(2,1)S(1)}, f32[1,2048]{1,0:T(1,128)S(1)}) custom-call(bf16[2,32,2048]{2,1,0:T(8,128)(2,1)S(1)} %get-tuple-element.49.gn2_own, bf16[2,32,2048]{2,1,0:T(8,128)(2,1)S(1)} %collective-permute-done.gn2_got, ...), custom_call_target="tpu_custom_call" | custom-call | tf_op jit(solution)/shard_map/pallas_call | solution.py:600
  49.2 0.9 %collective-permute-start.1 = (bf16[3,32,2048]{2,1,0:T(8,128)(2,1)S(1)}, bf16[3,32,2048]{2,1,0:T(8,128)(2,1)S(1)}, u32[]{:S(2)}, u32[]{:S(2)}) collective-permute-start(bf16[3,32,2048]{2,1,0:T(8,128)(2,1)S(1)} %get-tuple-element.63.give), channel_id=1, source_target_pairs={{0,2},{1,3},{2,0},{3,1},{4,6},{5,7},{6,4},{7,5},{8,10},{9,11},{10,... | collective-permute-start | bytes 1179656 | tf_op jit(solution)/shard_map/ppermute | solution.py:612
  50.0 0.0 copy-start
  50.0 0.0 copy-start.2
  50.0 13.5 %shard_map.224 = (f32[2048,2048]{1,0:T(8,128)}, f32[2048,2048]{1,0:T(8,128)}, f32[512,2048]{1,0:T(8,128)}, f32[512,2048]{1,0:T(8,128)}, f32[128,2048]{1,0:T(8,12...) custom-call(bf16[128,2048]{1,0:T(8,128)(2,1)S(1)} %bitcast.31, ...), custom_call_target="tpu_custom_call", output_to_operand_aliasing={{0}: (8, {})} | custom-call | flops 2550136832 | bytes 39845888 | tf_op jit(solution)/shard_map/pallas_call | solution.py:507
  63.5 0.0 collective-permute-done.1.got
  63.6 0.0 copy-done
  63.6 1.7 %shard_map.225 = (bf16[2,2,32,2048]{3,2,1,0:T(8,128)(2,1)S(1)}, f32[2,2048]{1,0:T(2,128)S(1)}, bf16[32,2048]{1,0:T(8,128)(2,1)S(1)}) custom-call(bf16[3,32,2048]{2,1,0:T(8,128)(2,1)S(1)} %get-tuple-element.63.give, bf16[3,32,2048]{2,1,0:T(8,128)(2,1)S(1)} %collective-permute-done.1.got, bf16[32,2048]{1,0:T(8,128)(2,1)S(1)} %get-tuple-element.64.keep, ...), custom_call_target="tpu_custom_call" | custom-call | tf_op jit(solution)/shard_map/pallas_call | solution.py:619
  65.3 0.0 copy-done.2
  65.3 6.4 %shard_map.226 = (f32[2048,2048]{1,0:T(8,128)}, f32[1,2048]{1,0:T(1,128)}, f32[1,2048]{1,0:T(1,128)}, bf16[32,2048]{1,0:T(8,128)(2,1)}) custom-call(s32[1,128]{1,0:T(1,128)S(1)} %copy-done.2, bf16[2,2,32,2048]{3,2,1,0:T(8,128)(2,1)S(1)} %get-tuple-element.73.gx, f32[2,2048]{1,0:T(2,128)S(1)} %get-tuple-element.74.gains, ...), custom_call_target="tpu_custom_call" | custom-call | tf_op jit(solution)/shard_map/pallas_call | solution.py:628
Async XLA Ops:
  34.1 9.2 %copy-start.1 = (f32[2048]{0:T(1024)S(1)}, f32[2048]{0:T(1024)}, u32[]{:S(2)}) copy-start(f32[2048]{0:T(1024)} %param.18) | copy-start | bytes 24580
  34.1 9.2 %collective-permute-start = (bf16[2,32,2048]{2,1,0:T(8,128)(2,1)S(1)}, bf16[2,32,2048]{2,1,0:T(8,128)(2,1)S(1)}, u32[]{:S(2)}, u32[]{:S(2)}) collective-permute-start(bf16[2,32,2048]{2,1,0:T(8,128)(2,1)S(1)} %get-tuple-element.49.gn2_own), channel_id=1, source_target_pairs={{0,2},{1,3},{2,0},{3,1},{4,6},{5,7},{6,4},{7,5},{8,10},{9,11},{10,... | collective-permute-start | bytes 786440 | tf_op jit(solution)/shard_map/ppermute | solution.py:594
  49.2 14.4 %collective-permute-start.1 = (bf16[3,32,2048]{2,1,0:T(8,128)(2,1)S(1)}, bf16[3,32,2048]{2,1,0:T(8,128)(2,1)S(1)}, u32[]{:S(2)}, u32[]{:S(2)}) collective-permute-start(bf16[3,32,2048]{2,1,0:T(8,128)(2,1)S(1)} %get-tuple-element.63.give), channel_id=1, source_target_pairs={{0,2},{1,3},{2,0},{3,1},{4,6},{5,7},{6,4},{7,5},{8,10},{9,11},{10,... | collective-permute-start | bytes 1179656 | tf_op jit(solution)/shard_map/ppermute | solution.py:612
  50.0 13.5 %copy-start = (f32[2048]{0:T(1024)S(1)}, f32[2048]{0:T(1024)}, u32[]{:S(2)}) copy-start(f32[2048]{0:T(1024)} %param.17) | copy-start | bytes 24580
  50.0 15.3 %copy-start.2 = (s32[1,128]{1,0:T(1,128)S(1)}, s32[1,128]{1,0:T(1,128)}, u32[]{:S(2)}) copy-start(s32[1,128]{1,0:T(1,128)} %tok.3) | copy-start | bytes 1540

commit v7 on v6

--- a/solution.py
+++ b/solution.py
@@ -73,15 +73,19 @@
     return pl.ds(pl.multiple_of(j * width, width), width)
 
 
+def dma(*shape):
+    return pltpu.SemaphoreType.DMA(shape)
+
+
 class PairSum:
-    def __init__(self, part, got, own, sems, c, partner, n=NC):
+    def __init__(self, part, got, own, sems, c, partner, n=NC, base=0):
         self.part, self.got, self.own, self.c, self.partner = part, got, own, c, partner
         self.send, self.recv = sems
-        self.n, self.width = n, DIM // n
+        self.n, self.width, self.base = n, DIM // n, base
 
     def copy(self, j):
         return remote(self.part.at[:, 1 - self.c, :, cols(j, self.width)], self.got.at[:, :, cols(j, self.width)],
-                      self.send.at[j], self.recv.at[j], self.partner)
+                      self.send.at[self.base + j], self.recv.at[self.base + j], self.partner)
 
     def put(self, j, value):
         self.part[:, :, :, cols(j, self.width)] = value.astype(BF).reshape(2, 2, 32, self.width)
@@ -209,9 +213,9 @@
 
     def cross_copy(k, src, dst, j):
         cj = cols(j, WE if k == 0 else W)
-        return remote(src.at[:, :, cj], dst.at[:, :, cj], xs.at[k, j], xr.at[k, j], cross)
-
-    sum0 = PairSum(p0, g0, s0, (ps.at[0], pr.at[0]), c, partner, NE)
+        return remote(src.at[:, :, cj], dst.at[:, :, cj], xs.at[k * NE + j], xr.at[k * NE + j], cross)
+
+    sum0 = PairSum(p0, g0, s0, (ps, pr), c, partner, NE)
 
     def lookup(j):
         fetch_emb(j).wait()
@@ -266,21 +270,19 @@
     n1 = n1_o[...].reshape(SEQ, DIM)
     cos_tab, sin_tab = cs_o[0], cs_o[1]
 
-    for v in range(QKV // 256):
-        lin = nn(n1, wqkvt_v[:, v * 256:(v + 1) * 256])
-        for h in range(2):
-            lo = v * 256 + h * 128
-            piece = lin[:, h * 128:(h + 1) * 128]
-            if lo < QC + KC:
-                piece = rope_pair(piece, cos_tab, sin_tab)
-            qkv_o[:, lo:lo + 128] = piece.astype(BF)
+    lin = nn(n1, wqkvt_v[:, 0:QKV])
+    for lo in range(0, QKV, 128):
+        piece = lin[:, lo:lo + 128]
+        if lo < QC + KC:
+            piece = rope_pair(piece, cos_tab, sin_tab)
+        qkv_o[:, lo:lo + 128] = piece.astype(BF)
     for g in range(KVLOC):
         k = qkv_o[:, QC + g * HD:QC + (g + 1) * HD]
         v = qkv_o[:, QC + KC + g * HD:QC + KC + (g + 1) * HD]
         unstack(heads_o, g, nn(probs_of(stack(qkv_o, g), k).astype(BF), v).astype(BF))
     get_out.wait()
 
-    sum1 = PairSum(p1, g1, s1, (ps.at[1], pr.at[1]), c, partner)
+    sum1 = PairSum(p1, g1, s1, (ps, pr), c, partner, NC, NE)
     sum1.run(lambda j: nn(heads_o[...], wo_v[:, cols(j)]), lambda j: cross_copy(1, s1, r1, j).start())
 
     to_cross.wait_recv()
@@ -333,7 +335,7 @@
         return carry
     lax.fori_loop(0, FLOC // WB, mlp, 0)
 
-    sum2 = PairSum(p2, g2, gn2_o, (ps.at[2], pr.at[2]), c, partner, NB2)
+    sum2 = PairSum(p2, g2, gn2_o, (ps, pr), c, partner, NB2, NE + NC)
     sum2.run(lambda j: nn(ggate_o[...], wgt_v[:, cols(j, WB)]) + nn(gup_o[...], wut_v[:, cols(j, WB)]))
 
     for s in (sum0, sum1, sum2):
@@ -363,15 +365,14 @@
     share = remote(gh1_o.at[:, c], gh1_o.at[:, c], hs.at[0], hr.at[0], partner)
     share.start()
     gain_o[...] = gains[0] + gains[1] + gains[2] + gains[3]
-    sum0 = PairSum(part, g0, s0, (ps.at[0], pr.at[0]), c, partner, 1)
+    sum0 = PairSum(part, g0, s0, (ps, pr), c, partner, 1)
     sum0.copy(0).start()
     for g in range(KVLOC):
         probs_v[g] = probs_of(stack(qkv, g), qkv[:, QC + g * HD:QC + (g + 1) * HD])
     share.wait_recv()
 
     gh1 = gh1_o[...].reshape(SEQ, DIM)
-    for v in range(QC // 256):
-        gheads_v[:, v * 256:(v + 1) * 256] = nt(gh1, wo[v * 256:(v + 1) * 256, :]).astype(BF)
+    gheads_v[...] = nt(gh1, wo[...]).astype(BF)
 
     cos_tab, sin_tab = cs[0], -cs[1]
     turn_back = lambda pair: rope_pair(pair.astype(F32), cos_tab, sin_tab)
@@ -389,7 +390,7 @@
     gqkv_o[:, QC:QC + KC] = rope_pair(jnp.concatenate(gks, axis=1), cos_tab, sin_tab).astype(BF)
     gqkv_o[:, QC + KC:] = jnp.concatenate(gvs, axis=1)
 
-    sum1 = PairSum(p1, g1, give_o, (ps.at[1], pr.at[1]), c, partner, NB2)
+    sum1 = PairSum(p1, g1, give_o, (ps, pr), c, partner, NB2, 1)
     sum1.send_all(lambda j: nn(gqkv_o[...], wqkv[:, cols(j, WB)]))
     sum0.take(0)
     give_o[2] = s0[1 - x]
@@ -439,9 +440,10 @@
     return pltpu.VMEM(shape, dtype)
 
 
-NB = 3
-BM = 512
-UP_FIRST = 512
+NB = 5
+BM = 256
+UP_FIRST = 768
+RAMP = ((0, 64), (64, 64), (128, 128))
 EB = 256
 ENB = 4
 
@@ -449,12 +451,20 @@
 def outer_kernel(spec, n_in, n_held, side, *refs):
     n_out = 1 + max(o for _, _, _, o, _, _ in spec)
     ins, outs = refs[:n_in], refs[n_in + n_held:n_in + n_held + n_out]
-    *part, token, buf, sem = refs[n_in + n_held + n_out:]
+    *part, token, buf, sem, ramp, ramp_sem = refs[n_in + n_held + n_out:]
     token[...] = jnp.zeros_like(token)
     done = 0
     flying = {}
+    small = []
     for l, r, off, o, row, rows in spec:
         lhs, rhs, out = ins[l], ins[r], outs[o]
+        if not small:
+            for i, (lo, size) in enumerate(RAMP):
+                ramp[lo:lo + size] = tn(lhs[:, off + lo:off + lo + size], rhs[...])
+                small.append(pltpu.make_async_copy(
+                    ramp.at[pl.ds(lo, size)], out.at[pl.ds(row + lo, size)], ramp_sem.at[i]))
+                small[-1].start()
+            off, row, rows = off + BM, row + BM, rows - BM
         bm = min(BM, rows)
         steps = rows // bm
 
@@ -497,6 +507,8 @@
                 lo, hi = j * WB, (j + 1) * WB
                 out = nn(ins[side[0]][...], ins[side[1]][:, lo:hi])
                 part[0][:, :, :, lo:hi] = out.astype(BF).reshape(2, 2, 32, WB)
+    for copy in small:
+        copy.wait()
     for slot, size in flying.items():
         pltpu.make_async_copy(buf.at[slot, pl.ds(0, size)], outs[0].at[pl.ds(0, size)], sem.at[slot]).wait()
 
@@ -509,14 +521,25 @@
         out_shape=tuple(jax.ShapeDtypeStruct((m, DIM), F32) for m in rows) + extra + (on((8, 128), F32),),
         in_specs=vm(len(ins)) + hb(len(held)),
         out_specs=tuple(hb(len(rows)) + vm(1 + len(extra))),
-        scratch_shapes=[pltpu.VMEM((NB, BM, DIM), F32), pltpu.SemaphoreType.DMA((NB,))],
+        scratch_shapes=[pltpu.VMEM((NB, BM, DIM), F32), dma(NB), pltpu.VMEM((BM, DIM), F32), dma(len(RAMP))],
         input_output_aliases={len(ins) + i: o for i, (_, o) in enumerate(held)},
         cost_estimate=pl.CostEstimate(flops=2 * total * DIM * SEQ, bytes_accessed=4 * total * DIM, transcendentals=0),
         compiler_params=pltpu.CompilerParams(vmem_limit_bytes=24 * 2 ** 20),
     )(*ins, *[h for h, _ in held])
 
 
-def emb_kernel(tok, gx, gains, hid, out, ga_o, gm_o, hid_o, buf, sem, out_sem):
+def emb_kernel(tok, gx, gains, hid, out, ga_o, gm_o, hid_o, buf, sem, out_sem, ramp, ramp_sem):
+    base = lax.axis_index("tp") * VLOC
+    ids = jnp.broadcast_to(tok[...], (EB, SEQ)) - base
+    row = lax.broadcasted_iota(jnp.int32, (EB, SEQ), 0)
+    grad = gx[...].reshape(SEQ, DIM)
+
+    small = []
+    for i, (lo, size) in enumerate(RAMP):
+        hot = jnp.where(ids[:size] == row[:size] + lo, 1.0, 0.0).astype(BF)
+        ramp[lo:lo + size] = nn(hot, grad)
+        small.append(pltpu.make_async_copy(ramp.at[pl.ds(lo, size)], out.at[pl.ds(lo, size)], ramp_sem.at[i]))
+        small[-1].start()
     extra = (
         pltpu.make_async_copy(gains.at[pl.ds(0, 1)], ga_o, out_sem.at[0]),
         pltpu.make_async_copy(gains.at[pl.ds(1, 1)], gm_o, out_sem.at[1]),
@@ -524,28 +547,24 @@
     )
     for e in extra:
         e.start()
-    base = lax.axis_index("tp") * VLOC
-    ids = jnp.broadcast_to(tok[...], (EB, SEQ)) - base
-    row = lax.broadcasted_iota(jnp.int32, (EB, SEQ), 0)
-    grad = gx[...].reshape(SEQ, DIM)
 
     def copy(i):
-        slot = lax.rem(i, ENB)
+        slot = lax.rem(i - 1, ENB)
         return pltpu.make_async_copy(buf.at[slot], out.at[pl.ds(pl.multiple_of(i * EB, EB), EB)], sem.at[slot])
 
     def step(i, carry):
-        @pl.when(i >= ENB)
+        @pl.when(i >= ENB + 1)
         def _():
             copy(i).wait()
         hot = jnp.where(ids == row + i * EB, 1.0, 0.0).astype(BF)
-        buf[lax.rem(i, ENB)] = nn(hot, grad)
+        buf[lax.rem(i - 1, ENB)] = nn(hot, grad)
         copy(i).start()
         return carry
     steps = VLOC // EB
-    lax.fori_loop(0, steps, step, 0)
+    lax.fori_loop(1, steps, step, 0)
     for k in range(steps - ENB, steps):
         copy(k).wait()
-    for e in extra:
+    for e in (*small, *extra):
         e.wait()
 
 
@@ -555,10 +574,6 @@
 
 FULL = (2, 2, 32, DIM)
 MINE = (2, 32, DIM)
-
-
-def dma(*shape):
-    return pltpu.SemaphoreType.DMA(shape)
 
 
 def device_fn(tokens, positions, emb, gain_a, gain_m, wq, wk, wv, wo, wg, wu, wd, gh):
@@ -586,7 +601,7 @@
             pltpu.VMEM(FULL, BF), pltpu.VMEM(MINE, BF), pltpu.VMEM(MINE, BF), pltpu.VMEM(MINE, BF),
             pltpu.VMEM(FULL, BF), pltpu.VMEM(MINE, BF), pltpu.VMEM(MINE, BF), pltpu.VMEM(MINE, BF),
             pltpu.VMEM(FULL, BF), pltpu.VMEM(MINE, BF),
-            dma(6), dma(NE), dma(7), dma(3, NE), dma(3, NE), dma(2, NE), dma(2, NE), dma(5), dma(5)],
+            dma(6), dma(NE), dma(7), dma(NE + NC + NB2), dma(NE + NC + NB2), dma(NE + NC), dma(NE + NC), dma(5), dma(5)],
         compiler_params=pltpu.CompilerParams(collective_id=0, has_side_effects=True, vmem_limit_bytes=44 * 2 ** 20),
     )(tokens, positions, freq, ga, gm, gh2, emb, wqt, wkt, wvt, wo2, wd, wg, wu)
 
@@ -605,7 +620,7 @@
         scratch_shapes=[
             pltpu.VMEM((SEQ, QC), BF), pltpu.VMEM((KVLOC, GROUP * SEQ, SEQ), F32),
             pltpu.VMEM(MINE, BF), pltpu.VMEM(MINE, BF), pltpu.VMEM(FULL, BF), pltpu.VMEM(MINE, BF),
-            dma(2, NC), dma(2, NC), dma(1), dma(1)],
+            dma(1 + NB2), dma(1 + NB2), dma(1), dma(1)],
         compiler_params=pltpu.CompilerParams(collective_id=1, has_side_effects=True, vmem_limit_bytes=8 * 2 ** 20),
     )(gn2, gn2_got, part, h1, gfull, gm, qkv, cs, wqkv_v, wo_v, token)
 
@@ -630,7 +645,7 @@
         out_shape=(sds((VLOC, DIM), F32), sds((1, DIM), F32), sds((1, DIM), F32), sds((32, DIM))),
         in_specs=vm(4),
         out_specs=tuple(hb(4)),
-        scratch_shapes=[pltpu.VMEM((ENB, EB, DIM), F32), dma(ENB), dma(3)],
+        scratch_shapes=[pltpu.VMEM((ENB, EB, DIM), F32), dma(ENB), dma(3), pltpu.VMEM((EB, DIM), F32), dma(len(RAMP))],
         compiler_params=pltpu.CompilerParams(vmem_limit_bytes=24 * 2 ** 20),
     )(tokens, gx, gains, hid)
 

time: 72 us -> 70.7 us (0.982)
  Pallas kernels: 68.9 us -> 67.6 us
    pallas_call x2, Pallas kernels: 21.4 us -> 20.5 us  [outer(): pl.pallas_call(functools.partial(outer_kernel, spec, len(ins), len(held),...]
  transfers between devices with their start and end apart: 2 -> 2, of which waited for: 0 -> 0; matrix products, arithmetic and copies ran while one was open for 0% -> 0% of each run, Pallas kernels for 30% -> 29%
where the time goes in v7:
time: 70.7 us; the launch traced here: 70.6 us
  Pallas kernels  67.6 us (96%)
  starting transfers between devices  2.1 us (3%)
  between operations  0.9 us (1%)
    pallas_call x1, Pallas kernels, device_fn(): pl.pallas_call(front_kernel, out_shape=(on(FULL), on(MINE), on((SEQ, QKV)...  33.2 us
    pallas_call x2, Pallas kernels, outer(): pl.pallas_call(functools.partial(outer_kernel, spec, len(ins), len(held),...  20.5 us
    pallas_call x1, Pallas kernels, device_fn(): pl.pallas_call(emb_kernel, out_shape=(sds((VLOC, DIM), F32), sds((1, DIM)...  6.18 us
    pallas_call x1, Pallas kernels, device_fn(): pl.pallas_call(middle_kernel, out_shape=(on(FULL), on((SEQ, QKV)), on((3,...  5.97 us
    pallas_call x1, Pallas kernels, device_fn(): pl.pallas_call(back_kernel, out_shape=(on(FULL), on((2, DIM), F32), on((3...  1.75 us
  transfers between devices with their start and end apart: 2, of which 0 were waited for; matrix products, arithmetic and copies ran while one was open for 0% of the time, Pallas kernels for 29%

profile of v7, /device:TPU:0, one launch (start us, length us, event | category | flops | bytes accessed | tf_op | source)
XLA Modules:
  0.0 70.6 jit_solution(6267513901302219309)
XLA Ops:
  0.6 33.2 %shard_map.221 = (bf16[2,2,32,2048]{3,2,1,0:T(8,128)(2,1)S(1)}, bf16[2,32,2048]{2,1,0:T(8,128)(2,1)S(1)}, bf16[128,768]{1,0:T(8,128)(2,1)S(1)}, f32[2,128,128]{2...) custom-call(s32[1,128]{1,0:T(1,128)} %tok.3, ...), custom_call_target="tpu_custom_call" | custom-call | tf_op jit(solution)/shard_map/pallas_call | solution.py:588
  33.8 0.0 copy-start.1
  33.8 1.2 %collective-permute-start = (bf16[2,32,2048]{2,1,0:T(8,128)(2,1)S(1)}, bf16[2,32,2048]{2,1,0:T(8,128)(2,1)S(1)}, u32[]{:S(2)}, u32[]{:S(2)}) collective-permute-start(bf16[2,32,2048]{2,1,0:T(8,128)(2,1)S(1)} %get-tuple-element.49.gn2_own), channel_id=1, source_target_pairs={{0,2},{1,3},{2,0},{3,1},{4,6},{5,7},{6,4},{7,5},{8,10},{9,11},{10,... | collective-permute-start | bytes 786440 | tf_op jit(solution)/shard_map/ppermute | solution.py:609
  35.1 8.1 %shard_map.222 = (f32[2048,2048]{1,0:T(8,128)}, f32[2048,2048]{1,0:T(8,128)}, bf16[2,2,32,2048]{3,2,1,0:T(8,128)(2,1)S(1)}, f32[8,128]{1,0:T(8,128)S(1)}) custom-call(bf16[128,2048]{1,0:T(8,128)(2,1)S(1)} %bitcast.30, bf16[128,2048]{1,0:T(8,128)(2,1)S(1)} %get-tuple-element.51.refs_1_, bf16[128,2048]{1,0:T(8,128)(2,1)S(1)} %get-tuple-element.52.refs_2_.refs_1_, ...), custom_call_target="tpu_custom_call" | custom-call | flops 1476395008 | bytes 23068672 | tf_op jit(solution)/shard_map/pallas_call | solution.py:519
  43.2 0.0 collective-permute-done.gn2_got
  43.2 0.0 copy-done.1
  43.2 6.0 %shard_map.223 = (bf16[2,2,32,2048]{3,2,1,0:T(8,128)(2,1)S(1)}, bf16[128,768]{1,0:T(8,128)(2,1)S(1)}, bf16[3,32,2048]{2,1,0:T(8,128)(2,1)S(1)}, bf16[32,2048]{1,0:T(8,128)(2,1)S(1)}, f32[1,2048]{1,0:T(1,128)S(1)}) custom-call(bf16[2,32,2048]{2,1,0:T(8,128)(2,1)S(1)} %get-tuple-element.49.gn2_own, bf16[2,32,2048]{2,1,0:T(8,128)(2,1)S(1)} %collective-permute-done.gn2_got, ...), custom_call_target="tpu_custom_call" | custom-call | tf_op jit(solution)/shard_map/pallas_call | solution.py:615
  49.1 0.9 %collective-permute-start.1 = (bf16[3,32,2048]{2,1,0:T(8,128)(2,1)S(1)}, bf16[3,32,2048]{2,1,0:T(8,128)(2,1)S(1)}, u32[]{:S(2)}, u32[]{:S(2)}) collective-permute-start(bf16[3,32,2048]{2,1,0:T(8,128)(2,1)S(1)} %get-tuple-element.63.give), channel_id=1, source_target_pairs={{0,2},{1,3},{2,0},{3,1},{4,6},{5,7},{6,4},{7,5},{8,10},{9,11},{10,... | collective-permute-start | bytes 1179656 | tf_op jit(solution)/shard_map/ppermute | solution.py:627
  50.0 0.0 copy-start
  50.0 0.0 copy-start.2
  50.0 12.5 %shard_map.224 = (f32[2048,2048]{1,0:T(8,128)}, f32[2048,2048]{1,0:T(8,128)}, f32[512,2048]{1,0:T(8,128)}, f32[512,2048]{1,0:T(8,128)}, f32[128,2048]{1,0:T(8,12...) custom-call(bf16[128,2048]{1,0:T(8,128)(2,1)S(1)} %bitcast.31, ...), custom_call_target="tpu_custom_call", output_to_operand_aliasing={{0}: (8, {})} | custom-call | flops 2415919104 | bytes 37748736 | tf_op jit(solution)/shard_map/pallas_call | solution.py:519
  62.5 0.0 collective-permute-done.1.got
  62.5 0.0 copy-done
  62.5 1.7 %shard_map.225 = (bf16[2,2,32,2048]{3,2,1,0:T(8,128)(2,1)S(1)}, f32[2,2048]{1,0:T(2,128)S(1)}, bf16[32,2048]{1,0:T(8,128)(2,1)S(1)}) custom-call(bf16[3,32,2048]{2,1,0:T(8,128)(2,1)S(1)} %get-tuple-element.63.give, bf16[3,32,2048]{2,1,0:T(8,128)(2,1)S(1)} %collective-permute-done.1.got, bf16[32,2048]{1,0:T(8,128)(2,1)S(1)} %get-tuple-element.64.keep, ...), custom_call_target="tpu_custom_call" | custom-call | tf_op jit(solution)/shard_map/pallas_call | solution.py:634
  64.3 0.0 copy-done.2
  64.3 6.2 %shard_map.226 = (f32[2048,2048]{1,0:T(8,128)}, f32[1,2048]{1,0:T(1,128)}, f32[1,2048]{1,0:T(1,128)}, bf16[32,2048]{1,0:T(8,128)(2,1)}) custom-call(s32[1,128]{1,0:T(1,128)S(1)} %copy-done.2, bf16[2,2,32,2048]{3,2,1,0:T(8,128)(2,1)S(1)} %get-tuple-element.73.gx, f32[2,2048]{1,0:T(2,128)S(1)} %get-tuple-element.74.gains, ...), custom_call_target="tpu_custom_call" | custom-call | tf_op jit(solution)/shard_map/pallas_call | solution.py:643
Async XLA Ops:
  33.8 9.4 %copy-start.1 = (f32[2048]{0:T(1024)S(1)}, f32[2048]{0:T(1024)}, u32[]{:S(2)}) copy-start(f32[2048]{0:T(1024)} %param.18) | copy-start | bytes 24580
  33.8 9.3 %collective-permute-start = (bf16[2,32,2048]{2,1,0:T(8,128)(2,1)S(1)}, bf16[2,32,2048]{2,1,0:T(8,128)(2,1)S(1)}, u32[]{:S(2)}, u32[]{:S(2)}) collective-permute-start(bf16[2,32,2048]{2,1,0:T(8,128)(2,1)S(1)} %get-tuple-element.49.gn2_own), channel_id=1, source_target_pairs={{0,2},{1,3},{2,0},{3,1},{4,6},{5,7},{6,4},{7,5},{8,10},{9,11},{10,... | collective-permute-start | bytes 786440 | tf_op jit(solution)/shard_map/ppermute | solution.py:609
  49.1 13.3 %collective-permute-start.1 = (bf16[3,32,2048]{2,1,0:T(8,128)(2,1)S(1)}, bf16[3,32,2048]{2,1,0:T(8,128)(2,1)S(1)}, u32[]{:S(2)}, u32[]{:S(2)}) collective-permute-start(bf16[3,32,2048]{2,1,0:T(8,128)(2,1)S(1)} %get-tuple-element.63.give), channel_id=1, source_target_pairs={{0,2},{1,3},{2,0},{3,1},{4,6},{5,7},{6,4},{7,5},{8,10},{9,11},{10,... | collective-permute-start | bytes 1179656 | tf_op jit(solution)/shard_map/ppermute | solution.py:627
  50.0 12.5 %copy-start = (f32[2048]{0:T(1024)S(1)}, f32[2048]{0:T(1024)}, u32[]{:S(2)}) copy-start(f32[2048]{0:T(1024)} %param.17) | copy-start | bytes 24580
  50.0 14.2 %copy-start.2 = (s32[1,128]{1,0:T(1,128)S(1)}, s32[1,128]{1,0:T(1,128)}, u32[]{:S(2)}) copy-start(s32[1,128]{1,0:T(1,128)} %tok.3) | copy-start | bytes 1540

commit v8 on v7

--- a/solution.py
+++ b/solution.py
@@ -30,10 +30,10 @@
 W = DIM // NC
 NE = 8
 WE = DIM // NE
-AHEAD = 6
+AHEAD = 4
 NB2 = 2
 WB = DIM // NB2
-LAG = 2
+LAG = 1
 VMEM = pltpu.VMEM
 HBM = pltpu.HBM
 
@@ -291,9 +291,9 @@
     get_up.wait()
 
     def turn_up(j, carry):
-        wut_v[:, cols(j)] = jnp.transpose(wu_v[cols(j), :])
+        wut_v[:, cols(j, WB)] = jnp.transpose(wu_v[cols(j, WB), :])
         return carry
-    lax.fori_loop(0, NC, turn_up, 0)
+    lax.fori_loop(0, NB2, turn_up, 0)
 
     to_partner.wait_recv()
     onward.wait_recv()
@@ -303,10 +303,10 @@
     wgt_v = emb_v
 
     def grad_act(j, carry):
-        gact_v[:, cols(j)] = nt(gfull, wd_v[cols(j), :]).astype(BF)
-        wgt_v[:, cols(j)] = jnp.transpose(wg_v[cols(j), :])
+        gact_v[:, cols(j, WB)] = nt(gfull, wd_v[cols(j, WB), :]).astype(BF)
+        wgt_v[:, cols(j, WB)] = jnp.transpose(wg_v[cols(j, WB), :])
         return carry
-    lax.fori_loop(0, NC, grad_act, 0)
+    lax.fori_loop(0, NB2, grad_act, 0)
 
     for j in range(NC):
         cross_copy(1, s1, r1, j).wait_recv()
@@ -322,18 +322,14 @@
     share2.wait_recv()
     n2 = n2_o[...].reshape(SEQ, DIM)
 
-    def mlp(j, carry):
-        cj = cols(j, WB)
-        gate = nn(n2, wg_v[:, cj])
-        up = nn(n2, wu_v[:, cj])
-        sig = jax.nn.sigmoid(gate)
-        gate_act = gate * sig
-        act_o[:, cj] = (gate_act * up).astype(BF)
-        grad = gact_v[:, cj].astype(F32)
-        gup_o[:, cj] = (grad * gate_act).astype(BF)
-        ggate_o[:, cj] = (grad * up * sig * (1.0 + gate * (1.0 - sig))).astype(BF)
-        return carry
-    lax.fori_loop(0, FLOC // WB, mlp, 0)
+    gate = nn(n2, wg_v[...])
+    up = nn(n2, wu_v[...])
+    sig = jax.nn.sigmoid(gate)
+    gate_act = gate * sig
+    act_o[...] = (gate_act * up).astype(BF)
+    grad = gact_v[...].astype(F32)
+    gup_o[...] = (grad * gate_act).astype(BF)
+    ggate_o[...] = (grad * up * sig * (1.0 + gate * (1.0 - sig))).astype(BF)
 
     sum2 = PairSum(p2, g2, gn2_o, (ps, pr), c, partner, NB2, NE + NC)
     sum2.run(lambda j: nn(ggate_o[...], wgt_v[:, cols(j, WB)]) + nn(gup_o[...], wut_v[:, cols(j, WB)]))

time: 70.7 us -> 70.3 us (level)
  transfers between devices with their start and end apart: 2 -> 2, of which waited for: 0 -> 0; matrix products, arithmetic and copies ran while one was open for 0% -> 0% of each run, Pallas kernels for 29% -> 30%
where the time goes in v8:
time: 70.3 us; the launch traced here: 70.2 us
  Pallas kernels  67.2 us (96%)
  starting transfers between devices  2.09 us (3%)
  between operations  0.9 us (1%)
    pallas_call x1, Pallas kernels, device_fn(): pl.pallas_call(front_kernel, out_shape=(on(FULL), on(MINE), on((SEQ, QKV)...  32.8 us
    pallas_call x2, Pallas kernels, outer(): pl.pallas_call(functools.partial(outer_kernel, spec, len(ins), len(held),...  20.7 us
    pallas_call x1, Pallas kernels, device_fn(): pl.pallas_call(emb_kernel, out_shape=(sds((VLOC, DIM), F32), sds((1, DIM)...  6.18 us
    pallas_call x1, Pallas kernels, device_fn(): pl.pallas_call(middle_kernel, out_shape=(on(FULL), on((SEQ, QKV)), on((3,...  5.79 us
    pallas_call x1, Pallas kernels, device_fn(): pl.pallas_call(back_kernel, out_shape=(on(FULL), on((2, DIM), F32), on((3...  1.75 us
    ppermute x1, starting transfers between devices, device_fn(): gn2_got = lax.ppermute(gn2, 'tp', swap)  1.43 us
  transfers between devices with their start and end apart: 2, of which 0 were waited for; matrix products, arithmetic and copies ran while one was open for 0% of the time, Pallas kernels for 30%

profile of v8, /device:TPU:0, one launch (start us, length us, event | category | flops | bytes accessed | tf_op | source)
XLA Modules:
  0.0 70.2 jit_solution(14850677625234480931)
XLA Ops:
  0.6 32.8 %shard_map.221 = (bf16[2,2,32,2048]{3,2,1,0:T(8,128)(2,1)S(1)}, bf16[2,32,2048]{2,1,0:T(8,128)(2,1)S(1)}, bf16[128,768]{1,0:T(8,128)(2,1)S(1)}, f32[2,128,128]{2...) custom-call(s32[1,128]{1,0:T(1,128)} %tok.3, ...), custom_call_target="tpu_custom_call" | custom-call | tf_op jit(solution)/shard_map/pallas_call | solution.py:584
  33.4 0.0 copy-start.1
  33.4 1.4 %collective-permute-start = (bf16[2,32,2048]{2,1,0:T(8,128)(2,1)S(1)}, bf16[2,32,2048]{2,1,0:T(8,128)(2,1)S(1)}, u32[]{:S(2)}, u32[]{:S(2)}) collective-permute-start(bf16[2,32,2048]{2,1,0:T(8,128)(2,1)S(1)} %get-tuple-element.49.gn2_own), channel_id=1, source_target_pairs={{0,2},{1,3},{2,0},{3,1},{4,6},{5,7},{6,4},{7,5},{8,10},{9,11},{10,... | collective-permute-start | bytes 786440 | tf_op jit(solution)/shard_map/ppermute | solution.py:605
  34.9 8.3 %shard_map.222 = (f32[2048,2048]{1,0:T(8,128)}, f32[2048,2048]{1,0:T(8,128)}, bf16[2,2,32,2048]{3,2,1,0:T(8,128)(2,1)S(1)}, f32[8,128]{1,0:T(8,128)S(1)}) custom-call(bf16[128,2048]{1,0:T(8,128)(2,1)S(1)} %bitcast.30, bf16[128,2048]{1,0:T(8,128)(2,1)S(1)} %get-tuple-element.51.refs_1_, bf16[128,2048]{1,0:T(8,128)(2,1)S(1)} %get-tuple-element.52.refs_2_.refs_1_, ...), custom_call_target="tpu_custom_call" | custom-call | flops 1476395008 | bytes 23068672 | tf_op jit(solution)/shard_map/pallas_call | solution.py:515
  43.1 0.0 collective-permute-done.gn2_got
  43.1 0.0 copy-done.1
  43.1 5.8 %shard_map.223 = (bf16[2,2,32,2048]{3,2,1,0:T(8,128)(2,1)S(1)}, bf16[128,768]{1,0:T(8,128)(2,1)S(1)}, bf16[3,32,2048]{2,1,0:T(8,128)(2,1)S(1)}, bf16[32,2048]{1,0:T(8,128)(2,1)S(1)}, f32[1,2048]{1,0:T(1,128)S(1)}) custom-call(bf16[2,32,2048]{2,1,0:T(8,128)(2,1)S(1)} %get-tuple-element.49.gn2_own, bf16[2,32,2048]{2,1,0:T(8,128)(2,1)S(1)} %collective-permute-done.gn2_got, ...), custom_call_target="tpu_custom_call" | custom-call | tf_op jit(solution)/shard_map/pallas_call | solution.py:611
  48.9 0.7 collective-permute-start.1
  49.6 0.0 copy-start
  49.6 0.0 copy-start.2
  49.6 12.5 %shard_map.224 = (f32[2048,2048]{1,0:T(8,128)}, f32[2048,2048]{1,0:T(8,128)}, f32[512,2048]{1,0:T(8,128)}, f32[512,2048]{1,0:T(8,128)}, f32[128,2048]{1,0:T(8,12...) custom-call(bf16[128,2048]{1,0:T(8,128)(2,1)S(1)} %bitcast.31, ...), custom_call_target="tpu_custom_call", output_to_operand_aliasing={{0}: (8, {})} | custom-call | flops 2415919104 | bytes 37748736 | tf_op jit(solution)/shard_map/pallas_call | solution.py:515
  62.1 0.0 collective-permute-done.1.got
  62.1 0.0 copy-done
  62.1 1.7 %shard_map.225 = (bf16[2,2,32,2048]{3,2,1,0:T(8,128)(2,1)S(1)}, f32[2,2048]{1,0:T(2,128)S(1)}, bf16[32,2048]{1,0:T(8,128)(2,1)S(1)}) custom-call(bf16[3,32,2048]{2,1,0:T(8,128)(2,1)S(1)} %get-tuple-element.63.give, bf16[3,32,2048]{2,1,0:T(8,128)(2,1)S(1)} %collective-permute-done.1.got, bf16[32,2048]{1,0:T(8,128)(2,1)S(1)} %get-tuple-element.64.keep, ...), custom_call_target="tpu_custom_call" | custom-call | tf_op jit(solution)/shard_map/pallas_call | solution.py:630
  63.8 0.0 copy-done.2
  63.9 6.2 %shard_map.226 = (f32[2048,2048]{1,0:T(8,128)}, f32[1,2048]{1,0:T(1,128)}, f32[1,2048]{1,0:T(1,128)}, bf16[32,2048]{1,0:T(8,128)(2,1)}) custom-call(s32[1,128]{1,0:T(1,128)S(1)} %copy-done.2, bf16[2,2,32,2048]{3,2,1,0:T(8,128)(2,1)S(1)} %get-tuple-element.73.gx, f32[2,2048]{1,0:T(2,128)S(1)} %get-tuple-element.74.gains, ...), custom_call_target="tpu_custom_call" | custom-call | tf_op jit(solution)/shard_map/pallas_call | solution.py:639
Async XLA Ops:
  33.4 9.7 %copy-start.1 = (f32[2048]{0:T(1024)S(1)}, f32[2048]{0:T(1024)}, u32[]{:S(2)}) copy-start(f32[2048]{0:T(1024)} %param.18) | copy-start | bytes 24580
  33.4 9.7 %collective-permute-start = (bf16[2,32,2048]{2,1,0:T(8,128)(2,1)S(1)}, bf16[2,32,2048]{2,1,0:T(8,128)(2,1)S(1)}, u32[]{:S(2)}, u32[]{:S(2)}) collective-permute-start(bf16[2,32,2048]{2,1,0:T(8,128)(2,1)S(1)} %get-tuple-element.49.gn2_own), channel_id=1, source_target_pairs={{0,2},{1,3},{2,0},{3,1},{4,6},{5,7},{6,4},{7,5},{8,10},{9,11},{10,... | collective-permute-start | bytes 786440 | tf_op jit(solution)/shard_map/ppermute | solution.py:605
  48.9 13.1 %collective-permute-start.1 = (bf16[3,32,2048]{2,1,0:T(8,128)(2,1)S(1)}, bf16[3,32,2048]{2,1,0:T(8,128)(2,1)S(1)}, u32[]{:S(2)}, u32[]{:S(2)}) collective-permute-start(bf16[3,32,2048]{2,1,0:T(8,128)(2,1)S(1)} %get-tuple-element.63.give), channel_id=1, source_target_pairs={{0,2},{1,3},{2,0},{3,1},{4,6},{5,7},{6,4},{7,5},{8,10},{9,11},{10,... | collective-permute-start | bytes 1179656 | tf_op jit(solution)/shard_map/ppermute | solution.py:623
  49.6 12.5 %copy-start = (f32[2048]{0:T(1024)S(1)}, f32[2048]{0:T(1024)}, u32[]{:S(2)}) copy-start(f32[2048]{0:T(1024)} %param.17) | copy-start | bytes 24580
  49.6 14.2 %copy-start.2 = (s32[1,128]{1,0:T(1,128)S(1)}, s32[1,128]{1,0:T(1,128)}, u32[]{:S(2)}) copy-start(s32[1,128]{1,0:T(1,128)} %tok.3) | copy-start | bytes 1540

commit v9 on v8

--- a/solution.py
+++ b/solution.py
@@ -190,10 +190,10 @@
     get_q = pltpu.make_async_copy(wq, wqkv_v.at[pl.ds(0, QC)], w_sem.at[0])
     get_k = pltpu.make_async_copy(wk, wqkv_v.at[pl.ds(QC, KC)], w_sem.at[1])
     get_v = pltpu.make_async_copy(wv, wqkv_v.at[pl.ds(QC + KC, KC)], w_sem.at[2])
-    get_out = pltpu.make_async_copy(wo, wo_v, w_sem.at[3])
-    get_down = pltpu.make_async_copy(wd, wd_v, w_sem.at[4])
-    get_gate = pltpu.make_async_copy(wg, wg_v, w_sem.at[5])
-    get_up = pltpu.make_async_copy(wu, wu_v, w_sem.at[6])
+    get_out = pltpu.make_async_copy(wo, wo_v, emb_sem.at[0])
+    get_down = pltpu.make_async_copy(wd, wd_v, emb_sem.at[1])
+    get_gate = pltpu.make_async_copy(wg, wg_v, emb_sem.at[2])
+    get_up = pltpu.make_async_copy(wu, wu_v, emb_sem.at[3])
     get_small = [pltpu.make_async_copy(src, dst, in_sem.at[i]) for i, (src, dst) in enumerate(
         ((tok, tok_v), (pos, pos_v), (freq, freq_v), (gain_a, ga_v), (gain_m, gm_v), (gh, gfull_o.at[x, c])))]
     get_small[0].start()
@@ -282,7 +282,8 @@
         unstack(heads_o, g, nn(probs_of(stack(qkv_o, g), k).astype(BF), v).astype(BF))
     get_out.wait()
 
-    sum1 = PairSum(p1, g1, s1, (ps, pr), c, partner, NC, NE)
+    sum0.drain()
+    sum1 = PairSum(p1, g1, s1, (ps, pr), c, partner)
     sum1.run(lambda j: nn(heads_o[...], wo_v[:, cols(j)]), lambda j: cross_copy(1, s1, r1, j).start())
 
     to_cross.wait_recv()
@@ -331,11 +332,11 @@
     gup_o[...] = (grad * gate_act).astype(BF)
     ggate_o[...] = (grad * up * sig * (1.0 + gate * (1.0 - sig))).astype(BF)
 
-    sum2 = PairSum(p2, g2, gn2_o, (ps, pr), c, partner, NB2, NE + NC)
+    sum1.drain()
+    sum2 = PairSum(p2, g2, gn2_o, (ps, pr), c, partner, NB2)
     sum2.run(lambda j: nn(ggate_o[...], wgt_v[:, cols(j, WB)]) + nn(gup_o[...], wut_v[:, cols(j, WB)]))
 
-    for s in (sum0, sum1, sum2):
-        s.drain()
+    sum2.drain()
     for j in range(NE):
         cross_copy(0, s0, r0, j).wait_send()
     for j in range(NC):
@@ -597,7 +598,7 @@
             pltpu.VMEM(FULL, BF), pltpu.VMEM(MINE, BF), pltpu.VMEM(MINE, BF), pltpu.VMEM(MINE, BF),
             pltpu.VMEM(FULL, BF), pltpu.VMEM(MINE, BF), pltpu.VMEM(MINE, BF), pltpu.VMEM(MINE, BF),
             pltpu.VMEM(FULL, BF), pltpu.VMEM(MINE, BF),
-            dma(6), dma(NE), dma(7), dma(NE + NC + NB2), dma(NE + NC + NB2), dma(NE + NC), dma(NE + NC), dma(5), dma(5)],
+            dma(6), dma(NE), dma(3), dma(NE), dma(NE), dma(NE + NC), dma(NE + NC), dma(5), dma(5)],
         compiler_params=pltpu.CompilerParams(collective_id=0, has_side_effects=True, vmem_limit_bytes=44 * 2 ** 20),
     )(tokens, positions, freq, ga, gm, gh2, emb, wqt, wkt, wvt, wo2, wd, wg, wu)
 

time: 70.3 us -> 70.2 us (level)
  no operation moved by 1% of the time
where the time goes in v9:
time: 70.2 us; the launch traced here: 70 us
  Pallas kernels  67 us (95%)
  starting transfers between devices  2.11 us (3%)
  between operations  0.9 us (1%)
    pallas_call x1, Pallas kernels, device_fn(): pl.pallas_call(front_kernel, out_shape=(on(FULL), on(MINE), on((SEQ, QKV)...  32.6 us
    pallas_call x2, Pallas kernels, outer(): pl.pallas_call(functools.partial(outer_kernel, spec, len(ins), len(held),...  20.7 us
    pallas_call x1, Pallas kernels, device_fn(): pl.pallas_call(emb_kernel, out_shape=(sds((VLOC, DIM), F32), sds((1, DIM)...  6.18 us
    pallas_call x1, Pallas kernels, device_fn(): pl.pallas_call(middle_kernel, out_shape=(on(FULL), on((SEQ, QKV)), on((3,...  5.78 us
    pallas_call x1, Pallas kernels, device_fn(): pl.pallas_call(back_kernel, out_shape=(on(FULL), on((2, DIM), F32), on((3...  1.75 us
    ppermute x1, starting transfers between devices, device_fn(): gn2_got = lax.ppermute(gn2, 'tp', swap)  1.44 us
  transfers between devices with their start and end apart: 2, of which 0 were waited for; matrix products, arithmetic and copies ran while one was open for 0% of the time, Pallas kernels for 30%

profile of v9, /device:TPU:0, one launch (start us, length us, event | category | flops | bytes accessed | tf_op | source)
XLA Modules:
  0.0 70.0 jit_solution(3988018883186774942)
XLA Ops:
  0.6 32.6 %shard_map.221 = (bf16[2,2,32,2048]{3,2,1,0:T(8,128)(2,1)S(1)}, bf16[2,32,2048]{2,1,0:T(8,128)(2,1)S(1)}, bf16[128,768]{1,0:T(8,128)(2,1)S(1)}, f32[2,128,128]{2...) custom-call(s32[1,128]{1,0:T(1,128)} %tok.3, ...), custom_call_target="tpu_custom_call" | custom-call | tf_op jit(solution)/shard_map/pallas_call | solution.py:585
  33.3 0.0 copy-start.1
  33.3 1.4 %collective-permute-start = (bf16[2,32,2048]{2,1,0:T(8,128)(2,1)S(1)}, bf16[2,32,2048]{2,1,0:T(8,128)(2,1)S(1)}, u32[]{:S(2)}, u32[]{:S(2)}) collective-permute-start(bf16[2,32,2048]{2,1,0:T(8,128)(2,1)S(1)} %get-tuple-element.49.gn2_own), channel_id=1, source_target_pairs={{0,2},{1,3},{2,0},{3,1},{4,6},{5,7},{6,4},{7,5},{8,10},{9,11},{10,... | collective-permute-start | bytes 786440 | tf_op jit(solution)/shard_map/ppermute | solution.py:606
  34.7 8.2 %shard_map.222 = (f32[2048,2048]{1,0:T(8,128)}, f32[2048,2048]{1,0:T(8,128)}, bf16[2,2,32,2048]{3,2,1,0:T(8,128)(2,1)S(1)}, f32[8,128]{1,0:T(8,128)S(1)}) custom-call(bf16[128,2048]{1,0:T(8,128)(2,1)S(1)} %bitcast.30, bf16[128,2048]{1,0:T(8,128)(2,1)S(1)} %get-tuple-element.51.refs_1_, bf16[128,2048]{1,0:T(8,128)(2,1)S(1)} %get-tuple-element.52.refs_2_.refs_1_, ...), custom_call_target="tpu_custom_call" | custom-call | flops 1476395008 | bytes 23068672 | tf_op jit(solution)/shard_map/pallas_call | solution.py:516
  43.0 0.0 collective-permute-done.gn2_got
  43.0 0.0 copy-done.1
  43.0 5.8 %shard_map.223 = (bf16[2,2,32,2048]{3,2,1,0:T(8,128)(2,1)S(1)}, bf16[128,768]{1,0:T(8,128)(2,1)S(1)}, bf16[3,32,2048]{2,1,0:T(8,128)(2,1)S(1)}, bf16[32,2048]{1,0:T(8,128)(2,1)S(1)}, f32[1,2048]{1,0:T(1,128)S(1)}) custom-call(bf16[2,32,2048]{2,1,0:T(8,128)(2,1)S(1)} %get-tuple-element.49.gn2_own, bf16[2,32,2048]{2,1,0:T(8,128)(2,1)S(1)} %collective-permute-done.gn2_got, ...), custom_call_target="tpu_custom_call" | custom-call | tf_op jit(solution)/shard_map/pallas_call | solution.py:612
  48.8 0.7 collective-permute-start.1
  49.5 0.0 copy-start
  49.5 0.0 copy-start.2
  49.5 12.5 %shard_map.224 = (f32[2048,2048]{1,0:T(8,128)}, f32[2048,2048]{1,0:T(8,128)}, f32[512,2048]{1,0:T(8,128)}, f32[512,2048]{1,0:T(8,128)}, f32[128,2048]{1,0:T(8,12...) custom-call(bf16[128,2048]{1,0:T(8,128)(2,1)S(1)} %bitcast.31, ...), custom_call_target="tpu_custom_call", output_to_operand_aliasing={{0}: (8, {})} | custom-call | flops 2415919104 | bytes 37748736 | tf_op jit(solution)/shard_map/pallas_call | solution.py:516
  61.9 0.0 collective-permute-done.1.got
  61.9 0.0 copy-done
  61.9 1.7 %shard_map.225 = (bf16[2,2,32,2048]{3,2,1,0:T(8,128)(2,1)S(1)}, f32[2,2048]{1,0:T(2,128)S(1)}, bf16[32,2048]{1,0:T(8,128)(2,1)S(1)}) custom-call(bf16[3,32,2048]{2,1,0:T(8,128)(2,1)S(1)} %get-tuple-element.63.give, bf16[3,32,2048]{2,1,0:T(8,128)(2,1)S(1)} %collective-permute-done.1.got, bf16[32,2048]{1,0:T(8,128)(2,1)S(1)} %get-tuple-element.64.keep, ...), custom_call_target="tpu_custom_call" | custom-call | tf_op jit(solution)/shard_map/pallas_call | solution.py:631
  63.7 0.0 copy-done.2
  63.7 6.2 %shard_map.226 = (f32[2048,2048]{1,0:T(8,128)}, f32[1,2048]{1,0:T(1,128)}, f32[1,2048]{1,0:T(1,128)}, bf16[32,2048]{1,0:T(8,128)(2,1)}) custom-call(s32[1,128]{1,0:T(1,128)S(1)} %copy-done.2, bf16[2,2,32,2048]{3,2,1,0:T(8,128)(2,1)S(1)} %get-tuple-element.73.gx, f32[2,2048]{1,0:T(2,128)S(1)} %get-tuple-element.74.gains, ...), custom_call_target="tpu_custom_call" | custom-call | tf_op jit(solution)/shard_map/pallas_call | solution.py:640
Async XLA Ops:
  33.3 9.7 %copy-start.1 = (f32[2048]{0:T(1024)S(1)}, f32[2048]{0:T(1024)}, u32[]{:S(2)}) copy-start(f32[2048]{0:T(1024)} %param.18) | copy-start | bytes 24580
  33.3 9.7 %collective-permute-start = (bf16[2,32,2048]{2,1,0:T(8,128)(2,1)S(1)}, bf16[2,32,2048]{2,1,0:T(8,128)(2,1)S(1)}, u32[]{:S(2)}, u32[]{:S(2)}) collective-permute-start(bf16[2,32,2048]{2,1,0:T(8,128)(2,1)S(1)} %get-tuple-element.49.gn2_own), channel_id=1, source_target_pairs={{0,2},{1,3},{2,0},{3,1},{4,6},{5,7},{6,4},{7,5},{8,10},{9,11},{10,... | collective-permute-start | bytes 786440 | tf_op jit(solution)/shard_map/ppermute | solution.py:606
  48.8 13.1 %collective-permute-start.1 = (bf16[3,32,2048]{2,1,0:T(8,128)(2,1)S(1)}, bf16[3,32,2048]{2,1,0:T(8,128)(2,1)S(1)}, u32[]{:S(2)}, u32[]{:S(2)}) collective-permute-start(bf16[3,32,2048]{2,1,0:T(8,128)(2,1)S(1)} %get-tuple-element.63.give), channel_id=1, source_target_pairs={{0,2},{1,3},{2,0},{3,1},{4,6},{5,7},{6,4},{7,5},{8,10},{9,11},{10,... | collective-permute-start | bytes 1179656 | tf_op jit(solution)/shard_map/ppermute | solution.py:624
  49.5 12.5 %copy-start = (f32[2048]{0:T(1024)S(1)}, f32[2048]{0:T(1024)}, u32[]{:S(2)}) copy-start(f32[2048]{0:T(1024)} %param.17) | copy-start | bytes 24580
  49.5 14.2 %copy-start.2 = (s32[1,128]{1,0:T(1,128)S(1)}, s32[1,128]{1,0:T(1,128)}, u32[]{:S(2)}) copy-start(s32[1,128]{1,0:T(1,128)} %tok.3) | copy-start | bytes 1540

commit v10 on v9

--- a/solution.py
+++ b/solution.py
@@ -318,7 +318,8 @@
         h1_o[b, r] = h1
         n2_o[b, c, r] = norm_rows(h1.astype(F32), gm_v[...])
     rows16(second)
-    share2 = remote(n2_o.at[:, c], n2_o.at[:, c], hs.at[4], hr.at[4], partner)
+    share1.wait_send()
+    share2 = remote(n2_o.at[:, c], n2_o.at[:, c], hs.at[2], hr.at[2], partner)
     share2.start()
     share2.wait_recv()
     n2 = n2_o[...].reshape(SEQ, DIM)
@@ -341,7 +342,7 @@
         cross_copy(0, s0, r0, j).wait_send()
     for j in range(NC):
         cross_copy(1, s1, r1, j).wait_send()
-    for copy in (to_cross, to_partner, share1, onward, share2):
+    for copy in (to_cross, to_partner, onward, share2):
         copy.wait_send()
 
 
@@ -598,7 +599,7 @@
             pltpu.VMEM(FULL, BF), pltpu.VMEM(MINE, BF), pltpu.VMEM(MINE, BF), pltpu.VMEM(MINE, BF),
             pltpu.VMEM(FULL, BF), pltpu.VMEM(MINE, BF), pltpu.VMEM(MINE, BF), pltpu.VMEM(MINE, BF),
             pltpu.VMEM(FULL, BF), pltpu.VMEM(MINE, BF),
-            dma(6), dma(NE), dma(3), dma(NE), dma(NE), dma(NE + NC), dma(NE + NC), dma(5), dma(5)],
+            dma(6), dma(NE), dma(3), dma(NE), dma(NE), dma(NE + NC), dma(NE + NC), dma(4), dma(4)],
         compiler_params=pltpu.CompilerParams(collective_id=0, has_side_effects=True, vmem_limit_bytes=44 * 2 ** 20),
     )(tokens, positions, freq, ga, gm, gh2, emb, wqt, wkt, wvt, wo2, wd, wg, wu)
 

time: 70.2 us -> 70.2 us (level)
  no operation moved by 1% of the time
where the time goes in v10:
time: 70.2 us; the launch traced here: 70 us
  Pallas kernels  67 us (95%)
  starting transfers between devices  2.1 us (3%)
  between operations  0.9 us (1%)
    pallas_call x1, Pallas kernels, device_fn(): pl.pallas_call(front_kernel, out_shape=(on(FULL), on(MINE), on((SEQ, QKV)...  32.6 us
    pallas_call x2, Pallas kernels, outer(): pl.pallas_call(functools.partial(outer_kernel, spec, len(ins), len(held),...  20.7 us
    pallas_call x1, Pallas kernels, device_fn(): pl.pallas_call(emb_kernel, out_shape=(sds((VLOC, DIM), F32), sds((1, DIM)...  6.18 us
    pallas_call x1, Pallas kernels, device_fn(): pl.pallas_call(middle_kernel, out_shape=(on(FULL), on((SEQ, QKV)), on((3,...  5.79 us
    pallas_call x1, Pallas kernels, device_fn(): pl.pallas_call(back_kernel, out_shape=(on(FULL), on((2, DIM), F32), on((3...  1.75 us
    ppermute x1, starting transfers between devices, device_fn(): gn2_got = lax.ppermute(gn2, 'tp', swap)  1.43 us
  transfers between devices with their start and end apart: 2, of which 0 were waited for; matrix products, arithmetic and copies ran while one was open for 0% of the time, Pallas kernels for 30%

profile of v10, /device:TPU:0, one launch (start us, length us, event | category | flops | bytes accessed | tf_op | source)
XLA Modules:
  0.0 70.0 jit_solution(16951593323151148059)
XLA Ops:
  0.6 32.6 %shard_map.221 = (bf16[2,2,32,2048]{3,2,1,0:T(8,128)(2,1)S(1)}, bf16[2,32,2048]{2,1,0:T(8,128)(2,1)S(1)}, bf16[128,768]{1,0:T(8,128)(2,1)S(1)}, f32[2,128,128]{2...) custom-call(s32[1,128]{1,0:T(1,128)} %tok.3, ...), custom_call_target="tpu_custom_call" | custom-call | tf_op jit(solution)/shard_map/pallas_call | solution.py:586
  33.2 0.0 copy-start.1
  33.3 1.4 %collective-permute-start = (bf16[2,32,2048]{2,1,0:T(8,128)(2,1)S(1)}, bf16[2,32,2048]{2,1,0:T(8,128)(2,1)S(1)}, u32[]{:S(2)}, u32[]{:S(2)}) collective-permute-start(bf16[2,32,2048]{2,1,0:T(8,128)(2,1)S(1)} %get-tuple-element.49.gn2_own), channel_id=1, source_target_pairs={{0,2},{1,3},{2,0},{3,1},{4,6},{5,7},{6,4},{7,5},{8,10},{9,11},{10,... | collective-permute-start | bytes 786440 | tf_op jit(solution)/shard_map/ppermute | solution.py:607
  34.7 8.2 %shard_map.222 = (f32[2048,2048]{1,0:T(8,128)}, f32[2048,2048]{1,0:T(8,128)}, bf16[2,2,32,2048]{3,2,1,0:T(8,128)(2,1)S(1)}, f32[8,128]{1,0:T(8,128)S(1)}) custom-call(bf16[128,2048]{1,0:T(8,128)(2,1)S(1)} %bitcast.30, bf16[128,2048]{1,0:T(8,128)(2,1)S(1)} %get-tuple-element.51.refs_1_, bf16[128,2048]{1,0:T(8,128)(2,1)S(1)} %get-tuple-element.52.refs_2_.refs_1_, ...), custom_call_target="tpu_custom_call" | custom-call | flops 1476395008 | bytes 23068672 | tf_op jit(solution)/shard_map/pallas_call | solution.py:517
  42.9 0.0 collective-permute-done.gn2_got
  43.0 0.0 copy-done.1
  43.0 5.8 %shard_map.223 = (bf16[2,2,32,2048]{3,2,1,0:T(8,128)(2,1)S(1)}, bf16[128,768]{1,0:T(8,128)(2,1)S(1)}, bf16[3,32,2048]{2,1,0:T(8,128)(2,1)S(1)}, bf16[32,2048]{1,0:T(8,128)(2,1)S(1)}, f32[1,2048]{1,0:T(1,128)S(1)}) custom-call(bf16[2,32,2048]{2,1,0:T(8,128)(2,1)S(1)} %get-tuple-element.49.gn2_own, bf16[2,32,2048]{2,1,0:T(8,128)(2,1)S(1)} %collective-permute-done.gn2_got, ...), custom_call_target="tpu_custom_call" | custom-call | tf_op jit(solution)/shard_map/pallas_call | solution.py:613
  48.8 0.7 collective-permute-start.1
  49.4 0.0 copy-start
  49.4 0.0 copy-start.2
  49.4 12.5 %shard_map.224 = (f32[2048,2048]{1,0:T(8,128)}, f32[2048,2048]{1,0:T(8,128)}, f32[512,2048]{1,0:T(8,128)}, f32[512,2048]{1,0:T(8,128)}, f32[128,2048]{1,0:T(8,12...) custom-call(bf16[128,2048]{1,0:T(8,128)(2,1)S(1)} %bitcast.31, ...), custom_call_target="tpu_custom_call", output_to_operand_aliasing={{0}: (8, {})} | custom-call | flops 2415919104 | bytes 37748736 | tf_op jit(solution)/shard_map/pallas_call | solution.py:517
  61.9 0.0 collective-permute-done.1.got
  61.9 0.0 copy-done
  61.9 1.7 %shard_map.225 = (bf16[2,2,32,2048]{3,2,1,0:T(8,128)(2,1)S(1)}, f32[2,2048]{1,0:T(2,128)S(1)}, bf16[32,2048]{1,0:T(8,128)(2,1)S(1)}) custom-call(bf16[3,32,2048]{2,1,0:T(8,128)(2,1)S(1)} %get-tuple-element.63.give, bf16[3,32,2048]{2,1,0:T(8,128)(2,1)S(1)} %collective-permute-done.1.got, bf16[32,2048]{1,0:T(8,128)(2,1)S(1)} %get-tuple-element.64.keep, ...), custom_call_target="tpu_custom_call" | custom-call | tf_op jit(solution)/shard_map/pallas_call | solution.py:632
  63.7 0.0 copy-done.2
  63.7 6.2 %shard_map.226 = (f32[2048,2048]{1,0:T(8,128)}, f32[1,2048]{1,0:T(1,128)}, f32[1,2048]{1,0:T(1,128)}, bf16[32,2048]{1,0:T(8,128)(2,1)}) custom-call(s32[1,128]{1,0:T(1,128)S(1)} %copy-done.2, bf16[2,2,32,2048]{3,2,1,0:T(8,128)(2,1)S(1)} %get-tuple-element.73.gx, f32[2,2048]{1,0:T(2,128)S(1)} %get-tuple-element.74.gains, ...), custom_call_target="tpu_custom_call" | custom-call | tf_op jit(solution)/shard_map/pallas_call | solution.py:641
Async XLA Ops:
  33.2 9.7 %copy-start.1 = (f32[2048]{0:T(1024)S(1)}, f32[2048]{0:T(1024)}, u32[]{:S(2)}) copy-start(f32[2048]{0:T(1024)} %param.18) | copy-start | bytes 24580
  33.3 9.7 %collective-permute-start = (bf16[2,32,2048]{2,1,0:T(8,128)(2,1)S(1)}, bf16[2,32,2048]{2,1,0:T(8,128)(2,1)S(1)}, u32[]{:S(2)}, u32[]{:S(2)}) collective-permute-start(bf16[2,32,2048]{2,1,0:T(8,128)(2,1)S(1)} %get-tuple-element.49.gn2_own), channel_id=1, source_target_pairs={{0,2},{1,3},{2,0},{3,1},{4,6},{5,7},{6,4},{7,5},{8,10},{9,11},{10,... | collective-permute-start | bytes 786440 | tf_op jit(solution)/shard_map/ppermute | solution.py:607
  48.8 13.1 %collective-permute-start.1 = (bf16[3,32,2048]{2,1,0:T(8,128)(2,1)S(1)}, bf16[3,32,2048]{2,1,0:T(8,128)(2,1)S(1)}, u32[]{:S(2)}, u32[]{:S(2)}) collective-permute-start(bf16[3,32,2048]{2,1,0:T(8,128)(2,1)S(1)} %get-tuple-element.63.give), channel_id=1, source_target_pairs={{0,2},{1,3},{2,0},{3,1},{4,6},{5,7},{6,4},{7,5},{8,10},{9,11},{10,... | collective-permute-start | bytes 1179656 | tf_op jit(solution)/shard_map/ppermute | solution.py:625
  49.4 12.5 %copy-start = (f32[2048]{0:T(1024)S(1)}, f32[2048]{0:T(1024)}, u32[]{:S(2)}) copy-start(f32[2048]{0:T(1024)} %param.17) | copy-start | bytes 24580
  49.4 14.2 %copy-start.2 = (s32[1,128]{1,0:T(1,128)S(1)}, s32[1,128]{1,0:T(1,128)}, u32[]{:S(2)}) copy-start(s32[1,128]{1,0:T(1,128)} %tok.3) | copy-start | bytes 1540
